TPU v7x, 32 devices: a whole 2x2x4 slice. The times are simulated.
32 devices in a mesh: group: 8 (over y, x, core), expert: 4 (over z).
Axes of the slice: x: 2, y: 2, z: 4, core: 2. Of those that a mesh axis runs over, the one named last changes fastest.
Arguments:
- tokens: bfloat16 [8192, 2048], P(('group', 'expert')), may hold values from -6 to 6
- routes: int32 [8192, 8], P(('group', 'expert')), may hold values from 0 to 15, all different within a row; in each aligned block of 256 rows (0 to 255, 256 to 511, ...) at most 256 rows name the same one
- prefix: int32 [8], P('group'), may hold values from 102 to 512
- query_weight: float32 [2048, 2048], P('group'), may hold values from -0.125 to 0.125
- key_weight: float32 [2048, 2048], P('group'), may hold values from -0.125 to 0.125
- value_weight: float32 [2048, 2048], P('group'), may hold values from -0.125 to 0.125
- output_weight: float32 [2048, 2048], P('group'), may hold values from -1 to 1
- router_weight: float32 [2048, 16], P('group'), may hold values from -0.0625 to 0.0625
- attention_gain: float32 [2048], P('group'), may hold values from 0.5 to 1.5
- feedforward_gain: float32 [2048], P('group'), may hold values from 0.5 to 1.5
- query_gain: float32 [2048], P('group'), may hold values from 0.8 to 1.6
- key_gain: float32 [2048], P('group'), may hold values from 0.8 to 1.6
- expert_in: float32 [2048, 16, 2048], P('group', 'expert'), may hold values from -0.125 to 0.125
- expert_down: float32 [1024, 16, 2048], P('group', 'expert'), may hold values from -1.75 to 1.75
- cotangent: bfloat16 [8192, 2048], P(('group', 'expert')), may hold values from -6 to 6
Outputs:
- output: bfloat16 [8192, 2048], P(('group', 'expert'))
- grad_tokens: float32 [8192, 2048], P(('group', 'expert'))
- grad_query: float32 [2048, 2048], P('group')
- grad_key: float32 [2048, 2048], P('group')
- grad_value: float32 [2048, 2048], P('group')
- grad_output: float32 [2048, 2048], P('group')
- grad_router: float32 [2048, 16], P('group')
- grad_attention_gain: float32 [2048], P('group')
- grad_feedforward_gain: float32 [2048], P('group')
- grad_query_gain: float32 [2048], P('group')
- grad_key_gain: float32 [2048], P('group')
- grad_expert_in: float32 [2048, 16, 2048], P('group', 'expert')
- grad_expert_down: float32 [1024, 16, 2048], P('group', 'expert')
Inputs may be any that keep to these rules, and one draw needn't show every extreme that they name: `routes`: in each aligned block of 256 rows (the rows of one device) no expert is named by more than 256 rows, and in some block one expert is named by exactly 256 rows; the 8 experts of a row differ.
All inputs are finite; a program needn't handle non-finite values.
Results may differ from a plain program's by a relative error of at most 0.025.
Values may be sent and summed in bfloat16 or wider, within the bound.
A program may use at most 448 MiB of HBM per device.

v0:
```python
import math

import jax
import jax.numpy as jnp
from jax import lax
from jax.sharding import PartitionSpec as P

HEADS = 16
HEAD_DIM = 128
TOP = 8
LEN = 1024


EPS = 1e-05
THETA = 10000.0


def rope_tables(positions):
    steps = jnp.arange(HEAD_DIM // 2).astype(jnp.float32)
    freq = jnp.exp(steps * (-2.0 * math.log(THETA) / HEAD_DIM))
    angle = positions[:, None] * freq[None, :]
    return (jnp.cos(angle)[:, None, :], jnp.sin(angle)[:, None, :])


def rotate(values, cosine, sine):
    half = values.shape[-1] // 2
    first = values[..., :half]
    second = values[..., half:]
    return jnp.concatenate([first * cosine - second * sine, second * cosine + first * sine], -1)


def unrotate(values, cosine, sine):
    half = values.shape[-1] // 2
    first = values[..., :half]
    second = values[..., half:]
    return jnp.concatenate([first * cosine + second * sine, second * cosine - first * sine], -1)


def row_scale(values):
    return lax.rsqrt(jnp.mean(values * values, -1, keepdims=True) + EPS)


def norm_back(values, scale_rows, upstream):
    inner = jnp.mean(upstream * values, -1, keepdims=True)
    return scale_rows * upstream - values * (scale_rows * scale_rows * scale_rows) * inner


def masked_scores(query_bf, key_all, prefix, offset, slice_len):
    raw = jnp.einsum("sqhd,skhd->shqk", query_bf, key_all, preferred_element_type=jnp.float32)
    row_pos = offset + jnp.arange(slice_len)
    col_pos = jnp.arange(key_all.shape[1])
    allowed = (col_pos[None, None, :] <= row_pos[None, :, None]) | (
        col_pos[None, None, :] < prefix[:, None, None]
    )
    return jnp.where(allowed[:, None], raw, -1e30)


def outer_sum(left, right):
    return jnp.einsum("td,te->de", left, right, preferred_element_type=jnp.float32)


def back_product(grad_rows, weight):
    return jnp.einsum("te,de->td", grad_rows, weight, preferred_element_type=jnp.float32)


def body(
    tokens,
    routes,
    prefix,
    query_weight,
    key_weight,
    value_weight,
    output_weight,
    router_weight,
    attention_gain,
    feedforward_gain,
    query_gain,
    key_gain,
    expert_in,
    expert_down,
    cotangent,
):
    (
        full_query,
        full_key,
        full_value,
        full_output,
        full_router,
        gain_one,
        gain_two,
        gain_query,
        gain_key,
    ) = (
        lax.all_gather(query_weight.astype(jnp.bfloat16), "group", axis=0, tiled=True),
        lax.all_gather(key_weight.astype(jnp.bfloat16), "group", axis=0, tiled=True),
        lax.all_gather(value_weight.astype(jnp.bfloat16), "group", axis=0, tiled=True),
        lax.all_gather(output_weight.astype(jnp.bfloat16), "group", axis=0, tiled=True),
        lax.all_gather(router_weight.astype(jnp.bfloat16), "group", axis=0, tiled=True),
        lax.all_gather(attention_gain.astype(jnp.bfloat16), "group", axis=0, tiled=True),
        lax.all_gather(feedforward_gain.astype(jnp.bfloat16), "group", axis=0, tiled=True),
        lax.all_gather(query_gain.astype(jnp.bfloat16), "group", axis=0, tiled=True),
        lax.all_gather(key_gain.astype(jnp.bfloat16), "group", axis=0, tiled=True),
    )
    gain_one = gain_one.astype(jnp.float32)
    gain_two = gain_two.astype(jnp.float32)
    gain_query = gain_query.astype(jnp.float32)
    gain_key = gain_key.astype(jnp.float32)
    full_in, full_down = (
        lax.all_gather(expert_in.astype(jnp.bfloat16), "group", axis=0, tiled=True),
        lax.all_gather(expert_down.astype(jnp.bfloat16), "group", axis=0, tiled=True),
    )
    width = tokens.shape[1]
    groups = lax.axis_size("expert")
    slice_len = LEN // groups
    seq_count = tokens.shape[0] // slice_len
    row_count = tokens.shape[0]
    experts_all = router_weight.shape[1]
    local_experts = experts_all // groups
    capacity = 2 * row_count * TOP // experts_all
    expert_width = full_down.shape[0]
    offset = lax.axis_index("expert") * slice_len
    cosine, sine = rope_tables((offset + jnp.arange(slice_len)).astype(jnp.float32))
    head_scale = HEAD_DIM ** (-0.5)
    xfloat = tokens.astype(jnp.float32)
    scale_one = row_scale(xfloat)
    normed_one = xfloat * scale_one
    hidden_one = (normed_one * gain_one).astype(jnp.bfloat16)
    query_lin = jnp.dot(hidden_one, full_query, preferred_element_type=jnp.float32)
    key_lin = jnp.dot(hidden_one, full_key, preferred_element_type=jnp.float32)
    value_bf = jnp.dot(hidden_one, full_value, preferred_element_type=jnp.float32).astype(
        jnp.bfloat16
    )
    scale_query = row_scale(query_lin)
    query_normed = query_lin * scale_query
    scale_key = row_scale(key_lin)
    key_normed = key_lin * scale_key
    heads_shape = (seq_count, slice_len, HEADS, HEAD_DIM)
    query_bf = (
        rotate((query_normed * gain_query).reshape(heads_shape), cosine, sine) * head_scale
    ).astype(jnp.bfloat16)
    key_bf = rotate((key_normed * gain_key).reshape(heads_shape), cosine, sine).astype(jnp.bfloat16)
    key_all, value_all = (
        lax.all_gather(key_bf.reshape(seq_count, slice_len, width), "expert", axis=1, tiled=True),
        lax.all_gather(value_bf.reshape(seq_count, slice_len, width), "expert", axis=1, tiled=True),
    )
    key_all = key_all.reshape(seq_count, LEN, HEADS, HEAD_DIM)
    value_all = value_all.reshape(seq_count, LEN, HEADS, HEAD_DIM)
    masked = masked_scores(query_bf, key_all, prefix, offset, slice_len)
    peak = jnp.max(masked, -1, keepdims=True)
    expo = jnp.exp(masked - peak)
    totals = jnp.sum(expo, -1, keepdims=True)
    probs_bf = (expo / totals).astype(jnp.bfloat16)
    logsum = peak + jnp.log(totals)
    attended = jnp.einsum(
        "shqk,skhd->sqhd", probs_bf, value_all, preferred_element_type=jnp.float32
    )
    attended_bf = attended.astype(jnp.bfloat16).reshape(row_count, width)
    resid = xfloat + jnp.dot(attended_bf, full_output, preferred_element_type=jnp.float32)
    scale_two = row_scale(resid)
    normed_two = resid * scale_two
    hidden_two = (normed_two * gain_two).astype(jnp.bfloat16)
    logits = jnp.dot(hidden_two, full_router, preferred_element_type=jnp.float32)
    router_probs = jax.nn.softmax(logits, -1)
    expert_ids = jnp.arange(experts_all)
    onehot = (routes[:, :, None] == expert_ids[None, None, :]).astype(jnp.float32)
    gates = jnp.sum(onehot * router_probs[:, None, :], -1)
    flat_routes = routes.reshape(-1)
    flat_hot = (flat_routes[:, None] == expert_ids[None, :]).astype(jnp.int32)
    before = jnp.cumsum(flat_hot, 0) - flat_hot
    places = flat_routes * capacity + jnp.sum(before * flat_hot, 1)
    slot_shape = (groups, local_experts, capacity, width)
    outgoing = (
        jnp.zeros((experts_all * capacity, width), jnp.bfloat16)
        .at[places]
        .set(jnp.repeat(hidden_two, TOP, 0))
    )
    received = lax.all_to_all(
        outgoing.reshape(slot_shape), "expert", split_axis=0, concat_axis=0, tiled=True
    )
    both = jnp.einsum("sjcd,djf->sjcf", received, full_in, preferred_element_type=jnp.float32)
    gate_part = both[..., :expert_width]
    up_part = both[..., expert_width:]
    sigma = jax.nn.sigmoid(gate_part)
    silu_val = gate_part * sigma
    hidden_exp = (silu_val * up_part).astype(jnp.bfloat16)
    result = jnp.einsum(
        "sjcf,fjd->sjcd", hidden_exp, full_down, preferred_element_type=jnp.float32
    ).astype(jnp.bfloat16)
    returned = lax.all_to_all(result, "expert", split_axis=0, concat_axis=0, tiled=True).reshape(
        experts_all * capacity, width
    )
    per_choice = returned[places].reshape(row_count, TOP, width).astype(jnp.float32)
    output = (resid + jnp.sum(gates[:, :, None] * per_choice, 1)).astype(jnp.bfloat16)
    grad_out = cotangent.astype(jnp.float32)
    grad_gates = jnp.sum(grad_out[:, None, :] * per_choice, -1)
    grad_choice = (
        (gates[:, :, None] * grad_out[:, None, :])
        .astype(jnp.bfloat16)
        .reshape(row_count * TOP, width)
    )
    grad_outgoing = (
        jnp.zeros((experts_all * capacity, width), jnp.bfloat16).at[places].set(grad_choice)
    )
    grad_received = lax.all_to_all(
        grad_outgoing.reshape(slot_shape), "expert", split_axis=0, concat_axis=0, tiled=True
    )
    grad_hidden = jnp.einsum(
        "sjcd,fjd->sjcf", grad_received, full_down, preferred_element_type=jnp.float32
    )
    grad_gate = grad_hidden * up_part * (sigma * (1.0 + gate_part * (1.0 - sigma)))
    grad_up = grad_hidden * silu_val
    grad_both = jnp.concatenate([grad_gate, grad_up], -1).astype(jnp.bfloat16)
    grad_rows = jnp.einsum(
        "sjcf,djf->sjcd", grad_both, full_in, preferred_element_type=jnp.float32
    ).astype(jnp.bfloat16)
    grad_returned = lax.all_to_all(
        grad_rows, "expert", split_axis=0, concat_axis=0, tiled=True
    ).reshape(experts_all * capacity, width)
    grad_from_experts = jnp.sum(
        grad_returned[places].reshape(row_count, TOP, width).astype(jnp.float32), 1
    )
    piece = received
    grad_in = lax.psum_scatter(
        jnp.einsum("sjcd,sjcf->djf", piece, grad_both, preferred_element_type=jnp.float32).astype(
            jnp.bfloat16
        ),
        "group",
        scatter_dimension=0,
        tiled=True,
    ).astype(jnp.float32)
    piece = hidden_exp
    grad_down = lax.psum_scatter(
        jnp.einsum(
            "sjcf,sjcd->fjd", piece, grad_received, preferred_element_type=jnp.float32
        ).astype(jnp.bfloat16),
        "group",
        scatter_dimension=0,
        tiled=True,
    ).astype(jnp.float32)
    grad_probs = jnp.sum(grad_gates[:, :, None] * onehot, 1)
    grad_logits = (
        router_probs * (grad_probs - jnp.sum(grad_probs * router_probs, -1, keepdims=True))
    ).astype(jnp.bfloat16)
    grad_router_term = outer_sum(hidden_two, grad_logits)
    grad_two = grad_from_experts + back_product(grad_logits, full_router)
    gain_two_term = jnp.sum(grad_two * normed_two, 0)
    grad_resid = grad_out + norm_back(resid, scale_two, grad_two * gain_two)
    grad_attn_out = grad_resid.astype(jnp.bfloat16)
    grad_output_term = outer_sum(attended_bf, grad_attn_out)
    grad_attended = (
        back_product(grad_attn_out, full_output).astype(jnp.bfloat16).reshape(heads_shape)
    )
    again = masked_scores(query_bf, key_all, prefix, offset, slice_len)
    probs_again = jnp.exp(again - logsum)
    probs_again_bf = probs_again.astype(jnp.bfloat16)
    grad_weights = jnp.einsum(
        "sqhd,skhd->shqk", grad_attended, value_all, preferred_element_type=jnp.float32
    )
    grad_scores = (
        probs_again * (grad_weights - jnp.sum(grad_weights * probs_again, -1, keepdims=True))
    ).astype(jnp.bfloat16)
    grad_query_rot = jnp.einsum(
        "shqk,skhd->sqhd", grad_scores, key_all, preferred_element_type=jnp.float32
    )
    key_term = jnp.einsum(
        "shqk,sqhd->skhd", grad_scores, query_bf, preferred_element_type=jnp.float32
    )
    value_term = jnp.einsum(
        "shqk,sqhd->skhd", probs_again_bf, grad_attended, preferred_element_type=jnp.float32
    )
    grad_key_rot, grad_value_lin = (
        lax.psum_scatter(
            key_term.reshape(seq_count, LEN, width).astype(jnp.bfloat16),
            "expert",
            scatter_dimension=1,
            tiled=True,
        ).astype(jnp.float32),
        lax.psum_scatter(
            value_term.reshape(seq_count, LEN, width).astype(jnp.bfloat16),
            "expert",
            scatter_dimension=1,
            tiled=True,
        ).astype(jnp.float32),
    )
    grad_query_normed = unrotate(grad_query_rot * head_scale, cosine, sine).reshape(
        row_count, width
    )
    query_gain_term = jnp.sum(grad_query_normed * query_normed, 0)
    grad_query_lin = norm_back(query_lin, scale_query, grad_query_normed * gain_query).astype(
        jnp.bfloat16
    )
    grad_key_normed = unrotate(grad_key_rot.reshape(heads_shape), cosine, sine).reshape(
        row_count, width
    )
    key_gain_term = jnp.sum(grad_key_normed * key_normed, 0)
    grad_key_lin = norm_back(key_lin, scale_key, grad_key_normed * gain_key).astype(jnp.bfloat16)
    grad_value_bf = grad_value_lin.reshape(row_count, width).astype(jnp.bfloat16)
    grad_query_term = outer_sum(hidden_one, grad_query_lin)
    grad_key_term = outer_sum(hidden_one, grad_key_lin)
    grad_value_term = outer_sum(hidden_one, grad_value_bf)
    grad_hidden_one = (
        back_product(grad_query_lin, full_query)
        + back_product(grad_key_lin, full_key)
        + back_product(grad_value_bf, full_value)
    )
    gain_one_term = jnp.sum(grad_hidden_one * normed_one, 0)
    grad_tokens = grad_resid + norm_back(xfloat, scale_one, grad_hidden_one * gain_one)
    dense_terms = (
        grad_query_term,
        grad_key_term,
        grad_value_term,
        grad_output_term,
        grad_router_term,
        gain_one_term,
        gain_two_term,
        query_gain_term,
        key_gain_term,
    )
    shards = (
        lax.psum_scatter(
            dense_terms[0].astype(jnp.bfloat16), "group", scatter_dimension=0, tiled=True
        ).astype(jnp.float32),
        lax.psum_scatter(
            dense_terms[1].astype(jnp.bfloat16), "group", scatter_dimension=0, tiled=True
        ).astype(jnp.float32),
        lax.psum_scatter(
            dense_terms[2].astype(jnp.bfloat16), "group", scatter_dimension=0, tiled=True
        ).astype(jnp.float32),
        lax.psum_scatter(
            dense_terms[3].astype(jnp.bfloat16), "group", scatter_dimension=0, tiled=True
        ).astype(jnp.float32),
        lax.psum_scatter(
            dense_terms[4].astype(jnp.bfloat16), "group", scatter_dimension=0, tiled=True
        ).astype(jnp.float32),
        lax.psum_scatter(
            dense_terms[5].astype(jnp.bfloat16), "group", scatter_dimension=0, tiled=True
        ).astype(jnp.float32),
        lax.psum_scatter(
            dense_terms[6].astype(jnp.bfloat16), "group", scatter_dimension=0, tiled=True
        ).astype(jnp.float32),
        lax.psum_scatter(
            dense_terms[7].astype(jnp.bfloat16), "group", scatter_dimension=0, tiled=True
        ).astype(jnp.float32),
        lax.psum_scatter(
            dense_terms[8].astype(jnp.bfloat16), "group", scatter_dimension=0, tiled=True
        ).astype(jnp.float32),
    )
    shards = (
        lax.psum(shards[0].astype(jnp.bfloat16), "expert").astype(jnp.float32),
        lax.psum(shards[1].astype(jnp.bfloat16), "expert").astype(jnp.float32),
        lax.psum(shards[2].astype(jnp.bfloat16), "expert").astype(jnp.float32),
        lax.psum(shards[3].astype(jnp.bfloat16), "expert").astype(jnp.float32),
        lax.psum(shards[4].astype(jnp.bfloat16), "expert").astype(jnp.float32),
        lax.psum(shards[5].astype(jnp.bfloat16), "expert").astype(jnp.float32),
        lax.psum(shards[6].astype(jnp.bfloat16), "expert").astype(jnp.float32),
        lax.psum(shards[7].astype(jnp.bfloat16), "expert").astype(jnp.float32),
        lax.psum(shards[8].astype(jnp.bfloat16), "expert").astype(jnp.float32),
    )
    return (
        output,
        grad_tokens,
        shards[0],
        shards[1],
        shards[2],
        shards[3],
        shards[4],
        shards[5],
        shards[6],
        shards[7],
        shards[8],
        grad_in,
        grad_down,
    )


def solution(mesh):
    in_specs = (
        P(("group", "expert"), None),
        P(("group", "expert"), None),
        P("group"),
        P("group", None),
        P("group", None),
        P("group", None),
        P("group", None),
        P("group", None),
        P("group"),
        P("group"),
        P("group"),
        P("group"),
        P("group", "expert", None),
        P("group", "expert", None),
        P(("group", "expert"), None),
    )
    out_specs = (
        P(("group", "expert"), None),
        P(("group", "expert"), None),
        P("group", None),
        P("group", None),
        P("group", None),
        P("group", None),
        P("group", None),
        P("group"),
        P("group"),
        P("group"),
        P("group"),
        P("group", "expert", None),
        P("group", "expert", None),
    )
    return jax.shard_map(body, mesh=mesh, in_specs=in_specs, out_specs=out_specs, check_vma=False)
```

profile of v0, /device:TPU:0, one launch (start us, length us, event | category | flops | bytes accessed | tf_op | source)
XLA Modules:
  0.0 3033.9 jit_solution(5109961156575843449)
XLA Ops:
  14.3 10.4 all-gather.3
  24.7 8.9 all-gather.2
  33.6 7.9 all-gather.1
  43.0 24.6 all-gather.18.cloned.1.call-done
  67.6 5.9 multiply_reduce_fusion.6
  75.4 49.1 %all-gather.16.cloned.1.call-done = bf16[2048,2048]{1,0:T(8,128)(2,1)} async-done(((bf16[256,2048]{1,0:T(8,128)(2,1)}), bf16[2048,2048]{1,0:T(8,128)(2,1)}) %all-gather.16.cloned.1.call-update) | async-done | bytes 8388624 | tf_op jit(solution)/shard_map/all_gather | solution.py:94
  124.5 5.9 multiply_reduce_fusion.7
  140.2 41.2 %all-gather.14.cloned.1.call-done = bf16[2048,2048]{1,0:T(8,128)(2,1)} async-done(((bf16[256,2048]{1,0:T(8,128)(2,1)}), bf16[2048,2048]{1,0:T(8,128)(2,1)}) %all-gather.14.cloned.1.call-update) | async-done | bytes 8388624 | tf_op jit(solution)/shard_map/all_gather | solution.py:96
  181.4 6.7 convolution_convert_fusion.6
  189.4 10.5 copy.239
  201.6 9.1 all-gather.4
  219.6 44.4 %all-gather.20.cloned.1.call-done = bf16[1,1024,2048]{1,2,0:T(8,128)(2,1)} async-done(((bf16[1,256,2048]{1,2,0:T(8,128)(2,1)}), bf16[1,1024,2048]{1,2,0:T(8,128)(2,1)}) %all-gather.20.cloned.1.call-update) | async-done | bytes 4194320 | tf_op jit(solution)/shard_map/all_gather | solution.py:143
  268.5 6.6 copy-done
  279.1 65.9 %all-gather.28.cloned.1.call-done = bf16[1024,2048]{1,0:T(8,128)(2,1)} async-done(((bf16[256,2048]{1,0:T(8,128)(2,1)}), bf16[1024,2048]{1,0:T(8,128)(2,1)}) %all-gather.28.cloned.1.call-update) | async-done | bytes 4194320 | tf_op jit(solution)/shard_map/all_gather | solution.py:144
  345.0 10.7 fusion.64
  355.7 44.5 %all-gather.22.cloned.1.call-done = bf16[2048,2048]{1,0:T(8,128)(2,1)} async-done(((bf16[256,2048]{1,0:T(8,128)(2,1)}), bf16[2048,2048]{1,0:T(8,128)(2,1)}) %all-gather.22.cloned.1.call-update) | async-done | bytes 8388624 | tf_op jit(solution)/shard_map/all_gather | solution.py:97
  400.2 5.8 multiply_reduce_fusion.5
  407.7 21.7 scatter_custom_fusion
  429.4 7.0 all-to-all-start
  436.7 5.7 copy.240
  444.0 9.5 all_gather.49
  455.3 23.0 scatter_custom_fusion.1
  478.3 321.7 %all-to-all-done = bf16[4,4,256,2048]{3,2,1,0:T(8,128)(2,1)} async-done(((bf16[4,4,256,2048]{3,2,1,0:T(8,128)(2,1)}), bf16[4,4,256,2048]{3,2,1,0:T(8,128)(2,1)}, u32[]{:S(2)}, u32[]{:S(2)}) %all-to-all-start) | async-done | bytes 16777248 | tf_op jit(solution)/shard_map/all_to_all | solution.py:177
  800.0 7.5 all-to-all-start.2
  807.5 43.2 %fusion.5 = f32[4,4,256,2048]{3,2,0,1:T(8,128)} fusion(bf16[2048,4,2048]{2,0,1:T(8,128)(2,1)} %all-gather.24.cloned.1.call-done, bf16[4,4,256,2048]{3,2,1,0:T(8,128)(2,1)} %all-to-all-done), kind=kOutput, calls=%fused_computation.13 | convolution fusion | flops 34359738368 | bytes 83886080 | tf_op jit(solution)/shard_map/sjcd,djf->sjcf/dot_general | solution.py:180
  850.7 319.5 %all-to-all-done.2 = bf16[4,4,256,2048]{3,2,1,0:T(8,128)(2,1)} async-done(((bf16[4,4,256,2048]{3,2,1,0:T(8,128)(2,1)}), bf16[4,4,256,2048]{3,2,1,0:T(8,128)(2,1)}, u32[]{:S(2)}, u32[]{:S(2)}) %all-to-all-start.2) | async-done | bytes 16777248 | tf_op jit(solution)/shard_map/all_to_all | solution.py:204
  1170.2 36.6 %fusion.11 = (bf16[4,4,256,1024]{3,2,0,1:T(8,128)(2,1)}, bf16[4,4,256,1024]{3,2,0,1:T(8,128)(2,1)}, bf16[4,4,256,1024]{3,2,0,1:T(8,128)(2,1)}) fusion(f32[4,4,256,2048]{3,2,0,1:T(8,128)} %fusion.5, bf16[1024,4,2048]{2,0,1:T(8,128)(2,1)} %all-gather.26.cloned.1.call-done, bf16[4,4,256,2048]{3,2,1,0:T(8,128)(2,1)} %all-to-all-done.2), kind=kOutput, calls=%fused_computation.21 | convolution fusion | flops 17242783744 | bytes 92274688 | tf_op jit(solution)/shard_map/sjcd,fjd->sjcf/dot_general | solution.py:207
  1206.8 27.5 convert_bitcast_fusion.1
  1234.3 14.1 copy.159
  1248.4 7.1 all-to-all-start.1
  1255.5 43.3 %convert_bitcast_fusion = bf16[4,4,256,2048]{3,2,0,1:T(8,128)(2,1)} fusion(bf16[2048,4,2048]{2,0,1:T(8,128)(2,1)} %all-gather.24.cloned.1.call-done, bf16[4,4,256,1024]{3,2,0,1:T(8,128)(2,1)} %get-tuple-element.102, bf16[4,4,256,1024]{3,2,0,1:T(8,128)(2,1)} %get-tuple-element.101), kind=kOutput, calls=%fused_computation.33 | convolution fusion | flops 34401681408 | bytes 67108864 | tf_op jit(solution)/shard_map/sjcf,djf->sjcd/dot_general | solution.py:213
  1298.8 14.1 copy.162
  1312.9 304.9 %all-to-all-done.1 = bf16[4,4,256,2048]{3,2,1,0:T(8,128)(2,1)} async-done(((bf16[4,4,256,2048]{3,2,1,0:T(8,128)(2,1)}), bf16[4,4,256,2048]{3,2,1,0:T(8,128)(2,1)}, u32[]{:S(2)}, u32[]{:S(2)}) %all-to-all-start.1) | async-done | bytes 16777248 | tf_op jit(solution)/shard_map/all_to_all | solution.py:189
  1617.9 7.0 all-to-all-start.3
  1625.2 24.4 gather_fusion
  1649.7 9.5 fusion.9
  1659.3 327.9 %all-to-all-done.3 = bf16[4,4,256,2048]{3,2,1,0:T(8,128)(2,1)} async-done(((bf16[4,4,256,2048]{3,2,1,0:T(8,128)(2,1)}), bf16[4,4,256,2048]{3,2,1,0:T(8,128)(2,1)}, u32[]{:S(2)}, u32[]{:S(2)}) %all-to-all-start.3) | async-done | bytes 16777248 | tf_op jit(solution)/shard_map/all_to_all | solution.py:216
  1987.2 24.7 gather_fusion.1
  2012.0 11.5 convert_reduce_fusion
  2032.6 9.5 fusion.49
  2042.2 14.2 multiply_reduce_fusion
  2056.4 12.1 multiply_convert_fusion
  2074.8 5.6 convolution_convert_fusion
  2080.6 36.7 %reduce-scatter.14.cloned.1.call-done = bf16[1,256,2048]{1,2,0:T(8,128)(2,1)} async-done(((bf16[1,1024,2048]{1,2,0:T(8,128)(2,1)}), bf16[1,256,2048]{1,2,0:T(8,128)(2,1)}) %reduce-scatter.14.cloned.1.call-update) | async-done | bytes 1048592 | tf_op jit(solution)/shard_map/reduce_scatter | solution.py:278
  2117.2 7.0 convolution_convert_fusion.1
  2124.6 7.8 multiply_bitcast_fusion
  2132.3 65.0 %reduce-scatter.12.cloned.1.call-done = bf16[1,256,2048]{1,2,0:T(8,128)(2,1)} async-done(((bf16[1,1024,2048]{1,2,0:T(8,128)(2,1)}), bf16[1,256,2048]{1,2,0:T(8,128)(2,1)}) %reduce-scatter.12.cloned.1.call-update) | async-done | bytes 1048592 | tf_op jit(solution)/shard_map/reduce_scatter | solution.py:272
  2206.5 5.5 multiply_add_fusion
  2217.5 5.8 convolution_convert_fusion.2
  2231.8 5.7 convolution_convert_fusion.3
  2237.6 25.3 bitcast_convert_fusion.1
  2263.0 21.3 copy.189
  2286.6 61.0 %reduce-scatter.20.cloned.1.call-done = bf16[256,2048]{1,0:T(8,128)(2,1)} async-done(((bf16[2048,2048]{1,0:T(8,128)(2,1)}), bf16[256,2048]{1,0:T(8,128)(2,1)}) %reduce-scatter.20.cloned.1.call-update) | async-done | bytes 1048592 | tf_op jit(solution)/shard_map/reduce_scatter | solution.py:326
  2347.6 74.8 %reduce-scatter.18.cloned.1.call-done = bf16[256,2048]{1,0:T(8,128)(2,1)} async-done(((bf16[2048,2048]{1,0:T(8,128)(2,1)}), bf16[256,2048]{1,0:T(8,128)(2,1)}) %reduce-scatter.18.cloned.1.call-update) | async-done | bytes 1048592 | tf_op jit(solution)/shard_map/reduce_scatter | solution.py:323
  2422.4 75.0 %reduce-scatter.16.cloned.1.call-done = bf16[256,2048]{1,0:T(8,128)(2,1)} async-done(((bf16[2048,2048]{1,0:T(8,128)(2,1)}), bf16[256,2048]{1,0:T(8,128)(2,1)}) %reduce-scatter.16.cloned.1.call-update) | async-done | bytes 1048592 | tf_op jit(solution)/shard_map/reduce_scatter | solution.py:320
  2497.7 45.7 %fusion.4 = bf16[2048,4,2048]{0,2,1:T(8,128)(2,1)} fusion(bf16[4,4,256,2048]{3,2,1,0:T(8,128)(2,1)} %all-to-all-done, bf16[4,4,256,1024]{3,2,0,1:T(8,128)(2,1)} %get-tuple-element.102, bf16[4,4,256,1024]{3,2,0,1:T(8,128)(2,1)} %get-tuple-element.101), kind=kOutput, calls=%fused_computation.10 | convolution fusion | flops 34410070016 | bytes 67108864 | tf_op jit(solution)/shard_map/sjcd,sjcf->djf/dot_general | solution.py:224
  2545.3 71.6 %reduce-scatter.28.cloned.1.call-done = bf16[128,8192]{1,0:T(8,128)(2,1)} async-done(((bf16[1024,8192]{1,0:T(8,128)(2,1)}), bf16[128,8192]{1,0:T(8,128)(2,1)}) %reduce-scatter.28.cloned.1.call-update) | async-done | bytes 2097168
  2623.2 6.2 fusion.95
  2629.5 5.9 convolution_add_fusion.2
  2639.5 23.0 all-reduce.4
  2662.9 20.6 all-reduce.5
  2689.8 121.1 %all-reduce.9.cloned.1.call-done = (bf16[256,2048]{1,0:T(8,128)(2,1)}, bf16[256,2048]{1,0:T(8,128)(2,1)}, bf16[256,2048]{1,0:T(8,128)(2,1)}, bf16[256,2048]{1,0:T(8,128)(2,1)}) async-done(((bf16[256,2048]{1,0:T(8,128)(2,1)}, bf16[256,2048]{1,0:T(8,128)(2,1)}, bf16[256,2048]{1,0:T(8,128)(2,1)}, bf16[256,2048]{1,0:T(8,128)(2,1)}), (bf16[256,2048]{1,0:T(8,128)(2,1)}, bf16[256,2048]{1,0:T(8,128)(2,1)}, ...) | async-done | bytes 4194320 | tf_op jit(solution)/shard_map/psum | solution.py:349
  2819.8 198.8 %reduce-scatter.26.cloned.1.call-done = bf16[256,4,2048]{0,2,1:T(8,128)(2,1)} async-done(((bf16[2048,4,2048]{0,2,1:T(8,128)(2,1)}), bf16[256,4,2048]{0,2,1:T(8,128)(2,1)}) %reduce-scatter.26.cloned.1.call-update) | async-done | bytes 4194320 | tf_op jit(solution)/shard_map/reduce_scatter | solution.py:223
  3018.6 8.3 copy.177
  (322 shorter events, 113.8 us)
Async XLA Ops:
  7.2 60.4 %all-gather.18.cloned.1.call-start = ((), (), s32[]{:S(2)}) async-start(), calls=%async_computation.15 | async-start | bytes 9437184 | tf_op jit(solution)/shard_map/all_gather | solution.py:95
  10.1 31.4 %copy-start.2 = (bf16[256,2048]{1,0:T(8,128)(2,1)S(1)}, bf16[256,2048]{1,0:T(8,128)(2,1)}, u32[]{:S(2)}) copy-start(bf16[256,2048]{1,0:T(8,128)(2,1)} %param.15) | copy-start | bytes 3145732
  10.2 114.4 %all-gather.16.cloned.1.call-start = ((), (), s32[]{:S(2)}) async-start(), calls=%async_computation.14 | async-start | bytes 9437184 | tf_op jit(solution)/shard_map/all_gather | solution.py:94
  11.4 170.0 %all-gather.14.cloned.1.call-start = ((), (), s32[]{:S(2)}) async-start(), calls=%async_computation.13 | async-start | bytes 9437184 | tf_op jit(solution)/shard_map/all_gather | solution.py:96
  14.1 249.8 %all-gather.20.cloned.1.call-start = ((), (), s32[]{:S(2)}) async-start(), calls=%async_computation.16 | async-start | bytes 5242880 | tf_op jit(solution)/shard_map/all_gather | solution.py:143
  24.7 49.5 %copy-start.50 = (f32[8,1,256]{2,1,0:T(1,128)}, f32[8,1,256]{2,1,0:T(1,128)S(1)}, u32[]{:S(2)}) copy-start(f32[8,1,256]{2,1,0:T(1,128)S(1)} %convert_element_type.398) | copy-start | bytes 24580
  33.6 97.4 %copy-start.48 = (f32[8,1,256]{2,1,0:T(1,128)}, f32[8,1,256]{2,1,0:T(1,128)S(1)}, u32[]{:S(2)}) copy-start(f32[8,1,256]{2,1,0:T(1,128)S(1)} %convert_element_type.397) | copy-start | bytes 24580
  41.5 139.9 %copy-start.40 = (f32[8,1,256]{2,1,0:T(1,128)}, f32[8,1,256]{2,1,0:T(1,128)S(1)}, u32[]{:S(2)}) copy-start(f32[8,1,256]{2,1,0:T(1,128)S(1)} %convert_element_type.396) | copy-start | bytes 24580
  42.4 139.0 %copy-start.58 = (f32[256]{0:T(256)}, f32[256]{0:T(256)S(1)}, u32[]{:S(2)}) copy-start(f32[256]{0:T(256)S(1)} %get-tuple-element.127) | copy-start | bytes 3076
  43.0 90.1 %copy-start.31 = (f32[256,64]{1,0:T(8,128)}, f32[256,64]{1,0:T(8,128)S(1)}, u32[]{:S(2)}) copy-start(f32[256,64]{1,0:T(8,128)S(1)} %get-tuple-element.124) | copy-start | bytes 196612
  43.0 90.1 %copy-start.33 = (f32[256,64]{1,0:T(8,128)}, f32[256,64]{1,0:T(8,128)S(1)}, u32[]{:S(2)}) copy-start(f32[256,64]{1,0:T(8,128)S(1)} %get-tuple-element.125) | copy-start | bytes 196612
  139.6 48.6 %copy-start.30 = (f32[256,2048]{1,0:T(8,128)S(1)}, f32[256,2048]{1,0:T(8,128)}, u32[]{:S(2)}) copy-start(f32[256,2048]{1,0:T(8,128)} %param.21) | copy-start | bytes 6291460
  139.6 205.3 %all-gather.28.cloned.1.call-start = ((), (), s32[]{:S(2)}) async-start(), calls=%async_computation.28 | async-start | bytes 5242880 | tf_op jit(solution)/shard_map/all_gather | solution.py:144
  188.2 212.1 %all-gather.22.cloned.1.call-start = ((), (), s32[]{:S(2)}) async-start(), calls=%async_computation.17 | async-start | bytes 9437184 | tf_op jit(solution)/shard_map/all_gather | solution.py:97
  189.4 618.1 %all-gather.24.cloned.1.call-start = ((), (), s32[]{:S(2)}) async-start(), calls=%async_computation.18 | async-start | bytes 37748736 | tf_op jit(solution)/shard_map/all_gather | solution.py:109
  210.7 196.0 %copy-start.54 = (f32[8,1,256]{2,1,0:T(1,128)}, f32[8,1,256]{2,1,0:T(1,128)S(1)}, u32[]{:S(2)}) copy-start(f32[8,1,256]{2,1,0:T(1,128)S(1)} %convert_element_type.399) | copy-start | bytes 24580
  216.6 128.4 %copy-start.19 = (pred[256,1024]{1,0:T(8,128)(4,1)}, pred[256,1024]{1,0:T(8,128)(4,1)S(1)}, u32[]{:S(2)}) copy-start(pred[256,1024]{1,0:T(8,128)(4,1)S(1)} %fusion.69) | copy-start | bytes 786436
  216.6 238.7 %copy-start.60 = (s32[2048,1]{0,1:T(1,128)}, s32[2048,1]{0,1:T(1,128)S(1)}, u32[]{:S(2)}) copy-start(s32[2048,1]{0,1:T(1,128)S(1)} %compare_select_fusion) | copy-start | bytes 24580
  219.6 49.0 %copy-start.6 = (bf16[256,16,128]{2,0,1:T(8,128)(2,1)}, bf16[256,16,128]{2,0,1:T(8,128)(2,1)S(1)}, u32[]{:S(2)}) copy-start(bf16[256,16,128]{2,0,1:T(8,128)(2,1)S(1)} %fusion.63) | copy-start | bytes 3145732
  268.5 6.6 copy-start
  268.5 76.4 %copy-start.46 = (f32[16,256]{1,0:T(8,128)}, f32[16,256]{1,0:T(8,128)S(1)}, u32[]{:S(2)}) copy-start(f32[16,256]{1,0:T(8,128)S(1)} %get-tuple-element.138) | copy-start | bytes 49156
  279.1 76.6 %copy-start.56 = (f32[16,256]{1,0:T(8,128)}, f32[16,256]{1,0:T(8,128)S(1)}, u32[]{:S(2)}) copy-start(f32[16,256]{1,0:T(8,128)S(1)} %fusion.20) | copy-start | bytes 49156
  355.7 50.4 %copy-start.23 = (bf16[16,128,256]{2,1,0:T(8,128)(2,1)}, bf16[16,128,256]{2,1,0:T(8,128)(2,1)S(1)}, u32[]{:S(2)}) copy-start(bf16[16,128,256]{2,1,0:T(8,128)(2,1)S(1)} %fusion.64) | copy-start | bytes 3145732
  407.6 45.8 %copy-start.17 = (bf16[256,2048]{1,0:T(8,128)(2,1)}, bf16[256,2048]{1,0:T(8,128)(2,1)S(1)}, u32[]{:S(2)}) copy-start(bf16[256,2048]{1,0:T(8,128)(2,1)S(1)} %multiply_convert_fusion.2) | copy-start | bytes 3145732
  429.4 370.6 %all-to-all-start = ((bf16[4,4,256,2048]{3,2,1,0:T(8,128)(2,1)}), bf16[4,4,256,2048]{3,2,1,0:T(8,128)(2,1)}, u32[]{:S(2)}, u32[]{:S(2)}) async-start(bf16[4,4,256,2048]{3,2,1,0:T(8,128)(2,1)} %bitcast.214), calls=%async_computation | async-start | bytes 33554432 | tf_op jit(solution)/shard_map/all_to_all | solution.py:177
  436.5 414.2 %all-gather.26.cloned.1.call-start = ((), (), s32[]{:S(2)}) async-start(), calls=%async_computation.19 | async-start | bytes 18874368 | tf_op jit(solution)/shard_map/all_gather | solution.py:110
  444.0 34.4 %copy-start.8 = (f32[256,2048]{1,0:T(8,128)}, f32[256,2048]{1,0:T(8,128)S(1)}, u32[]{:S(2)}) copy-start(f32[256,2048]{1,0:T(8,128)S(1)} %convert_element_type.348) | copy-start | bytes 6291460
  455.2 23.1 copy-start.35
  800.0 370.2 %all-to-all-start.2 = ((bf16[4,4,256,2048]{3,2,1,0:T(8,128)(2,1)}), bf16[4,4,256,2048]{3,2,1,0:T(8,128)(2,1)}, u32[]{:S(2)}, u32[]{:S(2)}) async-start(bf16[4,4,256,2048]{3,2,1,0:T(8,128)(2,1)} %bitcast.215), calls=%async_computation.2 | async-start | bytes 33554432 | tf_op jit(solution)/shard_map/all_to_all | solution.py:204
  1248.4 369.5 %all-to-all-start.1 = ((bf16[4,4,256,2048]{3,2,1,0:T(8,128)(2,1)}), bf16[4,4,256,2048]{3,2,1,0:T(8,128)(2,1)}, u32[]{:S(2)}, u32[]{:S(2)}) async-start(bf16[4,4,256,2048]{3,2,1,0:T(8,128)(2,1)} %copy.159), calls=%async_computation.1 | async-start | bytes 33554432 | tf_op jit(solution)/shard_map/all_to_all | solution.py:189
  1312.9 312.2 %copy-start.61 = (s32[2048,1]{0,1:T(1,128)S(1)}, s32[2048,1]{0,1:T(1,128)}, u32[]{:S(2)}) copy-start(s32[2048,1]{0,1:T(1,128)} %copy-done.60) | copy-start | bytes 24580
  1312.9 312.2 %copy-start.47 = (f32[16,256]{1,0:T(8,128)S(1)}, f32[16,256]{1,0:T(8,128)}, u32[]{:S(2)}) copy-start(f32[16,256]{1,0:T(8,128)} %copy-done.46) | copy-start | bytes 49156
  1312.9 312.3 %copy-start.57 = (f32[16,256]{1,0:T(8,128)S(1)}, f32[16,256]{1,0:T(8,128)}, u32[]{:S(2)}) copy-start(f32[16,256]{1,0:T(8,128)} %copy-done.56) | copy-start | bytes 49156
  1617.9 369.4 %all-to-all-start.3 = ((bf16[4,4,256,2048]{3,2,1,0:T(8,128)(2,1)}), bf16[4,4,256,2048]{3,2,1,0:T(8,128)(2,1)}, u32[]{:S(2)}, u32[]{:S(2)}) async-start(bf16[4,4,256,2048]{3,2,1,0:T(8,128)(2,1)} %copy.162), calls=%async_computation.3 | async-start | bytes 33554432 | tf_op jit(solution)/shard_map/all_to_all | solution.py:216
  1624.9 492.3 %reduce-scatter.14.cloned.1.call-start = ((), (), s32[]{:S(2)}) async-start(), calls=%async_computation.21 | async-start | bytes 5242880 | tf_op jit(solution)/shard_map/reduce_scatter | solution.py:278
  1625.2 24.4 copy-start.9
  1625.2 24.4 copy-start.36
  1649.6 9.6 copy-start.53
  1649.6 9.6 copy-start.45
  1649.6 9.6 copy-start.63
  1649.7 9.6 copy-start.67
  2011.9 11.5 copy-start.5
  2011.9 11.5 copy-start.43
  2012.0 11.5 copy-start.55
  2012.0 11.5 copy-start.74
  2012.0 14.6 copy-start.25
  2042.2 155.2 %reduce-scatter.12.cloned.1.call-start = ((), (), s32[]{:S(2)}) async-start(), calls=%async_computation.20 | async-start | bytes 5242880 | tf_op jit(solution)/shard_map/reduce_scatter | solution.py:272
  2056.4 12.1 copy-start.7
  2073.0 213.6 %reduce-scatter.22.cloned.1.call-start = ((), (), s32[]{:S(2)}) async-start(), calls=%async_computation.25 | async-start | bytes 9437184 | tf_op jit(solution)/shard_map/reduce_scatter | solution.py:329
  2080.5 36.8 %copy-start.3 = (bf16[256,2048]{1,0:T(8,128)(2,1)S(1)}, bf16[256,2048]{1,0:T(8,128)(2,1)}, u32[]{:S(2)}) copy-start(bf16[256,2048]{1,0:T(8,128)(2,1)} %param.15) | copy-start | bytes 3145732
  2080.5 36.8 %copy-start.41 = (f32[8,1,256]{2,1,0:T(1,128)S(1)}, f32[8,1,256]{2,1,0:T(1,128)}, u32[]{:S(2)}) copy-start(f32[8,1,256]{2,1,0:T(1,128)} %copy-done.40) | copy-start | bytes 24580
  2080.5 36.8 %copy-start.59 = (f32[256]{0:T(256)S(1)}, f32[256]{0:T(256)}, u32[]{:S(2)}) copy-start(f32[256]{0:T(256)} %copy-done.58) | copy-start | bytes 3076
  2080.5 267.1 %reduce-scatter.20.cloned.1.call-start = ((), (), s32[]{:S(2)}) async-start(), calls=%async_computation.24 | async-start | bytes 9437184 | tf_op jit(solution)/shard_map/reduce_scatter | solution.py:326
  2124.3 298.1 %reduce-scatter.18.cloned.1.call-start = ((), (), s32[]{:S(2)}) async-start(), calls=%async_computation.23 | async-start | bytes 9437184 | tf_op jit(solution)/shard_map/reduce_scatter | solution.py:323
  2200.1 6.4 copy-start.34
  2223.3 274.1 %reduce-scatter.16.cloned.1.call-start = ((), (), s32[]{:S(2)}) async-start(), calls=%async_computation.22 | async-start | bytes 9437184 | tf_op jit(solution)/shard_map/reduce_scatter | solution.py:320
  2237.6 379.3 %reduce-scatter.28.cloned.1.call-start = ((), (), s32[]{:S(2)}) async-start(), calls=%async_computation.29 | async-start | bytes 18874368
  2284.3 378.6 %reduce-scatter.24.cloned.1.call-start = ((), (), s32[]{:S(2)}) async-start(), calls=%async_computation.26 | async-start | bytes 73728 | tf_op jit(solution)/shard_map/reduce_scatter | solution.py:332
  2286.5 524.4 %all-reduce.9.cloned.1.call-start = ((), (), s32[]{:S(2)}) async-start(), calls=%async_computation.30 | async-start | bytes 8388608 | tf_op jit(solution)/shard_map/psum | solution.py:349
  2497.4 521.1 %reduce-scatter.26.cloned.1.call-start = ((), (), s32[]{:S(2)}) async-start(), calls=%async_computation.27 | async-start | bytes 37748736 | tf_op jit(solution)/shard_map/reduce_scatter | solution.py:223
  2623.2 12.2 slice-start.2
  2635.5 50.9 %copy-start.12 = (f32[256,2048]{1,0:T(8,128)S(1)}, f32[256,2048]{1,0:T(8,128)}, u32[]{:S(2)}) copy-start(f32[256,2048]{1,0:T(8,128)} %copy-done.10) | copy-start | bytes 6291460
  2635.5 50.9 %copy-start.75 = (f32[256]{0:T(256)S(1)}, f32[256]{0:T(256)}, u32[]{:S(2)}) copy-start(f32[256]{0:T(256)} %get-tuple-element.126) | copy-start | bytes 3076
  2810.9 7.3 copy-start.37
  (46 other events, 128.3 us)
Sparse Core Ops, SparseCore 0:
  10.5 57.0 all-gather.17
  70.1 54.3 all-gather.15
  127.0 54.3 all-gather.13
  183.4 80.5 all-gather.19
  266.0 78.9 all-gather.27
  347.3 52.9 all-gather.21
  402.7 160.9 all-gather.23
  566.2 89.8 all-gather.25
  2042.3 74.9 reduce-scatter.13
  2120.1 77.2 reduce-scatter.11
  2200.8 71.7 reduce-scatter.21
  2276.3 71.2 reduce-scatter.19
  2351.1 71.2 reduce-scatter.17
  2426.1 71.2 reduce-scatter.15
  2500.8 115.9 reduce-scatter.27
  2620.3 31.3 reduce-scatter.23
  2654.3 156.5 all-reduce.8
  2814.3 204.1 reduce-scatter.25
where the time goes:
time: 3040 us; the launch traced here: 3030 us
  waiting for transfers between devices  2250 us (74%)
  matrix products  344 us (11%)
  local copies, waits for them, and re-layouts  188 us (6%)
  other arithmetic  117 us (4%)
  blocking collectives  89.3 us (3%)
  starting transfers between devices  31.1 us (1%)
    all_to_all x1, waiting for transfers between devices, body(): lax.all_to_all(grad_rows, 'expert', split_axis=0, concat_axis=0, tiled=True)  328 us
    all_to_all x1, waiting for transfers between devices, body(): lax.all_to_all(outgoing.reshape(slot_shape), 'expert', split_axis=0, conc...  322 us
    all_to_all x1, waiting for transfers between devices, body(): lax.all_to_all(grad_outgoing.reshape(slot_shape), 'expert', split_axis=0,...  320 us
    all_to_all x1, waiting for transfers between devices, body(): lax.all_to_all(result, 'expert', split_axis=0, concat_axis=0, tiled=True)  305 us
    reduce_scatter x1, waiting for transfers between devices, body(): lax.psum_scatter(jnp.einsum('sjcd,sjcf->djf', piece, grad_both, preferred...  199 us
    psum x1, waiting for transfers between devices, body(): lax.psum(shards[0].astype(jnp.bfloat16), 'expert').astype(jnp.float32)  121 us
    unnamed x196, local copies, waits for them, and re-layouts  79.1 us
    reduce_scatter x1, waiting for transfers between devices, body(): lax.psum_scatter(dense_terms[0].astype(jnp.bfloat16), 'group', scatter_di...  75 us
  transfers between devices with their start and end apart: 22, of which 18 were waited for; matrix products, arithmetic and copies ran while one was open for 16% of the time, Pallas kernels for 0%

commit v1 on v0

v1 whole, which is shorter than its diff:
```python
import functools
import math

import jax
import jax.numpy as jnp
from jax import lax
from jax.experimental import pallas as pl
from jax.experimental.pallas import tpu as pltpu
from jax.sharding import PartitionSpec as P

HEADS = 16
HEAD_DIM = 128
LEN = 1024
MAX_PREFIX = LEN // 2
QBLOCK = 256
EPS = 1e-05
THETA = 10000.0
BF = jnp.bfloat16
F32 = jnp.float32


def dot(left, right):
    return jnp.dot(left, right, preferred_element_type=F32)


def dot_nt(left, right):
    return lax.dot_general(left, right, (((1,), (1,)), ((), ())), preferred_element_type=F32)


def dot_tn(left, right):
    return lax.dot_general(left, right, (((0,), (0,)), ((), ())), preferred_element_type=F32)


def row_scale(values):
    return lax.rsqrt(jnp.mean(values * values, -1, keepdims=True) + EPS)


def norm_back(values, scale_rows, upstream):
    inner = jnp.mean(upstream * values, -1, keepdims=True)
    return scale_rows * upstream - values * (scale_rows * scale_rows * scale_rows) * inner


def shift(value, count, step):
    return lax.ppermute(value, "expert", [(i, (i + step) % count) for i in range(count)])


def ring_gather(value, count, here):
    rows = value.shape[0]
    whole = jnp.zeros((count * rows,) + value.shape[1:], value.dtype)
    for step in range(count):
        if step:
            value = shift(value, count, 1)
        whole = lax.dynamic_update_slice(whole, value, (((here - step) % count) * rows, 0))
    return whole


def ring_scatter(term, count, here):
    total = term((here - 1) % count)
    for step in range(1, count):
        arrived = shift(total.astype(BF), count, 1)
        total = term((here - 1 - step) % count) + arrived.astype(F32)
    return total


def exchange_sum(value, count):
    total = value
    for step in range(1, count):
        total = total + shift(value, count, step)
    return total


def key_limit(block):
    return max((block + 1) * QBLOCK, MAX_PREFIX)


def visible(block, limit, prefix):
    row = block * QBLOCK + lax.broadcasted_iota(jnp.int32, (QBLOCK, limit), 0)
    col = lax.broadcasted_iota(jnp.int32, (QBLOCK, limit), 1)
    return (col <= row) | (col < prefix)


def attend_kernel(prefix_ref, ql, kl, vb, sq, sk, gq, gk, cos, sin, ob, qb, kb, lse):
    prefix = prefix_ref[0]
    c, s = cos[...], sin[...]
    qn = ql[...] * sq[...] * gq[...]
    kn = kl[...] * sk[...] * gk[...]
    half = HEAD_DIM // 2
    qb[...] = ((qn * c + pltpu.roll(qn, half, 1) * s) * HEAD_DIM ** (-0.5)).astype(BF)
    kb[...] = (kn * c + pltpu.roll(kn, half, 1) * s).astype(BF)
    for block in range(LEN // QBLOCK):
        rows = slice(block * QBLOCK, (block + 1) * QBLOCK)
        limit = key_limit(block)
        scores = dot_nt(qb[rows, :], kb[:limit, :])
        scores = jnp.where(visible(block, limit, prefix), scores, -1e30)
        peak = jnp.max(scores, -1, keepdims=True)
        expo = jnp.exp(scores - peak)
        total = jnp.sum(expo, -1, keepdims=True)
        ob[rows, :] = (dot(expo.astype(BF), vb[:limit, :]) / total).astype(BF)
        lse[0, rows, :] = peak + jnp.log(total)


def attend(prefix, ql, kl, vb, sq, sk, gq, gk, cos, sin):
    heads = ql.shape[1] // HEAD_DIM
    col = pl.BlockSpec((LEN, HEAD_DIM), lambda h, p: (0, h))
    one = pl.BlockSpec((LEN, 1), lambda h, p: (0, 0))
    gain = pl.BlockSpec((1, HEAD_DIM), lambda h, p: (0, h))
    table = pl.BlockSpec((LEN, HEAD_DIM), lambda h, p: (0, 0))
    return pl.pallas_call(
        attend_kernel,
        out_shape=[jax.ShapeDtypeStruct(ql.shape, BF)] * 3
        + [jax.ShapeDtypeStruct((heads, LEN, 1), F32)],
        grid_spec=pltpu.PrefetchScalarGridSpec(
            num_scalar_prefetch=1,
            grid=(heads,),
            in_specs=[col, col, col, one, one, gain, gain, table, table],
            out_specs=[col, col, col, pl.BlockSpec((1, LEN, 1), lambda h, p: (h, 0, 0))],
        ),
        cost_estimate=pl.CostEstimate(
            flops=heads * LEN * LEN * HEAD_DIM * 3, bytes_accessed=16 << 20, transcendentals=heads * LEN * LEN
        ),
        name="attend",
    )(prefix, ql, kl, vb, sq, sk, gq, gk, cos, sin)


def attend_back_kernel(
    prefix_ref, qb, kb, vb, dob, lse, ql, kl, sq, sk, gq, gk, cos, sin,
    wq, wk, dv, inner, gain_q, gain_k, dq_sum, dk_sum, dv_sum,
):
    prefix = prefix_ref[0]
    dk_sum[...] = jnp.zeros_like(dk_sum)
    dv_sum[...] = jnp.zeros_like(dv_sum)
    for block in range(LEN // QBLOCK):
        rows = slice(block * QBLOCK, (block + 1) * QBLOCK)
        limit = key_limit(block)
        scores = dot_nt(qb[rows, :], kb[:limit, :])
        weights = jnp.where(visible(block, limit, prefix), jnp.exp(scores - lse[0, rows, :]), 0.0)
        grad = dob[rows, :]
        dweights = dot_nt(grad, vb[:limit, :])
        dscores = (weights * (dweights - jnp.sum(dweights * weights, -1, keepdims=True))).astype(BF)
        dq_sum[rows, :] = dot(dscores, kb[:limit, :])
        dk_sum[:limit, :] += dot_tn(dscores, qb[rows, :])
        dv_sum[:limit, :] += dot_tn(weights.astype(BF), grad)
    dv[...] = dv_sum[...].astype(BF)
    c, s = cos[...], sin[...]
    half = HEAD_DIM // 2
    dq = dq_sum[...] * HEAD_DIM ** (-0.5)
    dqn = dq * c - pltpu.roll(dq, half, 1) * s
    dk = dk_sum[...]
    dkn = dk * c - pltpu.roll(dk, half, 1) * s
    gain_q[...] = jnp.sum(dqn * (ql[...] * sq[...]), 0, keepdims=True)
    gain_k[...] = jnp.sum(dkn * (kl[...] * sk[...]), 0, keepdims=True)
    dqn = dqn * gq[...]
    dkn = dkn * gk[...]
    wq[...] = dqn
    wk[...] = dkn
    part = jnp.concatenate(
        [jnp.sum(dqn * ql[...], -1, keepdims=True), jnp.sum(dkn * kl[...], -1, keepdims=True)], 1
    )

    @pl.when(pl.program_id(0) == 0)
    def _():
        inner[...] = part

    @pl.when(pl.program_id(0) > 0)
    def _():
        inner[...] += part


def attend_back(prefix, qb, kb, vb, dob, lse, ql, kl, sq, sk, gq, gk, cos, sin):
    heads = ql.shape[1] // HEAD_DIM
    col = pl.BlockSpec((LEN, HEAD_DIM), lambda h, p: (0, h))
    one = pl.BlockSpec((LEN, 1), lambda h, p: (0, 0))
    gain = pl.BlockSpec((1, HEAD_DIM), lambda h, p: (0, h))
    table = pl.BlockSpec((LEN, HEAD_DIM), lambda h, p: (0, 0))
    return pl.pallas_call(
        attend_back_kernel,
        out_shape=[
            jax.ShapeDtypeStruct(ql.shape, F32),
            jax.ShapeDtypeStruct(ql.shape, F32),
            jax.ShapeDtypeStruct(ql.shape, BF),
            jax.ShapeDtypeStruct((LEN, 2), F32),
            jax.ShapeDtypeStruct((1, ql.shape[1]), F32),
            jax.ShapeDtypeStruct((1, ql.shape[1]), F32),
        ],
        grid_spec=pltpu.PrefetchScalarGridSpec(
            num_scalar_prefetch=1,
            grid=(heads,),
            in_specs=[col, col, col, col, pl.BlockSpec((1, LEN, 1), lambda h, p: (h, 0, 0)),
                      col, col, one, one, gain, gain, table, table],
            out_specs=[col, col, col, pl.BlockSpec((LEN, 2), lambda h, p: (0, 0)), gain, gain],
            scratch_shapes=[pltpu.VMEM((LEN, HEAD_DIM), F32)] * 3,
        ),
        cost_estimate=pl.CostEstimate(
            flops=heads * LEN * LEN * HEAD_DIM * 7, bytes_accessed=24 << 20, transcendentals=heads * LEN * LEN
        ),
        name="attend_back",
    )(prefix, qb, kb, vb, dob, lse, ql, kl, sq, sk, gq, gk, cos, sin)


FTILE = 256


def expert_kernel(b, c, wg, wu, wd, gate, hg, dg, du, dgate):
    g = dot(b[...], wg[...])
    u = dot(b[...], wu[...])
    back = dot_nt(c[...], wd[...])
    sigma = jax.nn.sigmoid(g)
    silu = g * sigma
    h = silu * u
    weight = gate[0]
    hg[...] = (weight * h).astype(BF)
    part = jnp.sum(h * back, -1, keepdims=True)
    dh = weight * back
    dg[...] = (dh * u * (sigma * (1.0 + g * (1.0 - sigma)))).astype(BF)
    du[...] = (dh * silu).astype(BF)

    @pl.when(pl.program_id(1) == 0)
    def _():
        dgate[0] = part

    @pl.when(pl.program_id(1) > 0)
    def _():
        dgate[0] += part


def experts(b, c, wg, wu, wd, gate):
    rows, width = b.shape
    count = gate.shape[0]
    ff = wg.shape[1] // count
    tiles = ff // FTILE
    whole = pl.BlockSpec((rows, width), lambda j, f: (0, 0), pipeline_mode=pl.Buffered(1))
    up = pl.BlockSpec((width, FTILE), lambda j, f: (0, j * tiles + f))
    one = pl.BlockSpec((1, rows, 1), lambda j, f: (j, 0, 0))
    out = pl.BlockSpec((rows, FTILE), lambda j, f: (0, j * tiles + f))
    return pl.pallas_call(
        expert_kernel,
        grid=(count, tiles),
        in_specs=[whole, whole, up, up, pl.BlockSpec((FTILE, width), lambda j, f: (f, j)), one],
        out_specs=[out, out, out, one],
        out_shape=[jax.ShapeDtypeStruct((rows, count * ff), BF)] * 3
        + [jax.ShapeDtypeStruct((count, rows, 1), F32)],
        cost_estimate=pl.CostEstimate(
            flops=6 * rows * width * count * ff, bytes_accessed=80 << 20, transcendentals=rows * count * ff
        ),
        name="experts",
    )(b, c, wg, wu, wd, gate)


def down_kernel(hg, wd, out, total):
    j = pl.program_id(0)

    @pl.when(j == 0)
    def _():
        total[...] = dot(hg[...], wd[...])

    @pl.when(j > 0)
    def _():
        total[...] += dot(hg[...], wd[...])

    @pl.when(j == pl.num_programs(0) - 1)
    def _():
        out[...] = total[...]


def down(hg, wd, width):
    rows = hg.shape[0]
    ff = wd.shape[0]
    count = hg.shape[1] // ff
    return pl.pallas_call(
        down_kernel,
        grid=(count,),
        in_specs=[
            pl.BlockSpec((rows, ff), lambda j: (0, j)),
            pl.BlockSpec((ff, width), lambda j: (0, j)),
        ],
        out_specs=pl.BlockSpec((rows, width), lambda j: (0, 0), pipeline_mode=pl.Buffered(1)),
        out_shape=jax.ShapeDtypeStruct((rows, width), F32),
        scratch_shapes=[pltpu.VMEM((rows, width), F32)],
        cost_estimate=pl.CostEstimate(
            flops=2 * rows * width * count * ff, bytes_accessed=40 << 20, transcendentals=0
        ),
        name="down",
    )(hg, wd)


def body(
    tokens,
    routes,
    prefix,
    query_weight,
    key_weight,
    value_weight,
    output_weight,
    router_weight,
    attention_gain,
    feedforward_gain,
    query_gain,
    key_gain,
    expert_in,
    expert_down,
    cotangent,
):
    count = lax.axis_size("expert")
    here = lax.axis_index("expert")
    group_here = lax.axis_index("group")
    rows, width = tokens.shape
    cols = width // count
    experts_all = router_weight.shape[1]
    local = expert_in.shape[1]
    ff_rows = expert_down.shape[0]
    ff = expert_in.shape[2] // 2
    master = query_weight.shape[0]

    def gather(value):
        return lax.all_gather(value, "group", axis=0, tiled=True)

    def scatter(value):
        return lax.psum_scatter(value, "group", scatter_dimension=0, tiled=True)

    def own_cols(weight):
        return lax.dynamic_slice(weight, (0, here * cols), (master, cols)).astype(BF)

    small = jnp.concatenate(
        [
            jnp.stack([attention_gain, feedforward_gain, query_gain, key_gain]),
            jnp.zeros((4, master), F32),
            router_weight.T,
        ]
    ).astype(BF)
    small = lax.all_gather(small, "group", axis=1, tiled=True).astype(F32)
    gain_one, gain_two = small[0:1], small[1:2]
    gain_query = lax.dynamic_slice(small[2:3], (0, here * cols), (1, cols))
    gain_key = lax.dynamic_slice(small[3:4], (0, here * cols), (1, cols))
    router = small[8:].astype(BF)
    qkv_weight = gather(
        jnp.concatenate([own_cols(query_weight), own_cols(key_weight), own_cols(value_weight)], 1)
    )
    out_weight = gather(output_weight.astype(BF))
    gate_weight = gather(expert_in[:, :, :ff].astype(BF).reshape(master, local * ff))
    up_weight = gather(expert_in[:, :, ff:].astype(BF).reshape(master, local * ff))
    down_weight = gather(expert_down.astype(BF).reshape(ff_rows, local * width))

    expert_ids = jnp.arange(experts_all, dtype=jnp.int32)
    selected = jnp.sum((routes[:, :, None] == expert_ids).astype(F32), 1)
    sent = jnp.concatenate(
        [tokens, jnp.pad(selected, ((0, 0), (0, 128 - experts_all))).astype(BF)], 1
    )
    sent = ring_gather(sent, count, here)
    x_all = sent[:, :width].astype(F32)
    chosen = sent[:, width : width + experts_all].astype(F32)

    steps = jnp.arange(HEAD_DIM // 2).astype(F32)
    freq = jnp.exp(steps * (-2.0 * math.log(THETA) / HEAD_DIM))
    angle = jnp.arange(LEN).astype(F32)[:, None] * freq[None, :]
    cosine = jnp.concatenate([jnp.cos(angle)] * 2, 1)
    sine = jnp.concatenate([-jnp.sin(angle), jnp.sin(angle)], 1)

    hidden_one = (x_all * row_scale(x_all) * gain_one).astype(BF)
    qkv = dot(hidden_one, qkv_weight)
    query_lin, key_lin = qkv[:, :cols], qkv[:, cols : 2 * cols]
    value_bf = qkv[:, 2 * cols :].astype(BF)
    squares = jnp.stack([jnp.sum(query_lin * query_lin, -1), jnp.sum(key_lin * key_lin, -1)])
    scales = lax.rsqrt(exchange_sum(squares, count) / width + EPS)
    scale_query, scale_key = scales[0][:, None], scales[1][:, None]
    attended, query_bf, key_bf, lse = attend(
        prefix, query_lin, key_lin, value_bf, scale_query, scale_key, gain_query, gain_key, cosine, sine
    )
    attended_bf = jnp.zeros((rows, width), BF)
    for step in range(count):
        block = lax.dynamic_slice(attended, (((here + step) % count) * rows, 0), (rows, cols))
        if step:
            block = shift(block, count, step)
        attended_bf = lax.dynamic_update_slice(attended_bf, block, (0, ((here - step) % count) * cols))

    cot, attended_bf = lax.optimization_barrier((cotangent, attended_bf))
    cot_all = ring_gather(cot, count, here)

    xfloat = tokens.astype(F32)
    resid = xfloat + dot(attended_bf, out_weight)
    scale_two = row_scale(resid)
    normed_two = resid * scale_two
    hidden_two = (normed_two * gain_two).astype(BF)
    b_all = ring_gather(hidden_two, count, here)
    probs = jax.nn.softmax(dot_nt(b_all, router), -1)
    gates = lax.dynamic_slice(probs * chosen, (0, here * local), (LEN, local))
    hg, dg, du, dgate = experts(b_all, cot_all, gate_weight, up_weight, down_weight, gates.T[:, :, None])

    dgate = dgate[:, :, 0].T * lax.dynamic_slice(chosen, (0, here * local), (LEN, local))
    dprobs = lax.dynamic_update_slice(jnp.zeros((LEN, 128), F32), dgate, (0, here * local))
    grad_down = jnp.einsum(
        "tjf,td->fjd", hg.reshape(LEN, local, ff), cot_all, preferred_element_type=F32
    ).astype(BF).reshape(ff, local * width)
    grad_down = scatter(grad_down).astype(F32).reshape(ff_rows, local, width)

    def back_term(block):
        at = block * rows
        left = lax.dynamic_slice(dg, (at, 0), (rows, local * ff))
        right = lax.dynamic_slice(du, (at, 0), (rows, local * ff))
        return jnp.concatenate(
            [
                dot_nt(left, gate_weight) + dot_nt(right, up_weight),
                lax.dynamic_slice(dprobs, (at, 0), (rows, 128)),
            ],
            1,
        )

    back = ring_scatter(back_term, count, here)
    grad_gate = scatter(dot_tn(b_all, dg).astype(BF))
    grad_up = scatter(dot_tn(b_all, du).astype(BF))
    grad_in = jnp.concatenate(
        [grad_gate.reshape(master, local, ff), grad_up.reshape(master, local, ff)], 2
    ).astype(F32)

    own_probs = jax.nn.softmax(dot_nt(hidden_two, router), -1)
    grad_probs = back[:, width : width + experts_all]
    grad_logits = (
        own_probs * (grad_probs - jnp.sum(grad_probs * own_probs, -1, keepdims=True))
    ).astype(BF)
    grad_router = dot_tn(grad_logits, hidden_two)
    grad_two = back[:, :width] + dot(grad_logits, router)
    gain_two_term = jnp.sum(grad_two * normed_two, 0)
    grad_out = cotangent.astype(F32)
    grad_resid = grad_out + norm_back(resid, scale_two, grad_two * gain_two)
    grad_attn_out = grad_resid.astype(BF)
    grad_attended = dot_nt(grad_attn_out, out_weight).astype(BF)
    heads_grad = jnp.zeros((LEN, cols), BF)
    for step in range(count):
        block = lax.dynamic_slice(grad_attended, (0, ((here + step) % count) * cols), (rows, cols))
        if step:
            block = shift(block, count, step)
        heads_grad = lax.dynamic_update_slice(heads_grad, block, (((here - step) % count) * rows, 0))
    grad_out_weight = scatter(dot_tn(attended_bf, grad_attn_out).astype(BF))

    wq, wk, dvl, inner, gain_q_term, gain_k_term = attend_back(
        prefix, query_bf, key_bf, value_bf, heads_grad, lse, query_lin, key_lin,
        scale_query, scale_key, gain_query, gain_key, cosine, sine,
    )
    inner = exchange_sum(inner.T, count) / width
    dql = scale_query * wq - query_lin * (scale_query**3 * inner[0][:, None])
    dkl = scale_key * wk - key_lin * (scale_key**3 * inner[1][:, None])
    dqkv = jnp.concatenate([dql.astype(BF), dkl.astype(BF), dvl], 1)

    def token_term(block):
        return dot_nt(lax.dynamic_slice(dqkv, (block * rows, 0), (rows, 3 * cols)), qkv_weight)

    grad_hidden = ring_scatter(token_term, count, here)
    grad_qkv = scatter(dot_tn(hidden_one, dqkv).astype(BF))

    partial, grad_hidden = lax.optimization_barrier((down(hg, down_weight, width), grad_hidden))

    def down_term(block):
        return lax.dynamic_slice(partial, (block * rows, 0), (rows, width))

    output = (resid + ring_scatter(down_term, count, here)).astype(BF)

    scale_one = row_scale(xfloat)
    gain_one_term = jnp.sum(grad_hidden * (xfloat * scale_one), 0)
    grad_tokens = grad_resid + norm_back(xfloat, scale_one, grad_hidden * gain_one)

    def own_part(value):
        return lax.dynamic_slice(value, (0, group_here * master), (value.shape[0], master))

    def spread(value):
        return lax.dynamic_update_slice(jnp.zeros((1, width), F32), value, (0, here * cols))

    sums = jnp.concatenate(
        [
            gain_one_term[None],
            gain_two_term[None],
            spread(gain_q_term),
            spread(gain_k_term),
            jnp.zeros((4, width), F32),
            grad_router,
        ]
    )
    sums = own_part(lax.psum(sums, ("group", "expert")))
    grad_out_weight = lax.psum(grad_out_weight, "expert").astype(F32)
    grad_qkv = lax.all_gather(grad_qkv, "expert", axis=0, tiled=False)
    grad_q, grad_k, grad_v = [
        grad_qkv[:, :, i * cols : (i + 1) * cols].transpose(1, 0, 2).reshape(master, width).astype(F32)
        for i in range(3)
    ]
    return (
        output,
        grad_tokens,
        grad_q,
        grad_k,
        grad_v,
        grad_out_weight,
        sums[8:].T,
        sums[0],
        sums[1],
        sums[2],
        sums[3],
        grad_in,
        grad_down,
    )


def solution(mesh):
    in_specs = (
        P(("group", "expert"), None),
        P(("group", "expert"), None),
        P("group"),
        P("group", None),
        P("group", None),
        P("group", None),
        P("group", None),
        P("group", None),
        P("group"),
        P("group"),
        P("group"),
        P("group"),
        P("group", "expert", None),
        P("group", "expert", None),
        P(("group", "expert"), None),
    )
    out_specs = (
        P(("group", "expert"), None),
        P(("group", "expert"), None),
        P("group", None),
        P("group", None),
        P("group", None),
        P("group", None),
        P("group", None),
        P("group"),
        P("group"),
        P("group"),
        P("group"),
        P("group", "expert", None),
        P("group", "expert", None),
    )
    return jax.shard_map(body, mesh=mesh, in_specs=in_specs, out_specs=out_specs, check_vma=False)
```

time: 3040 us -> 1500 us (0.49)
  waiting for transfers between devices: 2250 us -> 841 us
  Pallas kernels: 0 us -> 127 us
  matrix products: 344 us -> 236 us
  blocking collectives: 89.3 us -> 9.71 us
  local copies, waits for them, and re-layouts: 188 us -> 122 us
  other arithmetic: 117 us -> 70.3 us
  starting transfers between devices: 31.1 us -> 70.3 us
    all_to_all x4 -> x0, waiting for transfers between devices: 1270 us -> none  [the longest x1 328 us: body(): lax.all_to_all(grad_rows, 'expert', split_axis=0, concat_axis=0, tiled=True)]
    ppermute x0 -> x30, waiting for transfers between devices: none -> 417 us  [shift(): lax.ppermute(value, 'expert', [(i, (i + step) % count) for i in range(cou...]
    reduce_scatter x8 -> x4, waiting for transfers between devices: 511 us -> 229 us  [scatter(): return lax.psum_scatter(value, 'group', scatter_dimension=0, tiled=True)]
    all_gather x8 -> x6, waiting for transfers between devices: 270 us -> 61.7 us  [the longest x1 61.6 us: body(): grad_qkv = lax.all_gather(grad_qkv, 'expert', axis=0, tiled=False)]
    pallas_call x0 -> x4, Pallas kernels: none -> 127 us  [the longest x1 66 us: experts(): pl.pallas_call(expert_kernel, grid=(count, tiles), in_specs=[whole, whole...]
    dot_general x27 -> x24, matrix products: 344 us -> 236 us  [the longest x15 125 us: dot_nt(): lax.dot_general(left, right, (((1,), (1,)), ((), ())), preferred_element_...]
    psum x1 -> x2, waiting for transfers between devices: 121 us -> 21.2 us  [the longest x1 21.2 us: body(): grad_out_weight = lax.psum(grad_out_weight, 'expert').astype(F32)]
    ppermute x0 -> x30, starting transfers between devices: none -> 69.1 us  [shift(): lax.ppermute(value, 'expert', [(i, (i + step) % count) for i in range(cou...]
  transfers between devices with their start and end apart: 22 -> 43, of which waited for: 18 -> 29; matrix products, arithmetic and copies ran while one was open for 16% -> 23% of each run, Pallas kernels for 0% -> 4%
where the time goes in v1:
time: 1500 us; the launch traced here: 1490 us
  waiting for transfers between devices  841 us (56%)
  matrix products  236 us (16%)
  Pallas kernels  127 us (8%)
  local copies, waits for them, and re-layouts  122 us (8%)
  starting transfers between devices  70.3 us (5%)
  other arithmetic  70.3 us (5%)
  between operations  16.2 us (1%)
    ppermute x30, waiting for transfers between devices, shift(): lax.ppermute(value, 'expert', [(i, (i + step) % count) for i in range(cou...  417 us
    reduce_scatter x4, waiting for transfers between devices, scatter(): return lax.psum_scatter(value, 'group', scatter_dimension=0, tiled=True)  229 us
    dot_general x15, matrix products, dot_nt(): lax.dot_general(left, right, (((1,), (1,)), ((), ())), preferred_element_...  125 us
    unnamed x14, waiting for transfers between devices  113 us
    ppermute x30, starting transfers between devices, shift(): lax.ppermute(value, 'expert', [(i, (i + step) % count) for i in range(cou...  69.1 us
    dot_general x5, matrix products, dot_tn(): lax.dot_general(left, right, (((0,), (0,)), ((), ())), preferred_element_...  68.4 us
    pallas_call x1, Pallas kernels, experts(): pl.pallas_call(expert_kernel, grid=(count, tiles), in_specs=[whole, whole...  66 us
    all_gather x1, waiting for transfers between devices, body(): grad_qkv = lax.all_gather(grad_qkv, 'expert', axis=0, tiled=False)  61.6 us
  transfers between devices with their start and end apart: 43, of which 29 were waited for; matrix products, arithmetic and copies ran while one was open for 23% of the time, Pallas kernels for 4%

profile of v1, /device:TPU:0, one launch (start us, length us, event | category | flops | bytes accessed | tf_op | source)
XLA Modules:
  0.0 1493.6 jit_solution(6438424783306974883)
XLA Ops:
  12.5 5.6 convert.54
  37.6 26.8 %collective-permute-done = bf16[256,2176]{1,0:T(8,128)(2,1)} collective-permute-done((bf16[256,2176]{1,0:T(8,128)(2,1)S(1)}, bf16[256,2176]{1,0:T(8,128)(2,1)}, u32[]{:S(2)}, u32[]{:S(2)}) %collective-permute-start) | collective-permute-done | bytes 1114144 | tf_op jit(solution)/shard_map/ppermute | solution.py:44
  64.5 9.7 all_gather.24
  77.5 14.6 collective-permute-done.1
  97.0 22.0 %collective-permute-done.2 = bf16[256,2176]{1,0:T(8,128)(2,1)S(1)} collective-permute-done((bf16[256,2176]{1,0:T(8,128)(2,1)}, bf16[256,2176]{1,0:T(8,128)(2,1)S(1)}, u32[]{:S(2)}, u32[]{:S(2)}) %collective-permute-start.2) | collective-permute-done | bytes 1114144 | tf_op jit(solution)/shard_map/ppermute | solution.py:44
  123.2 10.7 fusion.44
  143.2 3.9 collective-permute-start.5
  147.3 12.1 collective-permute-done.5
  159.4 15.8 %collective-permute-done.4 = f32[2,1024]{0,1:T(8,128)S(1)} collective-permute-done((f32[2,1024]{0,1:T(8,128)S(1)}, f32[2,1024]{0,1:T(8,128)S(1)}, u32[]{:S(2)}, u32[]{:S(2)}) %collective-permute-start.4) | collective-permute-done | bytes 8224 | tf_op jit(solution)/shard_map/ppermute | solution.py:44
  177.1 12.5 attend.1
  198.1 7.0 collective-permute-done.6
  205.1 9.6 collective-permute-done.7
  214.8 28.6 %collective-permute-start.12 = (bf16[256,2048]{1,0:T(8,128)(2,1)}, bf16[256,2048]{1,0:T(8,128)(2,1)}, u32[]{:S(2)}, u32[]{:S(2)}) collective-permute-start(bf16[256,2048]{1,0:T(8,128)(2,1)} %param.29), channel_id=1, source_target_pairs={{0,1},{1,2},{2,3},{3,0},{4,5},{5,6},{6,7},{7,4},{8,9},{9,10},{10,1... | collective-permute-start | bytes 3145736 | tf_op jit(solution)/shard_map/ppermute | solution.py:44
  243.4 6.2 multiply_reduce_fusion.2
  254.4 12.8 collective-permute-done.12
  269.7 19.9 %collective-permute-done.9 = bf16[256,2048]{1,0:T(8,128)(2,1)} collective-permute-done((bf16[256,2048]{1,0:T(8,128)(2,1)S(1)}, bf16[256,2048]{1,0:T(8,128)(2,1)}, u32[]{:S(2)}, u32[]{:S(2)}) %collective-permute-start.9) | collective-permute-done | bytes 1048608 | tf_op jit(solution)/shard_map/ppermute | solution.py:44
  292.2 20.0 %collective-permute-done.13 = bf16[256,2048]{1,0:T(8,128)(2,1)} collective-permute-done((bf16[256,2048]{1,0:T(8,128)(2,1)}, bf16[256,2048]{1,0:T(8,128)(2,1)}, u32[]{:S(2)}, u32[]{:S(2)}) %collective-permute-start.13) | collective-permute-done | bytes 1048608 | tf_op jit(solution)/shard_map/ppermute | solution.py:44
  320.9 13.7 collective-permute-done.10
  337.5 19.6 %collective-permute-done.14 = bf16[256,2048]{1,0:T(8,128)(2,1)} collective-permute-done((bf16[256,2048]{1,0:T(8,128)(2,1)}, bf16[256,2048]{1,0:T(8,128)(2,1)}, u32[]{:S(2)}, u32[]{:S(2)}) %collective-permute-start.14) | collective-permute-done | bytes 1048608 | tf_op jit(solution)/shard_map/ppermute | solution.py:44
  365.7 13.1 collective-permute-done.11
  385.6 8.6 copy.84.gate
  394.1 66.0 %experts.1 = (bf16[1024,4096]{1,0:T(8,128)(2,1)}, bf16[1024,4096]{1,0:T(8,128)(2,1)}, bf16[1024,4096]{1,0:T(8,128)(2,1)}, f32[4,1024,1]{2,1,0:T(8,128)}) custom-call(bf16[1024,2048]{1,0:T(8,128)(2,1)} %constant_dynamic-update-slice_fusion.9.b, bf16[1024,2048]{1,0:T(8,128)(2,1)} %copy-done.15, bf16[2048,4096]{1,0:T(8,128)(2,1)} %all-gather.12.cloned.1.call-done.wg, ...), custom_call_target="tpu_custom_call" | custom-call | flops 51539607552 | bytes 83886080 | tf_op jit(solution)/shard_map/experts/pallas_call | solution.py:235
  460.2 7.6 copy.85
  468.9 4.1 dynamic_update_slice.85
  474.3 12.3 fusion.17
  486.6 11.5 fusion.6
  503.3 12.2 fusion.23
  515.6 12.2 fusion.20
  527.8 13.3 convolution_add_fusion.2
  541.1 12.8 convolution_add_fusion.1
  557.3 12.2 fusion.26
  569.5 15.3 %collective-permute-done.16 = bf16[256,2176]{1,0:T(8,128)(2,1)} collective-permute-done((bf16[256,2176]{1,0:T(8,128)(2,1)}, bf16[256,2176]{1,0:T(8,128)(2,1)}, u32[]{:S(2)}, u32[]{:S(2)}) %collective-permute-start.16) | collective-permute-done | bytes 1114144 | tf_op jit(solution)/shard_map/ppermute | solution.py:44
  588.1 12.8 convolution_add_fusion.3
  600.9 14.0 collective-permute-done.17
  621.7 5.7 convolution_convert_fusion.3
  629.0 6.7 convolution_convert_fusion.6
  636.0 3.9 collective-permute-start.20
  639.9 7.1 collective-permute-done.18
  647.0 6.7 collective-permute-done.19
  654.8 24.1 %attend_back.1 = (f32[1024,512]{1,0:T(8,128)}, f32[1024,512]{1,0:T(8,128)}, bf16[1024,512]{1,0:T(8,128)(2,1)}, f32[1024,2]{1,0:T(8,128)}, f32[1,512]{1,0:T(1,128)}, /*index=5*/f32[1,512]{1,0:T(1,128)}) custom-call(s32[1]{0:T(128)S(6)} %copy.130.prefix_ref, bf16[1024,512]{1,0:T(8,128)(2,1)} %get-tuple-element.35.qb, bf16[1024,512]{1,0:T(8,128)(2,1)} %get-tuple-element.36.kb, ...), custom_call_target="tpu_custom_call" | custom-call | flops 3758096384 | bytes 25165824 | tf_op jit(solution)/shard_map/attend_back/pallas_call | solution.py:175
  685.6 10.1 collective-permute-done.23
  695.7 34.9 %collective-permute-done.22 = f32[2,1024]{0,1:T(8,128)S(1)} collective-permute-done((f32[2,1024]{0,1:T(8,128)}, f32[2,1024]{0,1:T(8,128)S(1)}, u32[]{:S(2)}, u32[]{:S(2)}) %collective-permute-start.22) | collective-permute-done | bytes 8224 | tf_op jit(solution)/shard_map/ppermute | solution.py:44
  735.7 12.2 convolution_convert_fusion.4
  748.2 6.4 convolution_convert_fusion.5
  755.1 24.7 %collective-permute-done.24 = bf16[256,2048]{1,0:T(8,128)(2,1)S(1)} collective-permute-done((bf16[256,2048]{1,0:T(8,128)(2,1)S(1)}, bf16[256,2048]{1,0:T(8,128)(2,1)S(1)}, u32[]{:S(2)}, u32[]{:S(2)}) %collective-permute-start.24) | collective-permute-done | bytes 1048608 | tf_op jit(solution)/shard_map/ppermute | solution.py:44
  782.0 23.4 %collective-permute-done.25 = bf16[256,2048]{1,0:T(8,128)(2,1)S(1)} collective-permute-done((bf16[256,2048]{1,0:T(8,128)(2,1)S(1)}, bf16[256,2048]{1,0:T(8,128)(2,1)S(1)}, u32[]{:S(2)}, u32[]{:S(2)}) %collective-permute-start.25) | collective-permute-done | bytes 1048608 | tf_op jit(solution)/shard_map/ppermute | solution.py:44
  807.3 24.8 %down.1 = f32[1024,2048]{1,0:T(8,128)} custom-call(bf16[1024,4096]{1,0:T(8,128)(2,1)} %get-tuple-element.34.hg, bf16[1024,8192]{1,0:T(8,128)(2,1)} %all-gather.16.cloned.1.call-done.wd), custom_call_target="tpu_custom_call" | custom-call | flops 17179869184 | bytes 41943040 | tf_op jit(solution)/shard_map/down/pallas_call | solution.py:269
  833.5 5.1 convert_add_fusion.1
  842.3 24.8 %convolution_convert_fusion.2 = bf16[2048,4,1024]{2,0,1:T(8,128)(2,1)} fusion(bf16[128,4,8,1024]{3,2,1,0:T(8,128)(2,1)} %bitcast.118, bf16[1024,2048]{1,0:T(8,128)(2,1)} %copy-done.15), kind=kOutput, calls=%fused_computation.2 | convolution fusion | flops 17188257792 | bytes 29360128 | tf_op jit(solution)/shard_map/tjf,td->fjd/dot_general | solution.py:390
  867.1 20.7 %copy.92 = bf16[1024,8192]{1,0:T(8,128)(2,1)} copy(bf16[1024,8192]{0,1:T(8,128)(2,1)} %bitcast.84) | data formatting | bytes 33554432
  888.1 24.6 %convolution_convert_fusion = bf16[2048,4096]{1,0:T(8,128)(2,1)} fusion(bf16[1024,2048]{1,0:T(8,128)(2,1)} %constant_dynamic-update-slice_fusion.9.b, bf16[1024,4096]{1,0:T(8,128)(2,1)} %get-tuple-element.38), kind=kOutput, calls=%fused_computation | convolution fusion | flops 17188257792 | bytes 29360128 | tf_op jit(solution)/shard_map/dot_general | solution.py:31
  913.0 24.6 %convolution_convert_fusion.1 = bf16[2048,4096]{1,0:T(8,128)(2,1)} fusion(bf16[1024,2048]{1,0:T(8,128)(2,1)} %constant_dynamic-update-slice_fusion.9.b, bf16[1024,4096]{1,0:T(8,128)(2,1)} %get-tuple-element.37), kind=kOutput, calls=%fused_computation.1 | convolution fusion | flops 17188257792 | bytes 29360128 | tf_op jit(solution)/shard_map/dot_general | solution.py:31
  939.6 23.8 %collective-permute-done.27 = bf16[256,2048]{1,0:T(8,128)(2,1)S(1)} collective-permute-done((bf16[256,2048]{1,0:T(8,128)(2,1)S(1)}, bf16[256,2048]{1,0:T(8,128)(2,1)S(1)}, u32[]{:S(2)}, u32[]{:S(2)}) %collective-permute-start.27) | collective-permute-done | bytes 1048608 | tf_op jit(solution)/shard_map/ppermute | solution.py:44
  965.3 38.2 %collective-permute-done.28 = bf16[256,2048]{1,0:T(8,128)(2,1)S(1)} collective-permute-done((bf16[256,2048]{1,0:T(8,128)(2,1)S(1)}, bf16[256,2048]{1,0:T(8,128)(2,1)S(1)}, u32[]{:S(2)}, u32[]{:S(2)}) %collective-permute-start.28) | collective-permute-done | bytes 1048608 | tf_op jit(solution)/shard_map/ppermute | solution.py:44
  1007.5 4.3 fusion.13
  1014.6 11.9 collective-permute-done.29
  1029.9 21.2 %all-reduce.4.cloned.1.call-done = bf16[256,2048]{1,0:T(8,128)(2,1)} async-done(((bf16[256,2048]{1,0:T(8,128)(2,1)}), bf16[256,2048]{1,0:T(8,128)(2,1)}) %all-reduce.4.cloned.1.call-update) | async-done | bytes 1048592 | tf_op jit(solution)/shard_map/psum | solution.py:477
  1053.9 61.6 %all-gather.18.cloned.1.call-done = bf16[1024,1536]{1,0:T(8,128)(2,1)} async-done(((bf16[256,1536]{1,0:T(8,128)(2,1)}), bf16[1024,1536]{1,0:T(8,128)(2,1)}) %all-gather.18.cloned.1.call-update) | async-done | bytes 3145744 | tf_op jit(solution)/shard_map/all_gather | solution.py:478
  1122.9 111.2 %reduce-scatter.16.cloned.1.call-done = bf16[128,8192]{1,0:T(8,128)(2,1)} async-done(((bf16[1024,8192]{1,0:T(8,128)(2,1)}), bf16[128,8192]{1,0:T(8,128)(2,1)}) %reduce-scatter.16.cloned.1.call-update) | async-done | bytes 2097168
  1240.5 113.5 %reduce-scatter.14.cloned.1.call-done = bf16[256,4096]{1,0:T(8,128)(2,1)} async-done(((bf16[2048,4096]{1,0:T(8,128)(2,1)}), bf16[256,4096]{1,0:T(8,128)(2,1)}) %reduce-scatter.14.cloned.1.call-update) | async-done | bytes 2097168 | tf_op jit(solution)/shard_map/reduce_scatter | solution.py:318
  1354.0 4.5 reshape.170
  1358.5 115.5 %reduce-scatter.12.cloned.1.call-done = bf16[256,4096]{1,0:T(8,128)(2,1)} async-done(((bf16[2048,4096]{1,0:T(8,128)(2,1)}), bf16[256,4096]{1,0:T(8,128)(2,1)}) %reduce-scatter.12.cloned.1.call-update) | async-done | bytes 2097168 | tf_op jit(solution)/shard_map/reduce_scatter | solution.py:318
  1473.9 4.5 reshape.169
  1478.5 8.1 maximum_convert_fusion
  (264 shorter events, 169.8 us)
Async XLA Ops:
  7.2 116.0 %all-gather.8.cloned.1.call-start = ((), (), s32[]{:S(2)}) async-start(), calls=%async_computation.5 | async-start | bytes 7077888 | tf_op jit(solution)/shard_map/all_gather | solution.py:315
  11.2 232.2 %all-gather.10.cloned.1.call-start = ((), (), s32[]{:S(2)}) async-start(), calls=%async_computation.6 | async-start | bytes 9437184 | tf_op jit(solution)/shard_map/all_gather | solution.py:315
  12.4 381.7 %all-gather.12.cloned.1.call-start = ((), (), s32[]{:S(2)}) async-start(), calls=%async_computation.7 | async-start | bytes 18874368 | tf_op jit(solution)/shard_map/all_gather | solution.py:315
  22.3 371.8 %all-gather.14.cloned.1.call-start = ((), (), s32[]{:S(2)}) async-start(), calls=%async_computation.8 | async-start | bytes 18874368 | tf_op jit(solution)/shard_map/all_gather | solution.py:315
  24.6 369.6 %all-gather.16.cloned.1.call-start = ((), (), s32[]{:S(2)}) async-start(), calls=%async_computation.9 | async-start | bytes 18874368 | tf_op jit(solution)/shard_map/all_gather | solution.py:315
  30.7 810.2 %reduce-scatter.10.cloned.1.call-start = ((), (), s32[]{:S(2)}) async-start(), calls=%async_computation.11 | async-start | bytes 9437184 | tf_op jit(solution)/shard_map/reduce_scatter | solution.py:318
  33.3 31.0 %copy-start.34 = (f32[256]{0:T(256)S(1)}, f32[256]{0:T(256)}, u32[]{:S(2)}) copy-start(f32[256]{0:T(256)} %param.23) | copy-start | bytes 3076
  33.3 31.0 %copy-start.35 = (f32[256]{0:T(256)S(1)}, f32[256]{0:T(256)}, u32[]{:S(2)}) copy-start(f32[256]{0:T(256)} %param.24) | copy-start | bytes 3076
  33.3 31.1 %copy-start.36 = (f32[256]{0:T(256)S(1)}, f32[256]{0:T(256)}, u32[]{:S(2)}) copy-start(f32[256]{0:T(256)} %param.25) | copy-start | bytes 3076
  33.3 31.1 %copy-start.37 = (f32[256]{0:T(256)S(1)}, f32[256]{0:T(256)}, u32[]{:S(2)}) copy-start(f32[256]{0:T(256)} %param.26) | copy-start | bytes 3076
  33.3 31.1 %copy-start.28 = (f32[256,16]{0,1:T(8,128)S(1)}, f32[256,16]{0,1:T(8,128)}, u32[]{:S(2)}) copy-start(f32[256,16]{0,1:T(8,128)} %param.22) | copy-start | bytes 49156
  34.6 29.7 %collective-permute-start = (bf16[256,2176]{1,0:T(8,128)(2,1)S(1)}, bf16[256,2176]{1,0:T(8,128)(2,1)}, u32[]{:S(2)}, u32[]{:S(2)}) collective-permute-start(bf16[256,2176]{1,0:T(8,128)(2,1)S(1)} %get-tuple-element.111), channel_id=1, source_target_pairs={{0,1},{1,2},{2,3},{3,0},{4,5},{5,6},{6,7},{7,4},{8,9},{9,10},{10,1... | collective-permute-start | bytes 3342344 | tf_op jit(solution)/shard_map/ppermute | solution.py:44
  64.3 27.9 %collective-permute-start.1 = (bf16[256,2176]{1,0:T(8,128)(2,1)}, bf16[256,2176]{1,0:T(8,128)(2,1)}, u32[]{:S(2)}, u32[]{:S(2)}) collective-permute-start(bf16[256,2176]{1,0:T(8,128)(2,1)} %collective-permute-done), channel_id=1, source_target_pairs={{0,1},{1,2},{2,3},{3,0},{4,5},{5,6},{6,7},{7,4},{8,9},{9,10},{10,1... | collective-permute-start | bytes 3342344 | tf_op jit(solution)/shard_map/ppermute | solution.py:44
  92.2 26.8 %collective-permute-start.2 = (bf16[256,2176]{1,0:T(8,128)(2,1)}, bf16[256,2176]{1,0:T(8,128)(2,1)S(1)}, u32[]{:S(2)}, u32[]{:S(2)}) collective-permute-start(bf16[256,2176]{1,0:T(8,128)(2,1)} %collective-permute-done.1), channel_id=1, source_target_pairs={{0,1},{1,2},{2,3},{3,0},{4,5},{5,6},{6,7},{7,4},{8,9},{9,10},{10,1... | collective-permute-start | bytes 3342344 | tf_op jit(solution)/shard_map/ppermute | solution.py:44
  92.2 31.0 %copy-start.24 = (f32[1,2048]{1,0:T(1,128)}, f32[1,2048]{1,0:T(1,128)S(1)}, u32[]{:S(2)}) copy-start(f32[1,2048]{1,0:T(1,128)S(1)} %get-tuple-element.133) | copy-start | bytes 24580
  138.9 8.1 collective-permute-start.3
  143.2 16.2 %collective-permute-start.5 = (f32[2,1024]{0,1:T(8,128)S(1)}, f32[2,1024]{0,1:T(8,128)S(1)}, u32[]{:S(2)}, u32[]{:S(2)}) collective-permute-start(f32[2,1024]{0,1:T(8,128)S(1)} %copy.79), channel_id=1, source_target_pairs={{0,3},{1,0},{2,1},{3,2},{4,7},{5,4},{6,5},{7,6},{8,11},{9,8},{10,9... | collective-permute-start | bytes 24584 | tf_op jit(solution)/shard_map/ppermute | solution.py:44
  147.0 28.2 %collective-permute-start.4 = (f32[2,1024]{0,1:T(8,128)S(1)}, f32[2,1024]{0,1:T(8,128)S(1)}, u32[]{:S(2)}, u32[]{:S(2)}) collective-permute-start(f32[2,1024]{0,1:T(8,128)S(1)} %copy.79), channel_id=1, source_target_pairs={{0,2},{1,3},{2,0},{3,1},{4,6},{5,7},{6,4},{7,5},{8,10},{9,11},{10,... | collective-permute-start | bytes 24584 | tf_op jit(solution)/shard_map/ppermute | solution.py:44
  191.8 13.3 collective-permute-start.6
  194.8 19.9 %collective-permute-start.7 = (bf16[256,512]{1,0:T(8,128)(2,1)}, bf16[256,512]{1,0:T(8,128)(2,1)S(1)}, u32[]{:S(2)}, u32[]{:S(2)}) collective-permute-start(bf16[256,512]{1,0:T(8,128)(2,1)} %get-tuple-element.118), channel_id=1, source_target_pairs={{0,2},{1,3},{2,0},{3,1},{4,6},{5,7},{6,4},{7,5},{8,10},{9,11},{10,... | collective-permute-start | bytes 786440 | tf_op jit(solution)/shard_map/ppermute | solution.py:44
  198.1 16.7 %collective-permute-start.8 = (bf16[256,512]{1,0:T(8,128)(2,1)S(1)}, bf16[256,512]{1,0:T(8,128)(2,1)S(1)}, u32[]{:S(2)}, u32[]{:S(2)}) collective-permute-start(bf16[256,512]{1,0:T(8,128)(2,1)S(1)} %get-tuple-element.117), channel_id=1, source_target_pairs={{0,3},{1,0},{2,1},{3,2},{4,7},{5,4},{6,5},{7,6},{8,11},{9,8},{10,9... | collective-permute-start | bytes 786440 | tf_op jit(solution)/shard_map/ppermute | solution.py:44
  214.8 28.6 %copy-start.12 = (bf16[256,2048]{1,0:T(8,128)(2,1)}, bf16[256,2048]{1,0:T(8,128)(2,1)S(1)}, u32[]{:S(2)}) copy-start(bf16[256,2048]{1,0:T(8,128)(2,1)S(1)} %constant_dynamic-update-slice_fusion.13) | copy-start | bytes 3145732
  214.8 52.4 %collective-permute-start.12 = (bf16[256,2048]{1,0:T(8,128)(2,1)}, bf16[256,2048]{1,0:T(8,128)(2,1)}, u32[]{:S(2)}, u32[]{:S(2)}) collective-permute-start(bf16[256,2048]{1,0:T(8,128)(2,1)} %param.29), channel_id=1, source_target_pairs={{0,1},{1,2},{2,3},{3,0},{4,5},{5,6},{6,7},{7,4},{8,9},{9,10},{10,1... | collective-permute-start | bytes 3145736 | tf_op jit(solution)/shard_map/ppermute | solution.py:44
  249.6 368.8 %copy-start.2 = (f32[256,2048]{1,0:T(8,128)}, f32[256,2048]{1,0:T(8,128)S(1)}, u32[]{:S(2)}) copy-start(f32[256,2048]{1,0:T(8,128)S(1)} %get-tuple-element.142) | copy-start | bytes 6291460
  253.9 104.7 %copy-start.9 = (bf16[256,2048]{1,0:T(8,128)(2,1)}, bf16[256,2048]{1,0:T(8,128)(2,1)S(1)}, u32[]{:S(2)}) copy-start(bf16[256,2048]{1,0:T(8,128)(2,1)S(1)} %get-tuple-element.101) | copy-start | bytes 3145732
  253.9 35.7 %collective-permute-start.9 = (bf16[256,2048]{1,0:T(8,128)(2,1)S(1)}, bf16[256,2048]{1,0:T(8,128)(2,1)}, u32[]{:S(2)}, u32[]{:S(2)}) collective-permute-start(bf16[256,2048]{1,0:T(8,128)(2,1)S(1)} %get-tuple-element.101), channel_id=1, source_target_pairs={{0,1},{1,2},{2,3},{3,0},{4,5},{5,6},{6,7},{7,4},{8,9},{9,10},{10,1... | collective-permute-start | bytes 3145736 | tf_op jit(solution)/shard_map/ppermute | solution.py:44
  267.2 44.9 %collective-permute-start.13 = (bf16[256,2048]{1,0:T(8,128)(2,1)}, bf16[256,2048]{1,0:T(8,128)(2,1)}, u32[]{:S(2)}, u32[]{:S(2)}) collective-permute-start(bf16[256,2048]{1,0:T(8,128)(2,1)} %collective-permute-done.12), channel_id=1, source_target_pairs={{0,1},{1,2},{2,3},{3,0},{4,5},{5,6},{6,7},{7,4},{8,9},{9,10},{10,1... | collective-permute-start | bytes 3145736 | tf_op jit(solution)/shard_map/ppermute | solution.py:44
  289.6 45.0 %collective-permute-start.10 = (bf16[256,2048]{1,0:T(8,128)(2,1)}, bf16[256,2048]{1,0:T(8,128)(2,1)}, u32[]{:S(2)}, u32[]{:S(2)}) collective-permute-start(bf16[256,2048]{1,0:T(8,128)(2,1)} %collective-permute-done.9), channel_id=1, source_target_pairs={{0,1},{1,2},{2,3},{3,0},{4,5},{5,6},{6,7},{7,4},{8,9},{9,10},{10,1... | collective-permute-start | bytes 3145736 | tf_op jit(solution)/shard_map/ppermute | solution.py:44
  312.2 44.9 %collective-permute-start.14 = (bf16[256,2048]{1,0:T(8,128)(2,1)}, bf16[256,2048]{1,0:T(8,128)(2,1)}, u32[]{:S(2)}, u32[]{:S(2)}) collective-permute-start(bf16[256,2048]{1,0:T(8,128)(2,1)} %collective-permute-done.13), channel_id=1, source_target_pairs={{0,1},{1,2},{2,3},{3,0},{4,5},{5,6},{6,7},{7,4},{8,9},{9,10},{10,1... | collective-permute-start | bytes 3145736 | tf_op jit(solution)/shard_map/ppermute | solution.py:44
  334.6 44.1 %collective-permute-start.11 = (bf16[256,2048]{1,0:T(8,128)(2,1)}, bf16[256,2048]{1,0:T(8,128)(2,1)}, u32[]{:S(2)}, u32[]{:S(2)}) collective-permute-start(bf16[256,2048]{1,0:T(8,128)(2,1)} %collective-permute-done.10), channel_id=1, source_target_pairs={{0,1},{1,2},{2,3},{3,0},{4,5},{5,6},{6,7},{7,4},{8,9},{9,10},{10,1... | collective-permute-start | bytes 3145736 | tf_op jit(solution)/shard_map/ppermute | solution.py:44
  500.0 53.9 %collective-permute-start.15 = (bf16[256,2176]{1,0:T(8,128)(2,1)}, bf16[256,2176]{1,0:T(8,128)(2,1)}, u32[]{:S(2)}, u32[]{:S(2)}) collective-permute-start(bf16[256,2176]{1,0:T(8,128)(2,1)} %pad_maximum_fusion.1), channel_id=1, source_target_pairs={{0,1},{1,2},{2,3},{3,0},{4,5},{5,6},{6,7},{7,4},{8,9},{9,10},{10,1... | collective-permute-start | bytes 3342344 | tf_op jit(solution)/shard_map/ppermute | solution.py:44
  557.1 27.7 %copy-start.22 = (f32[256,128]{1,0:T(8,128)S(1)}, f32[256,128]{1,0:T(8,128)}, u32[]{:S(2)}) copy-start(f32[256,128]{1,0:T(8,128)} %get-tuple-element.124) | copy-start | bytes 393220
  557.1 27.7 %collective-permute-start.16 = (bf16[256,2176]{1,0:T(8,128)(2,1)}, bf16[256,2176]{1,0:T(8,128)(2,1)}, u32[]{:S(2)}, u32[]{:S(2)}) collective-permute-start(bf16[256,2176]{1,0:T(8,128)(2,1)} %fusion.8), channel_id=1, source_target_pairs={{0,1},{1,2},{2,3},{3,0},{4,5},{5,6},{6,7},{7,4},{8,9},{9,10},{10,1... | collective-permute-start | bytes 3342344 | tf_op jit(solution)/shard_map/ppermute | solution.py:44
  588.0 27.0 %collective-permute-start.17 = (bf16[256,2176]{1,0:T(8,128)(2,1)}, bf16[256,2176]{1,0:T(8,128)(2,1)}, u32[]{:S(2)}, u32[]{:S(2)}) collective-permute-start(bf16[256,2176]{1,0:T(8,128)(2,1)} %fusion.7), channel_id=1, source_target_pairs={{0,1},{1,2},{2,3},{3,0},{4,5},{5,6},{6,7},{7,4},{8,9},{9,10},{10,1... | collective-permute-start | bytes 3342344 | tf_op jit(solution)/shard_map/ppermute | solution.py:44
  627.4 214.2 %reduce-scatter.8.cloned.1.call-start = ((), (), s32[]{:S(2)}) async-start(), calls=%async_computation.10 | async-start | bytes 7077888 | tf_op jit(solution)/shard_map/reduce_scatter | solution.py:318
  635.9 11.2 collective-permute-start.18
  635.9 17.8 %collective-permute-start.19 = (bf16[256,512]{1,0:T(8,128)(2,1)S(1)}, bf16[256,512]{1,0:T(8,128)(2,1)S(1)}, u32[]{:S(2)}, u32[]{:S(2)}) collective-permute-start(bf16[256,512]{1,0:T(8,128)(2,1)S(1)} %get-tuple-element.114), channel_id=1, source_target_pairs={{0,2},{1,3},{2,0},{3,1},{4,6},{5,7},{6,4},{7,5},{8,10},{9,11},{10,... | collective-permute-start | bytes 786440 | tf_op jit(solution)/shard_map/ppermute | solution.py:44
  636.0 17.8 %collective-permute-start.20 = (bf16[256,512]{1,0:T(8,128)(2,1)S(1)}, bf16[256,512]{1,0:T(8,128)(2,1)S(1)}, u32[]{:S(2)}, u32[]{:S(2)}) collective-permute-start(bf16[256,512]{1,0:T(8,128)(2,1)S(1)} %get-tuple-element.113), channel_id=1, source_target_pairs={{0,3},{1,0},{2,1},{3,2},{4,7},{5,4},{6,5},{7,6},{8,11},{9,8},{10,9... | collective-permute-start | bytes 786440 | tf_op jit(solution)/shard_map/ppermute | solution.py:44
  678.9 53.3 %copy-start.26 = (f32[1024]{0:T(1024)S(1)}, f32[1024]{0:T(1024)}, u32[]{:S(2)}) copy-start(f32[1024]{0:T(1024)} %get-tuple-element.94) | copy-start | bytes 12292
  678.9 53.3 %copy-start.27 = (f32[1024]{0:T(1024)S(1)}, f32[1024]{0:T(1024)}, u32[]{:S(2)}) copy-start(f32[1024]{0:T(1024)} %get-tuple-element.95) | copy-start | bytes 12292
  678.9 53.3 %copy-start.18 = (f32[1024,512]{1,0:T(8,128)S(1)}, f32[1024,512]{1,0:T(8,128)}, u32[]{:S(2)}) copy-start(f32[1024,512]{1,0:T(8,128)} %get-tuple-element.41) | copy-start | bytes 6291460
  678.9 16.7 %collective-permute-start.23 = (f32[2,1024]{0,1:T(8,128)}, f32[2,1024]{0,1:T(8,128)S(1)}, u32[]{:S(2)}, u32[]{:S(2)}) collective-permute-start(f32[2,1024]{0,1:T(8,128)} %bitcast.96), channel_id=1, source_target_pairs={{0,3},{1,0},{2,1},{3,2},{4,7},{5,4},{6,5},{7,6},{8,11},{9,8},{10,9... | collective-permute-start | bytes 24584 | tf_op jit(solution)/shard_map/ppermute | solution.py:44
  682.3 48.2 %collective-permute-start.22 = (f32[2,1024]{0,1:T(8,128)}, f32[2,1024]{0,1:T(8,128)S(1)}, u32[]{:S(2)}, u32[]{:S(2)}) collective-permute-start(f32[2,1024]{0,1:T(8,128)} %bitcast.97), channel_id=1, source_target_pairs={{0,2},{1,3},{2,0},{3,1},{4,6},{5,7},{6,4},{7,5},{8,10},{9,11},{10,... | collective-permute-start | bytes 24584 | tf_op jit(solution)/shard_map/ppermute | solution.py:44
  685.6 45.0 %collective-permute-start.21 = (f32[2,1024]{0,1:T(8,128)}, f32[2,1024]{0,1:T(8,128)S(1)}, u32[]{:S(2)}, u32[]{:S(2)}) collective-permute-start(f32[2,1024]{0,1:T(8,128)} %bitcast.98), channel_id=1, source_target_pairs={{0,1},{1,2},{2,3},{3,0},{4,5},{5,6},{6,7},{7,4},{8,9},{9,10},{10,1... | collective-permute-start | bytes 24584 | tf_op jit(solution)/shard_map/ppermute | solution.py:44
  747.9 263.9 %all-reduce.6.cloned.1.call-start = ((), (), s32[]{:S(2)}) async-start(), calls=%async_computation.13 | async-start | bytes 393216 | tf_op jit(solution)/shard_map/psum | solution.py:476
  747.9 31.8 %slice-start = ((s8[6291456]{0:T(1024)(128)(4,1)}), s8[4194304]{0:T(1024)(128)(4,1)S(1)}, s32[]{:S(2)}) async-start(s8[6291456]{0:T(1024)(128)(4,1)} %bitcast.116), calls=%async_computation.18 | async-start | bytes 8388608
  748.2 57.2 %copy-start.16 = (bf16[1024,1536]{1,0:T(8,128)(2,1)}, bf16[1024,1536]{1,0:T(8,128)(2,1)S(1)}, u32[]{:S(2)}) copy-start(bf16[1024,1536]{1,0:T(8,128)(2,1)S(1)} %pad_maximum_fusion) | copy-start | bytes 9437188
  748.2 31.6 %slice-start.1 = ((s8[6291456]{0:T(1024)(128)(4,1)}), s8[2097152]{0:T(1024)(128)(4,1)S(1)}, s32[]{:S(2)}) async-start(s8[6291456]{0:T(1024)(128)(4,1)} %bitcast.116), calls=%async_computation.19 | async-start | bytes 4194304
  754.6 27.0 %copy-start.7 = (bf16[256,2048]{1,0:T(8,128)(2,1)S(1)}, bf16[256,2048]{1,0:T(8,128)(2,1)}, u32[]{:S(2)}) copy-start(bf16[256,2048]{1,0:T(8,128)(2,1)} %param.15) | copy-start | bytes 3145732
  754.6 25.1 %collective-permute-start.24 = (bf16[256,2048]{1,0:T(8,128)(2,1)S(1)}, bf16[256,2048]{1,0:T(8,128)(2,1)S(1)}, u32[]{:S(2)}, u32[]{:S(2)}) collective-permute-start(bf16[256,2048]{1,0:T(8,128)(2,1)S(1)} %convolution_convert_fusion.5), channel_id=1, source_target_pairs={{0,1},{1,2},{2,3},{3,0},{4,5},{5,6},{6,7},{7,4},{8,9},{9,10},{10,1... | collective-permute-start | bytes 3145736 | tf_op jit(solution)/shard_map/ppermute | solution.py:44
  781.6 23.8 %collective-permute-start.25 = (bf16[256,2048]{1,0:T(8,128)(2,1)S(1)}, bf16[256,2048]{1,0:T(8,128)(2,1)S(1)}, u32[]{:S(2)}, u32[]{:S(2)}) collective-permute-start(bf16[256,2048]{1,0:T(8,128)(2,1)S(1)} %add_convert_fusion.4), channel_id=1, source_target_pairs={{0,1},{1,2},{2,3},{3,0},{4,5},{5,6},{6,7},{7,4},{8,9},{9,10},{10,1... | collective-permute-start | bytes 3145736 | tf_op jit(solution)/shard_map/ppermute | solution.py:44
  807.2 26.3 %collective-permute-start.26 = (bf16[256,2048]{1,0:T(8,128)(2,1)S(1)}, bf16[256,2048]{1,0:T(8,128)(2,1)}, u32[]{:S(2)}, u32[]{:S(2)}) collective-permute-start(bf16[256,2048]{1,0:T(8,128)(2,1)S(1)} %add_convert_fusion.3), channel_id=1, source_target_pairs={{0,1},{1,2},{2,3},{3,0},{4,5},{5,6},{6,7},{7,4},{8,9},{9,10},{10,1... | collective-permute-start | bytes 3145736 | tf_op jit(solution)/shard_map/ppermute | solution.py:44
  807.3 24.8 %copy-start.10 = (bf16[256,2048]{1,0:T(8,128)(2,1)S(1)}, bf16[256,2048]{1,0:T(8,128)(2,1)}, u32[]{:S(2)}) copy-start(bf16[256,2048]{1,0:T(8,128)(2,1)} %copy-done.9) | copy-start | bytes 3145732
  807.3 26.1 %copy-start.33 = (f32[1,512]{1,0:T(1,128)S(1)}, f32[1,512]{1,0:T(1,128)}, u32[]{:S(2)}) copy-start(f32[1,512]{1,0:T(1,128)} %get-tuple-element.47) | copy-start | bytes 6148
  807.3 26.2 %copy-start.32 = (f32[1,512]{1,0:T(1,128)S(1)}, f32[1,512]{1,0:T(1,128)}, u32[]{:S(2)}) copy-start(f32[1,512]{1,0:T(1,128)} %get-tuple-element.48) | copy-start | bytes 6148
  838.6 28.5 %copy-start.11 = (f32[256,2048]{1,0:T(8,128)}, f32[256,2048]{1,0:T(8,128)S(1)}, u32[]{:S(2)}) copy-start(f32[256,2048]{1,0:T(8,128)S(1)} %convert_add_fusion.1) | copy-start | bytes 6291460
  840.8 210.3 %all-reduce.4.cloned.1.call-start = ((), (), s32[]{:S(2)}) async-start(), calls=%async_computation.12 | async-start | bytes 2097152 | tf_op jit(solution)/shard_map/psum | solution.py:477
  841.5 274.0 %all-gather.18.cloned.1.call-start = ((), (), s32[]{:S(2)}) async-start(), calls=%async_computation.16 | async-start | bytes 3932160 | tf_op jit(solution)/shard_map/all_gather | solution.py:478
  842.1 392.1 %reduce-scatter.16.cloned.1.call-start = ((), (), s32[]{:S(2)}) async-start(), calls=%async_computation.17 | async-start | bytes 18874368
  887.9 466.1 %reduce-scatter.14.cloned.1.call-start = ((), (), s32[]{:S(2)}) async-start(), calls=%async_computation.15 | async-start | bytes 18874368 | tf_op jit(solution)/shard_map/reduce_scatter | solution.py:318
  912.7 561.2 %reduce-scatter.12.cloned.1.call-start = ((), (), s32[]{:S(2)}) async-start(), calls=%async_computation.14 | async-start | bytes 18874368 | tf_op jit(solution)/shard_map/reduce_scatter | solution.py:318
  939.4 24.0 %collective-permute-start.27 = (bf16[256,2048]{1,0:T(8,128)(2,1)S(1)}, bf16[256,2048]{1,0:T(8,128)(2,1)S(1)}, u32[]{:S(2)}, u32[]{:S(2)}) collective-permute-start(bf16[256,2048]{1,0:T(8,128)(2,1)S(1)} %dynamic-slice_convert_fusion), channel_id=1, source_target_pairs={{0,1},{1,2},{2,3},{3,0},{4,5},{5,6},{6,7},{7,4},{8,9},{9,10},{10,1... | collective-permute-start | bytes 3145736 | tf_op jit(solution)/shard_map/ppermute | solution.py:44
  965.2 38.2 %collective-permute-start.28 = (bf16[256,2048]{1,0:T(8,128)(2,1)S(1)}, bf16[256,2048]{1,0:T(8,128)(2,1)S(1)}, u32[]{:S(2)}, u32[]{:S(2)}) collective-permute-start(bf16[256,2048]{1,0:T(8,128)(2,1)S(1)} %add_convert_fusion.2), channel_id=1, source_target_pairs={{0,1},{1,2},{2,3},{3,0},{4,5},{5,6},{6,7},{7,4},{8,9},{9,10},{10,1... | collective-permute-start | bytes 3145736 | tf_op jit(solution)/shard_map/ppermute | solution.py:44
  1006.3 20.1 %collective-permute-start.29 = (bf16[256,2048]{1,0:T(8,128)(2,1)}, bf16[256,2048]{1,0:T(8,128)(2,1)}, u32[]{:S(2)}, u32[]{:S(2)}) collective-permute-start(bf16[256,2048]{1,0:T(8,128)(2,1)} %add_convert_fusion.1), channel_id=1, source_target_pairs={{0,1},{1,2},{2,3},{3,0},{4,5},{5,6},{6,7},{7,4},{8,9},{9,10},{10,1... | collective-permute-start | bytes 3145736 | tf_op jit(solution)/shard_map/ppermute | solution.py:44
  (19 other events, 87.6 us)
Sparse Core Ops, SparseCore 0:
  11.3 48.2 all-gather.7
  62.0 54.3 all-gather.9
  118.9 89.8 all-gather.11
  211.1 89.8 all-gather.13
  302.8 89.8 all-gather.15
  627.5 68.6 reduce-scatter.9
  748.0 59.0 reduce-scatter.7
  840.9 125.3 all-reduce.5
  968.6 82.3 all-reduce.3
  1052.6 62.8 all-gather.17
  1119.5 114.5 reduce-scatter.15
  1238.0 115.9 reduce-scatter.13
  1357.9 115.9 reduce-scatter.11

commit v2 on v1

v2 whole, which is shorter than its diff:
```python
import functools
import math

import jax
import jax.numpy as jnp
from jax import lax
from jax.experimental import pallas as pl
from jax.experimental.pallas import tpu as pltpu
from jax.sharding import PartitionSpec as P

HEADS = 16
HEAD_DIM = 128
LEN = 1024
MAX_PREFIX = LEN // 2
QBLOCK = 256
EPS = 1e-05
THETA = 10000.0
BF = jnp.bfloat16
F32 = jnp.float32
MESH = pl.DeviceIdType.MESH
LANES = 128
SHORT = pl.CostEstimate(flops=1000000, bytes_accessed=1000000, transcendentals=0)


def dot(left, right):
    return jnp.dot(left, right, preferred_element_type=F32)


def dot_nt(left, right):
    return lax.dot_general(left, right, (((1,), (1,)), ((), ())), preferred_element_type=F32)


def dot_tn(left, right):
    return lax.dot_general(left, right, (((0,), (0,)), ((), ())), preferred_element_type=F32)


def row_scale(values):
    return lax.rsqrt(jnp.mean(values * values, -1, keepdims=True) + EPS)


def norm_back(values, scale_rows, upstream):
    inner = jnp.mean(upstream * values, -1, keepdims=True)
    return scale_rows * upstream - values * (scale_rows * scale_rows * scale_rows) * inner


def shift(value, count, step):
    return lax.ppermute(value, "expert", [(i, (i + step) % count) for i in range(count)])


class Ring:
    def __init__(self, value, arrived, count, here):
        self.value, self.count, self.here = value, count, here
        self.step = 1
        self.total = self.term() + arrived.astype(F32)

    def term(self):
        rows = self.value.shape[0] // self.count
        block = (self.here - 1 - self.step) % self.count
        return lax.dynamic_slice(self.value, (block * rows, 0), (rows, self.value.shape[1]))

    def hop(self, *done):
        arrived = shift(self.total.astype(BF), self.count, 1)
        self.step += 1
        self.total = self.term() + after(arrived, *done).astype(F32)
        return self.total

    def finish(self, *done):
        while self.step < self.count - 1:
            self.hop(*done)
        return self.total


def exchange_kernel(count, value, out, slots, send_sem, recv_sem):
    here = lax.axis_index("expert")
    others = [lax.rem(here + step, count) for step in range(1, count)]
    barrier = pltpu.get_barrier_semaphore()
    for other in others:
        pl.semaphore_signal(barrier, inc=1, device_id={"expert": other}, device_id_type=MESH)
    pl.semaphore_wait(barrier, count - 1)
    copies = [
        pltpu.make_async_remote_copy(
            src_ref=value,
            dst_ref=slots.at[i],
            send_sem=send_sem.at[i],
            recv_sem=recv_sem.at[i],
            device_id={"expert": other},
            device_id_type=MESH,
        )
        for i, other in enumerate(others)
    ]
    for copy in copies:
        copy.start()
    for copy in copies:
        copy.wait()
    total = value[...]
    for i in range(count - 1):
        total = total + slots[i]
    out[...] = total


def exchange_sum(value, count, call):
    return pl.pallas_call(
        functools.partial(exchange_kernel, count),
        out_shape=jax.ShapeDtypeStruct(value.shape, F32),
        in_specs=[pl.BlockSpec(memory_space=pltpu.VMEM)],
        out_specs=pl.BlockSpec(memory_space=pltpu.VMEM),
        scratch_shapes=[
            pltpu.VMEM((count - 1,) + value.shape, F32),
            pltpu.SemaphoreType.DMA((count - 1,)),
            pltpu.SemaphoreType.DMA((count - 1,)),
        ],
        compiler_params=pltpu.CompilerParams(collective_id=call, has_side_effects=True),
        name="exchange%d" % call,
    )(value)


def after(value, *done):
    return lax.optimization_barrier((value,) + done)[0]


PIECES = 2


def gather_kernel(count, arrays, *refs):
    values, wholes = refs[:arrays], refs[arrays : 2 * arrays]
    local, sems = refs[2 * arrays : 3 * arrays], refs[3 * arrays :]
    send_sem, recv_sem, in_sem, out_sem = sems
    here = lax.axis_index("expert")
    right, left = lax.rem(here + 1, count), lax.rem(here + count - 1, count)
    other_core = flipped(lax.axis_index("group"), 1)

    def hop(array, step, piece):
        rows = values[array].shape[0]
        size = rows // PIECES
        owner = lax.rem(here - step + count, count)
        place = wholes[array].at[pl.ds(pl.multiple_of(owner * rows + piece * size, size), size)]
        return pltpu.make_async_remote_copy(
            src_ref=place if step else values[array].at[pl.ds(piece * size, size)],
            dst_ref=place,
            send_sem=send_sem.at[array, step, piece],
            recv_sem=recv_sem.at[array, step, piece],
            device_id={"expert": right},
            device_id_type=MESH,
        )

    loads = [pltpu.make_async_copy(values[i], local[i], in_sem.at[i]) for i in range(arrays)]

    @pl.when(pl.program_id(0) == 0)
    def _():
        barrier = pltpu.get_barrier_semaphore()
        for other in (left, right):
            pl.semaphore_signal(barrier, inc=1, device_id={"expert": other}, device_id_type=MESH)
        pl.semaphore_signal(barrier, inc=1, device_id={"group": other_core}, device_id_type=MESH)
        pl.semaphore_wait(barrier, 3)
        for i in range(arrays):
            for piece in range(PIECES):
                hop(i, 0, piece).start()
            loads[i].start()

    def rest():
        stores = []
        for i in range(arrays):
            rows = values[i].shape[0]
            loads[i].wait()
            stores.append(
                pltpu.make_async_copy(
                    local[i], wholes[i].at[pl.ds(pl.multiple_of(here * rows, rows), rows)], out_sem.at[i]
                )
            )
            stores[i].start()
        for i in range(arrays):
            for step in range(1, count - 1):
                for piece in range(PIECES):
                    hop(i, step - 1, piece).wait_recv()
                    hop(i, step, piece).start()
        for i in range(arrays):
            stores[i].wait()
            for piece in range(PIECES):
                hop(i, count - 2, piece).wait_recv()
                for step in range(count - 1):
                    hop(i, step, piece).wait_send()

    return rest


def gather_only(count, arrays, *refs):
    gather_kernel(count, arrays, *refs)()


def gather_scratch(values, count):
    arrays = len(values)
    hops = pltpu.SemaphoreType.DMA((arrays, count - 1, PIECES))
    return [pltpu.VMEM(v.shape, v.dtype) for v in values] + [
        hops, hops, pltpu.SemaphoreType.DMA((arrays,)), pltpu.SemaphoreType.DMA((arrays,))
    ]


def gather_rows(values, count, call):
    arrays = len(values)
    return pl.pallas_call(
        functools.partial(gather_only, count, arrays),
        grid=(1,),
        out_shape=[jax.ShapeDtypeStruct((count * v.shape[0],) + v.shape[1:], v.dtype) for v in values],
        in_specs=[pl.BlockSpec(memory_space=pl.ANY)] * arrays,
        out_specs=[pl.BlockSpec(memory_space=pl.ANY)] * arrays,
        scratch_shapes=gather_scratch(values, count),
        compiler_params=pltpu.CompilerParams(collective_id=call, has_side_effects=True),
        cost_estimate=SHORT,
        name="gather%d" % call,
    )(*values)


PREP_ROWS = 32


def prep_kernel(count, halves, value, up, lower, whole, out1, out2, *scratch):
    rest = gather_kernel(count, 1, value, whole, *scratch)
    ff = up.shape[2] // 2
    for pair, out in enumerate((out1, out2)):
        for j in range(PAIR):
            row = up[:, pair * PAIR + j, :].astype(BF)
            out[:, j * ff : (j + 1) * ff] = row[:, :ff]
            out[:, (PAIR + j) * ff : (PAIR + j + 1) * ff] = row[:, ff:]

        for j in range(PAIR):

            @pl.when(pl.program_id(0) // halves == j)
            def _():
                out[:, 2 * PAIR * ff :] = lower[:, pair * PAIR + j, :].astype(BF)

    pl.when(pl.program_id(0) == pl.num_programs(0) - 1)(rest)


def gather_and_prep(value, expert_in, expert_down, count, call):
    master, local, both = expert_in.shape
    halves = expert_down.shape[0] // PREP_ROWS
    width = expert_down.shape[2]
    columns = PAIR * both + width
    anywhere = pl.BlockSpec(memory_space=pl.ANY)
    return pl.pallas_call(
        functools.partial(prep_kernel, count, halves),
        grid=(master // PREP_ROWS,),
        in_specs=[
            anywhere,
            pl.BlockSpec((PREP_ROWS, local, both), lambda i: (i, 0, 0)),
            pl.BlockSpec((PREP_ROWS, local, width), lambda i: (lax.rem(i, halves), 0, 0)),
        ],
        out_specs=[anywhere] + [pl.BlockSpec((PREP_ROWS, columns), lambda i: (i, 0))] * 2,
        out_shape=[jax.ShapeDtypeStruct((count * value.shape[0],) + value.shape[1:], value.dtype)]
        + [jax.ShapeDtypeStruct((master, columns), BF)] * 2,
        scratch_shapes=gather_scratch((value,), count),
        compiler_params=pltpu.CompilerParams(collective_id=call, has_side_effects=True),
        cost_estimate=SHORT,
        name="gather%d" % call,
    )(value, expert_in, expert_down)


SLOTS = 3


def grads_kernel(count, hg, b, cot, dg, du, *refs):
    if count:
        partial, grad, *refs = refs
        weights, (out, first_in, heads_out), refs = refs[:count], refs[count : count + 3], refs[count + 3 :]
    else:
        out, *refs = refs
    hg_held, b_held, cot_held, dg_held, du_held, sent, landed, sem, send_sem, recv_sem = refs[:10]
    step = pl.program_id(0)
    group = lax.axis_index("group")
    core = lax.rem(group, 2)
    other = flipped(group, 1)
    size, columns = out.shape[0], cot_held.shape[1]
    chips = landed.shape[0]
    loads = [
        pltpu.make_async_copy(source, held, sem.at[i])
        for i, (source, held) in enumerate(
            ((hg, hg_held), (cot, cot_held), (b, b_held), (dg, dg_held), (du, du_held))
        )
    ]

    def copy(chip):
        return pltpu.make_async_remote_copy(
            src_ref=sent.at[lax.rem(chip, SLOTS)], dst_ref=landed.at[chip], send_sem=send_sem.at[chip], recv_sem=recv_sem.at[chip],
            device_id={"group": other}, device_id_type=MESH,
        )

    def terms(place):
        left_down = jnp.concatenate([hg_held[place, j] for j in range(PAIR)], -1)
        left = b_held[:, pl.ds(pl.multiple_of(place * size, size), size)]
        return (left_down, cot_held), (left, dg_held), (left, du_held)

    lanes = [slice(i * columns, (i + 1) * columns) for i in range(3)]
    if count:
        here = lax.axis_index("expert")
        right, left = lax.rem(here + 1, count), lax.rem(here + count - 1, count)
        rows = partial.shape[0] // count
        first = pltpu.make_async_remote_copy(
            src_ref=partial.at[pl.ds(pl.multiple_of(left * rows, rows), rows)], dst_ref=first_in,
            send_sem=refs[10].at[0], recv_sem=refs[10].at[1], device_id={"expert": right}, device_id_type=MESH,
        )
        heads_sent, heads_send, heads_recv, own_sem = refs[11:]
        own_rows, cols = grad.shape[0], heads_out.shape[1]
        others = [lax.rem(here + number, count) for number in range(1, count)]
        own_place = heads_out.at[pl.ds(pl.multiple_of(here * own_rows, own_rows), own_rows)]

        def heads(other):
            at = pl.ds(pl.multiple_of(other * cols, cols), cols)
            total = None
            for i, weight in enumerate(weights):
                term = dot_nt(grad[:, i * cols : (i + 1) * cols], weight[at, :])
                total = term if total is None else total + term
            return total.astype(BF)

        heads_copies = [
            pltpu.make_async_remote_copy(
                src_ref=heads_sent.at[i], dst_ref=own_place, send_sem=heads_send.at[i], recv_sem=heads_recv.at[i],
                device_id={"expert": device}, device_id_type=MESH,
            )
            for i, device in enumerate(others)
        ]

    @pl.when(step == 0)
    def _():
        barrier = pltpu.get_barrier_semaphore()
        pl.semaphore_signal(barrier, inc=1, device_id={"group": other}, device_id_type=MESH)
        if count:
            for device in others:
                pl.semaphore_signal(barrier, inc=1, device_id={"expert": device}, device_id_type=MESH)
        for load in loads:
            load.start()
        pl.semaphore_wait(barrier, count if count else 1)
        if count:
            for i, device in enumerate(others):
                heads_sent[i] = heads(device)
                heads_copies[i].start()
            first.start()
            heads_sent[count - 1] = heads(here)
            own_copy = pltpu.make_async_copy(heads_sent.at[count - 1], own_place, own_sem)
            own_copy.start()
        loads[0].wait()
        loads[2].wait()
        for i, (left_value, right_ref) in enumerate(terms(1 - core)):
            loads[(1, 3, 4)[i]].wait()
            sent[0, :, lanes[i]] = dot_tn(left_value, right_ref[...]).astype(BF)
        copy(0).start()

    @pl.when((step > 0) & (step < chips))
    def _():
        @pl.when(step >= SLOTS)
        def _():
            copy(step - SLOTS).wait_send()

        slot = lax.rem(step, SLOTS)
        for i, (left_value, right_ref) in enumerate(terms(2 * step + 1 - core)):
            sent[slot, :, lanes[i]] = dot_tn(left_value, right_ref[...]).astype(BF)
        copy(step).start()

    @pl.when(step >= chips)
    def _():
        chip = step - chips
        copy(chip).wait_recv()
        for i, (left_value, right_ref) in enumerate(terms(2 * chip + core)):
            total = dot_tn(left_value, right_ref[...]) + landed[chip, :, lanes[i]].astype(F32)
            out[:, lanes[i]] = total.astype(BF)

    @pl.when(step == 2 * chips - 1)
    def _():
        for chip in range(max(chips - SLOTS, 0), chips):
            copy(chip).wait_send()
        if count:
            pltpu.make_async_copy(heads_sent.at[count - 1], own_place, own_sem).wait()
            for copied in heads_copies:
                copied.wait()
            first.wait()


def grad_terms(hg, b, cot, dg, du, call, partial=None, grad=None, dense=None, count=0):
    blocks, _, rows, block = hg.shape
    size = b.shape[1] // blocks
    columns = cot.shape[1]
    chips = blocks // 2
    anywhere = pl.BlockSpec(memory_space=pl.ANY)
    dma = pltpu.SemaphoreType.DMA
    operands, in_specs = [hg, b, cot, dg, du], [anywhere] * 5
    out_specs = [pl.BlockSpec((size, 3 * columns), lambda p: (jnp.maximum(p - chips, 0), 0))]
    out_shape = [jax.ShapeDtypeStruct((chips * size, 3 * columns), BF)]
    scratch = (
        [pltpu.VMEM(hg.shape, BF)]
        + [pltpu.VMEM((rows, columns), BF)] * 4
        + [pltpu.VMEM((min(chips, SLOTS), size, 3 * columns), BF), pltpu.VMEM((chips, size, 3 * columns), BF)]
        + [dma((5,)), dma((chips,)), dma((chips,))]
    )
    if count:
        own_rows, cols = rows // count, columns // count
        once = pl.Buffered(1)
        operands += [partial, grad] + [dense] * count
        in_specs += [anywhere, pl.BlockSpec(grad.shape, lambda p: (0, 0), pipeline_mode=once)]
        in_specs += [pl.BlockSpec((columns, cols), lambda p, j=j: (0, 3 + j), pipeline_mode=once) for j in range(count)]
        out_specs += [anywhere, anywhere]
        out_shape += [jax.ShapeDtypeStruct((own_rows, columns), BF), jax.ShapeDtypeStruct((rows, cols), BF)]
        scratch += [dma((2,)), pltpu.VMEM((count, own_rows, cols), BF), dma((count - 1,)), dma((count - 1,)), dma]
    return pl.pallas_call(
        functools.partial(grads_kernel, count),
        grid=(blocks,),
        in_specs=in_specs,
        out_specs=out_specs,
        out_shape=out_shape,
        scratch_shapes=scratch,
        compiler_params=pltpu.CompilerParams(
            collective_id=call, has_side_effects=True, vmem_limit_bytes=67043328
        ),
        cost_estimate=SHORT,
        name="grads%d" % call,
    )(*operands)


def heads_kernel(count, value, out, send_sem, recv_sem, own_sem):
    here = lax.axis_index("expert")
    rows, cols = out.shape[0], value.shape[1]
    others = [lax.rem(here + step, count) for step in range(1, count)]
    barrier = pltpu.get_barrier_semaphore()
    for other in others:
        pl.semaphore_signal(barrier, inc=1, device_id={"expert": other}, device_id_type=MESH)
    pl.semaphore_wait(barrier, count - 1)
    place = out.at[:, pl.ds(pl.multiple_of(here * cols, cols), cols)]

    def block(other):
        return value.at[pl.ds(pl.multiple_of(other * rows, rows), rows)]

    copies = [
        pltpu.make_async_remote_copy(
            src_ref=block(other), dst_ref=place, send_sem=send_sem.at[i], recv_sem=recv_sem.at[i],
            device_id={"expert": other}, device_id_type=MESH,
        )
        for i, other in enumerate(others)
    ]
    for copy in copies:
        copy.start()
    own = pltpu.make_async_copy(block(here), place, own_sem)
    own.start()
    own.wait()
    for copy in copies:
        copy.wait()


def heads_to_rows(value, count, call):
    vmem = pl.BlockSpec(memory_space=pltpu.VMEM)
    dma = pltpu.SemaphoreType.DMA
    return pl.pallas_call(
        functools.partial(heads_kernel, count),
        out_shape=jax.ShapeDtypeStruct((value.shape[0] // count, value.shape[1] * count), value.dtype),
        in_specs=[vmem],
        out_specs=vmem,
        scratch_shapes=[dma((count - 1,)), dma((count - 1,)), dma],
        compiler_params=pltpu.CompilerParams(collective_id=call, has_side_effects=True),
        cost_estimate=SHORT,
        name="heads%d" % call,
    )(value)


def flipped(index, mask):
    bit = 1
    while bit <= mask:
        if mask & bit:
            index = index + bit * (1 - 2 * lax.rem(lax.div(index, bit), 2))
        bit *= 2
    return index


def subsets(bits):
    sums = [0]
    for bit in bits:
        sums = sums + [value + bit for value in sums]
    return sums


def tail_kernel(
    count, groups, grads, weight, hidden, output_sum, normed, sums, rows_out, *refs
):
    final_outs, sums_out, refs = refs[:4], refs[4], refs[5:]
    (
        query_out, key_out, value_out, output_out, final_sem,
        sent, landed, core_out, core_in, held, step_in, done, part_sent, part_in, small, small_in, small_sum,
        all_in, own_sem, token_send, token_recv, core_send, core_recv, step_send, step_recv, whole_send,
        whole_recv, part_send, part_recv, sum_send, sum_recv, small_send, small_recv, all_send, all_recv,
    ) = refs
    here, group = lax.axis_index("expert"), lax.axis_index("group")
    right, left = lax.rem(here + 1, count), lax.rem(here + count - 1, count)
    others = [lax.rem(here + step, count) for step in range(1, count)]
    bits = [1 << i for i in range(1, groups.bit_length() - 1)]
    orders = (bits, bits[::-1])
    barrier = pltpu.get_barrier_semaphore()
    for other in others:
        pl.semaphore_signal(barrier, inc=1, device_id={"expert": other}, device_id_type=MESH)
    peers = [lax.rem(group + step, groups) for step in range(1, groups)]
    for peer in peers:
        pl.semaphore_signal(barrier, inc=1, device_id={"group": peer}, device_id_type=MESH)
    pl.semaphore_wait(barrier, count + groups - 2)

    rows, width = rows_out.shape
    half = width // 2
    master, columns = held.shape[1:]
    cols = width // count
    slab = master // count

    def to(axis, other, source, target, send, receive):
        return pltpu.make_async_remote_copy(
            src_ref=source, dst_ref=target, send_sem=send, recv_sem=receive,
            device_id={axis: other}, device_id_type=MESH,
        )

    rest = subsets(bits)

    core = [
        to("group", flipped(group, 1), core_out.at[i], core_in.at[i], core_send.at[i], core_recv.at[i])
        for i in range(len(rest))
    ]
    backward = list(enumerate(rest))[::-1]

    def own_term(block):
        lanes = pl.ds(pl.multiple_of(block * master, master), master)
        return dot_tn(hidden[:, lanes], grads[...])

    def token_block(step, piece):
        block = lax.rem(here - 1 - step + count, count)
        return dot_nt(grads[pl.ds(pl.multiple_of(block * rows, rows), rows), :],
                      weight[piece * half : (piece + 1) * half, :])

    def token_hop(step, piece):
        return to("expert", right, sent.at[step % 2, piece], landed.at[step, piece],
                  token_send.at[step, piece], token_recv.at[step, piece])

    for piece in range(2):
        sent[0, piece] = token_block(0, piece).astype(BF)
        token_hop(0, piece).start()

    def token_step(step):
        terms = [token_block(step, piece) for piece in range(2)]
        for piece in range(2):
            token_hop(step - 1, piece).wait_recv()
            total = terms[piece] + landed[step - 1, piece].astype(F32)
            if step < count - 1:
                if step >= 2:
                    token_hop(step - 2, piece).wait_send()
                sent[step % 2, piece] = total.astype(BF)
                token_hop(step, piece).start()
            else:
                rows_out[:, piece * half : (piece + 1) * half] = total

    def moves(order, level):
        bit = order[level]
        sends = [r for r in rest if r & bit and not r & sum(order[:level])]
        return bit, sends, sum(len(rest) >> (i + 1) for i in range(level))

    outs = (query_out, key_out, value_out)
    pieces = len(outs)

    def whole_hop(step, piece):
        owner = lax.rem(here - step + count, count)
        target = outs[piece].at[:, pl.ds(pl.multiple_of(owner * cols, cols), cols)]
        source = done.at[:, pl.ds(piece * cols, cols)] if step == 0 else target
        return to("expert", right, source, target, whole_send.at[step, piece], whole_recv.at[step, piece])

    own = [
        pltpu.make_async_copy(
            done.at[:, pl.ds(piece * cols, cols)],
            outs[piece].at[:, pl.ds(pl.multiple_of(here * cols, cols), cols)],
            own_sem.at[piece],
        )
        for piece in range(pieces)
    ]

    def whole_start():
        for piece in range(pieces):
            whole_hop(0, piece).start()
        for copy in own:
            copy.start()

    streams = [(slice(0, columns // 2), orders[0]), (slice(columns // 2, columns), orders[1])]

    def step_copies(stream, level):
        lanes, order = streams[stream]
        bit, sends, first = moves(order, level)
        return [
            to("group", flipped(group, bit), held.at[rest.index(r), :, lanes],
               step_in.at[stream, first + i],
               step_send.at[stream, first + i], step_recv.at[stream, first + i])
            for i, r in enumerate(sends)
        ]

    copies = [[step_copies(stream, level) for level in range(len(bits))] for stream in range(2)]
    for i, r in backward:
        core_out[i] = own_term(flipped(group, 1 + r)).astype(BF)
        core[i].start()
    for i, r in backward:
        term = own_term(flipped(group, r))
        core[i].wait_recv()
        held[i] = (term + core_in[i].astype(F32)).astype(BF)
        for stream in range(2):
            sends = moves(streams[stream][1], 0)[1]
            if r in sends:
                copies[stream][0][sends.index(r)].start()

    def reduce_step(level):
        for stream in range(2):
            lanes, order = streams[stream]
            bit, sends, first = moves(order, level)
            for i, r in enumerate(sends):
                copies[stream][level][i].wait()
                kept = rest.index(r - bit)
                total = (held[kept, :, lanes].astype(F32) + step_in[stream, first + i].astype(F32)).astype(BF)
                if level < len(bits) - 1:
                    held[kept, :, lanes] = total
                else:
                    done[:, lanes] = total
            if level < len(bits) - 1:
                for copy in copies[stream][level + 1]:
                    copy.start()

    def slab_of(other):
        return pl.ds(pl.multiple_of(other * slab, slab), slab)

    def slab_hop(step):
        return to("expert", right, part_sent.at[step], part_in.at[step], part_send.at[step], part_recv.at[step])

    def slab_step(step):
        total = output_sum[slab_of(lax.rem(here - 1 - step + count, count)), :].astype(F32)
        if step:
            slab_hop(step - 1).wait_recv()
            total = total + part_in[step - 1].astype(F32)
        if step < count - 1:
            part_sent[step] = total.astype(BF)
            slab_hop(step).start()
        else:
            output_out[slab_of(here), :] = total.astype(BF)

    def sum_hop(step):
        place = output_out.at[slab_of(lax.rem(here - step + count, count))]
        return to("expert", right, place, place, sum_send.at[step], sum_recv.at[step])

    slab_step(0)
    levels = iter(range(len(bits)))
    for step in range(1, count):
        token_step(step)
        slab_step(step)
        level = next(levels, None)
        if level is not None:
            reduce_step(level)
    for level in levels:
        reduce_step(level)
    whole_start()
    sum_hop(0).start()
    small[...] = sums[...]
    small[0:1, :] = jnp.sum(rows_out[...] * normed[...], 0, keepdims=True)
    small_copies = [
        to("group", peer, small.at[:, pl.ds(pl.multiple_of(peer * master, master), master)], small_in.at[i],
           small_send.at[i], small_recv.at[i])
        for i, peer in enumerate(peers)
    ]
    for copy in small_copies:
        copy.start()
    total = small[:, pl.ds(pl.multiple_of(group * master, master), master)]
    for i, copy in enumerate(small_copies):
        copy.wait()
        total = total + small_in[i]
    small_sum[...] = total
    all_copies = [
        to("expert", other, small_sum, all_in.at[i], all_send.at[i], all_recv.at[i]) for i, other in enumerate(others)
    ]
    for copy in all_copies:
        copy.start()
    for step in range(1, count - 1):
        for piece in range(pieces):
            whole_hop(step - 1, piece).wait_recv()
            whole_hop(step, piece).start()
        sum_hop(step - 1).wait_recv()
        sum_hop(step).start()
    for i, copy in enumerate(all_copies):
        copy.wait()
        total = total + all_in[i]
    sums_out[...] = total
    for piece in range(pieces):
        own[piece].wait()
        whole_hop(count - 2, piece).wait_recv()
    sum_hop(count - 2).wait_recv()
    finals = [
        pltpu.make_async_copy(source, target, final_sem.at[i])
        for i, (source, target) in enumerate(zip((query_out, key_out, value_out, output_out), final_outs))
    ]
    for copy in finals:
        copy.start()
    for copy in core:
        copy.wait_send()
    for step in range(count - 1):
        slab_hop(step).wait_send()
        sum_hop(step).wait_send()
        if step >= count - 3:
            for piece in range(2):
                token_hop(step, piece).wait_send()
        for piece in range(pieces):
            whole_hop(step, piece).wait_send()
    for copy in finals:
        copy.wait()


def tail(grads, dense, hidden, output_sum, normed, sums, count, groups, call):
    rows, width = hidden.shape[0] // count, hidden.shape[1]
    own_columns = grads.shape[1]
    master = width // groups
    rest = groups // 2
    slab = master // count
    dma = pltpu.SemaphoreType.DMA
    vmem = pl.BlockSpec(memory_space=pltpu.VMEM)
    return pl.pallas_call(
        functools.partial(tail_kernel, count, groups),
        out_shape=[jax.ShapeDtypeStruct((rows, width), F32)] + [jax.ShapeDtypeStruct((master, width), BF)] * 4
        + [jax.ShapeDtypeStruct((sums.shape[0], master), F32)],
        grid=(1,),
        in_specs=[
            pl.BlockSpec(grads.shape, lambda i: (0, 0)),
            pl.BlockSpec((width, own_columns), lambda i: (0, 0)),
            pl.BlockSpec(hidden.shape, lambda i: (0, 0)),
            pl.BlockSpec(output_sum.shape, lambda i: (0, 0)),
            pl.BlockSpec(normed.shape, lambda i: (0, 0)),
            pl.BlockSpec(sums.shape, lambda i: (0, 0)),
        ],
        out_specs=[vmem] + [pl.BlockSpec(memory_space=pl.ANY)] * 4 + [vmem],
        scratch_shapes=[pltpu.VMEM((master, width), BF)] * 4
        + [
            dma((4,)),
            pltpu.VMEM((2, 2, rows, width // 2), BF),
            pltpu.VMEM((count - 1, 2, rows, width // 2), BF),
            pltpu.VMEM((rest, master, own_columns), BF),
            pltpu.VMEM((rest, master, own_columns), BF),
            pltpu.VMEM((rest, master, own_columns), BF),
            pltpu.VMEM((2, rest - 1, master, own_columns // 2), BF),
            pltpu.VMEM((master, own_columns), BF),
            pltpu.VMEM((count - 1, slab, width), BF),
            pltpu.VMEM((count - 1, slab, width), BF),
            pltpu.VMEM(sums.shape, F32),
            pltpu.VMEM((groups - 1, sums.shape[0], master), F32),
            pltpu.VMEM((sums.shape[0], master), F32),
            pltpu.VMEM((count - 1, sums.shape[0], master), F32),
            dma((3,)),
            dma((count - 1, 2)),
            dma((count - 1, 2)),
            dma((rest,)),
            dma((rest,)),
            dma((2, rest - 1)),
            dma((2, rest - 1)),
            dma((count - 1, 3)),
            dma((count - 1, 3)),
        ]
        + [dma((count - 1,))] * 4
        + [dma((groups - 1,))] * 2
        + [dma((count - 1,))] * 2,
        compiler_params=pltpu.CompilerParams(
            collective_id=call, has_side_effects=True, vmem_limit_bytes=67043328
        ),
        cost_estimate=SHORT,
        name="tail",
    )(grads, dense, hidden, output_sum, normed, sums)


def finish_kernel(*refs):
    in1, down1a, down1b, in2, down2a, down2b = refs[:6]
    dense, (out_in, out_down), dense_out = refs[6:10], refs[10:12], refs[12:]
    ff = out_in.shape[2] // 2
    for pair, value in enumerate((in1, in2)):
        for part in range(2):
            for j in range(PAIR):
                at = (PAIR * (1 + part) + j) * ff
                out_in[:, pair * PAIR + j, part * ff : (part + 1) * ff] = value[:, at : at + ff].astype(F32)
    for i, value in enumerate((down1a, down1b, down2a, down2b)):
        out_down[:, i, :] = value[...].astype(F32)
    for value, out in zip(dense, dense_out):
        out[...] = value[...].astype(F32)


def finish_grads(sum1, sum2, dense):
    master, columns = sum1.shape
    width = columns // 3
    steps = master // PREP_ROWS
    rows = PREP_ROWS // PAIR
    local = 2 * PAIR
    specs = [pl.BlockSpec((PREP_ROWS, columns), lambda i: (i, 0))]
    specs += [pl.BlockSpec((rows, width), lambda i, j=j: (j * steps + i, 0)) for j in range(PAIR)]
    whole = [pl.BlockSpec((PREP_ROWS, width), lambda i: (i, 0))] * len(dense)
    return pl.pallas_call(
        finish_kernel,
        grid=(steps,),
        in_specs=specs * 2 + whole,
        out_specs=[
            pl.BlockSpec((PREP_ROWS, local, width), lambda i: (i, 0, 0)),
            pl.BlockSpec((rows, local, width), lambda i: (i, 0, 0)),
        ]
        + whole,
        out_shape=[
            jax.ShapeDtypeStruct((master, local, width), F32),
            jax.ShapeDtypeStruct((master // PAIR, local, width), F32),
        ]
        + [jax.ShapeDtypeStruct((master, width), F32)] * len(dense),
        cost_estimate=SHORT,
        name="finish",
    )(sum1, sum1, sum1, sum2, sum2, sum2, *dense)


def key_limit(block):
    return max((block + 1) * QBLOCK, MAX_PREFIX)


def visible(block, limit, prefix):
    row = block * QBLOCK + lax.broadcasted_iota(jnp.int32, (QBLOCK, limit), 0)
    col = lax.broadcasted_iota(jnp.int32, (QBLOCK, limit), 1)
    return (col <= row) | (col < prefix)


def attend_kernel(prefix_ref, ql, kl, vb, sq, sk, gq, gk, cos, sin, ob, qb, kb, lse):
    prefix = prefix_ref[0]
    c, s = cos[...], sin[...]
    qn = ql[...] * sq[...] * gq[...]
    kn = kl[...] * sk[...] * gk[...]
    half = HEAD_DIM // 2
    qb[...] = ((qn * c + pltpu.roll(qn, half, 1) * s) * HEAD_DIM ** (-0.5)).astype(BF)
    kb[...] = (kn * c + pltpu.roll(kn, half, 1) * s).astype(BF)
    for block in range(LEN // QBLOCK):
        rows = slice(block * QBLOCK, (block + 1) * QBLOCK)
        limit = key_limit(block)
        scores = dot_nt(qb[rows, :], kb[:limit, :])
        scores = jnp.where(visible(block, limit, prefix), scores, -1e30)
        peak = jnp.max(scores, -1, keepdims=True)
        expo = jnp.exp(scores - peak)
        total = jnp.sum(expo, -1, keepdims=True)
        ob[rows, :] = (dot(expo.astype(BF), vb[:limit, :]) / total).astype(BF)
        lse[0, rows, :] = peak + jnp.log(total)


def attend(prefix, ql, kl, vb, sq, sk, gq, gk, cos, sin):
    heads = ql.shape[1] // HEAD_DIM
    col = pl.BlockSpec((LEN, HEAD_DIM), lambda h, p: (0, h))
    one = pl.BlockSpec((LEN, 1), lambda h, p: (0, 0))
    gain = pl.BlockSpec((1, HEAD_DIM), lambda h, p: (0, h))
    table = pl.BlockSpec((LEN, HEAD_DIM), lambda h, p: (0, 0))
    return pl.pallas_call(
        attend_kernel,
        out_shape=[jax.ShapeDtypeStruct(ql.shape, BF)] * 3
        + [jax.ShapeDtypeStruct((heads, LEN, 1), F32)],
        grid_spec=pltpu.PrefetchScalarGridSpec(
            num_scalar_prefetch=1,
            grid=(heads,),
            in_specs=[col, col, col, one, one, gain, gain, table, table],
            out_specs=[col, col, col, pl.BlockSpec((1, LEN, 1), lambda h, p: (h, 0, 0))],
        ),
        cost_estimate=SHORT,
        name="attend",
    )(prefix, ql, kl, vb, sq, sk, gq, gk, cos, sin)


def attend_back_kernel(
    prefix_ref, qb, kb, vb, dob, lse, ql, kl, sq, sk, gq, gk, cos, sin,
    wq, wk, dv, inner, gain_q, gain_k, dq_sum, dk_sum, dv_sum,
):
    prefix = prefix_ref[0]
    dk_sum[...] = jnp.zeros_like(dk_sum)
    dv_sum[...] = jnp.zeros_like(dv_sum)
    for block in range(LEN // QBLOCK):
        rows = slice(block * QBLOCK, (block + 1) * QBLOCK)
        limit = key_limit(block)
        scores = dot_nt(qb[rows, :], kb[:limit, :])
        weights = jnp.where(visible(block, limit, prefix), jnp.exp(scores - lse[0, rows, :]), 0.0)
        grad = dob[rows, :]
        dweights = dot_nt(grad, vb[:limit, :])
        dscores = (weights * (dweights - jnp.sum(dweights * weights, -1, keepdims=True))).astype(BF)
        dq_sum[rows, :] = dot(dscores, kb[:limit, :])
        dk_sum[:limit, :] += dot_tn(dscores, qb[rows, :])
        dv_sum[:limit, :] += dot_tn(weights.astype(BF), grad)
    dv[...] = dv_sum[...].astype(BF)
    c, s = cos[...], sin[...]
    half = HEAD_DIM // 2
    dq = dq_sum[...] * HEAD_DIM ** (-0.5)
    dqn = dq * c - pltpu.roll(dq, half, 1) * s
    dk = dk_sum[...]
    dkn = dk * c - pltpu.roll(dk, half, 1) * s
    gain_q[...] = jnp.sum(dqn * (ql[...] * sq[...]), 0, keepdims=True)
    gain_k[...] = jnp.sum(dkn * (kl[...] * sk[...]), 0, keepdims=True)
    dqn = dqn * gq[...]
    dkn = dkn * gk[...]
    wq[...] = dqn
    wk[...] = dkn
    part = jnp.concatenate(
        [jnp.sum(dqn * ql[...], -1, keepdims=True), jnp.sum(dkn * kl[...], -1, keepdims=True)], 1
    )

    @pl.when(pl.program_id(0) == 0)
    def _():
        inner[...] = part

    @pl.when(pl.program_id(0) > 0)
    def _():
        inner[...] += part


def attend_back(prefix, qb, kb, vb, dob, lse, ql, kl, sq, sk, gq, gk, cos, sin):
    heads = ql.shape[1] // HEAD_DIM
    col = pl.BlockSpec((LEN, HEAD_DIM), lambda h, p: (0, h))
    one = pl.BlockSpec((LEN, 1), lambda h, p: (0, 0))
    gain = pl.BlockSpec((1, HEAD_DIM), lambda h, p: (0, h))
    table = pl.BlockSpec((LEN, HEAD_DIM), lambda h, p: (0, 0))
    return pl.pallas_call(
        attend_back_kernel,
        out_shape=[
            jax.ShapeDtypeStruct(ql.shape, F32),
            jax.ShapeDtypeStruct(ql.shape, F32),
            jax.ShapeDtypeStruct(ql.shape, BF),
            jax.ShapeDtypeStruct((LEN, 2), F32),
            jax.ShapeDtypeStruct((1, ql.shape[1]), F32),
            jax.ShapeDtypeStruct((1, ql.shape[1]), F32),
        ],
        grid_spec=pltpu.PrefetchScalarGridSpec(
            num_scalar_prefetch=1,
            grid=(heads,),
            in_specs=[col, col, col, col, pl.BlockSpec((1, LEN, 1), lambda h, p: (h, 0, 0)),
                      col, col, one, one, gain, gain, table, table],
            out_specs=[col, col, col, pl.BlockSpec((LEN, 2), lambda h, p: (0, 0)), gain, gain],
            scratch_shapes=[pltpu.VMEM((LEN, HEAD_DIM), F32)] * 3,
        ),
        cost_estimate=SHORT,
        name="attend_back",
    )(prefix, qb, kb, vb, dob, lse, ql, kl, sq, sk, gq, gk, cos, sin)


FTILE = 256
PAIR = 2


def expert_kernel(first, b, c, wg, wu, wd, gates, hg, dg, du, dgate):
    lanes = lax.broadcasted_iota(jnp.int32, gates.shape, 1) == first[0] + pl.program_id(0)
    g = dot(b[...], wg[...])
    u = dot(b[...], wu[...])
    back = dot_nt(c[...], wd[...].reshape(FTILE, wd.shape[-1]))
    sigma = jax.nn.sigmoid(g)
    silu = g * sigma
    h = silu * u
    weight = jnp.sum(jnp.where(lanes, gates[...], 0.0), -1, keepdims=True)
    hidden = (weight * h).astype(BF)
    block = hg.shape[3]
    for i in range(hg.shape[0]):
        hg[i, 0] = hidden[:, i * block : (i + 1) * block]
    part = jnp.where(lanes, jnp.sum(h * back, -1, keepdims=True), 0.0)
    dh = weight * back
    dg[...] = (dh * u * (sigma * (1.0 + g * (1.0 - sigma)))).astype(BF)
    du[...] = (dh * silu).astype(BF)
    start = (pl.program_id(0) == 0) & (pl.program_id(1) == 0)

    @pl.when(start)
    def _():
        dgate[...] = part

    @pl.when(jnp.logical_not(start))
    def _():
        dgate[...] += part


def experts(first, b, c, weights, gates, ff):
    rows, width = b.shape
    tiles = ff // FTILE
    block = weights.shape[2]
    whole = pl.BlockSpec((rows, width), lambda j, f, p: (0, 0), pipeline_mode=pl.Buffered(1))
    one = pl.BlockSpec((rows, LANES), lambda j, f, p: (0, 0))
    out = pl.BlockSpec((rows, FTILE), lambda j, f, p: (0, j * tiles + f))
    flat = weights.reshape(width, weights.shape[3])
    return pl.pallas_call(
        expert_kernel,
        grid_spec=pltpu.PrefetchScalarGridSpec(
            num_scalar_prefetch=1,
            grid=(PAIR, tiles),
            in_specs=[
                whole,
                whole,
                pl.BlockSpec((width, FTILE), lambda j, f, p: (0, j * tiles + f)),
                pl.BlockSpec((width, FTILE), lambda j, f, p: (0, (PAIR + j) * tiles + f)),
                pl.BlockSpec((FTILE // block, 1, block, width), lambda j, f, p: (f, j, 0, 2)),
                one,
            ],
            out_specs=[
                pl.BlockSpec((FTILE // block, 1, rows, block), lambda j, f, p: (f, j, 0, 0)),
                out,
                out,
                one,
            ],
        ),
        out_shape=[jax.ShapeDtypeStruct((ff // block, PAIR, rows, block), BF)]
        + [jax.ShapeDtypeStruct((rows, PAIR * ff), BF)] * 2
        + [jax.ShapeDtypeStruct((rows, LANES), F32)],
        cost_estimate=SHORT,
        name="experts",
    )(first, b, c, flat, flat, weights, gates)


NTILE = 256
GROUPS = 8
STEP_BACK, STEP_DOWN, LINK_US, HOP_US = 5.4, 2.8, 2.85, 3.5


def ring_steps(count, tiles, last):
    per = tiles // GROUPS
    ends, now = [], 0.0
    for step in range(last + 1):
        now += STEP_BACK if step < tiles else STEP_DOWN
        ends.append(now)
    steps, ready, free = {}, {(GROUPS, 0): 0.0}, 0.0
    pending = []
    for step in range(last + 1):
        if step < tiles and step % per == per - 1:
            ready[step // per, 0] = ends[step]
        while ready:
            action = min(ready, key=lambda key: (ready[key], key))
            if ready[action] > ends[step] and step < last:
                break
            at = max(ready.pop(action), ends[step])
            steps.setdefault(step, []).append(action)
            group, hop = action
            if hop < count - 1:
                free = max(free, at) + LINK_US
                ready[group, hop + 1] = free + HOP_US
    return steps


def middle_kernel(
    count, tiles, steps, dg1, du1, dg2, du2, hg1, hg2, probs, wg1, wu1, wg2, wu2, wd1, wd2,
    back_out, partial,
    held1, held2, held3, held4, hidden1, hidden2, back, sent, landed, probs_sent, probs_landed,
    load_sem, send_sem, recv_sem,
):
    step = pl.program_id(0)
    here = lax.axis_index("expert")
    right, left = lax.rem(here + 1, count), lax.rem(here + count - 1, count)
    columns = tiles * NTILE
    lanes = columns // GROUPS
    rows = back.shape[0] // count
    loads = [
        pltpu.make_async_copy(source, target, load_sem.at[i])
        for i, (source, target) in enumerate(
            (
                (dg1, held1), (du1, held2), (dg2, held3), (du2, held4),
                (hg1, hidden1), (hg2, hidden2),
            )
        )
    ]

    @pl.when(step == 0)
    def _():
        barrier = pltpu.get_barrier_semaphore()
        for other in (left, right):
            pl.semaphore_signal(barrier, inc=1, device_id={"expert": other}, device_id_type=MESH)
        for load in loads:
            load.start()
        pl.semaphore_wait(barrier, 2)
        total = None
        for i, (left_ref, right_ref) in enumerate(((held1, wg1), (held2, wu1), (held3, wg2), (held4, wu2))):
            loads[i].wait()
            term = dot_nt(left_ref[...], right_ref[...])
            total = term if total is None else total + term
        back[:, :NTILE] = total.astype(BF)

    @pl.when((step > 0) & (step < tiles))
    def _():
        total = (
            dot_nt(held1[...], wg1[...])
            + dot_nt(held2[...], wu1[...])
            + dot_nt(held3[...], wg2[...])
            + dot_nt(held4[...], wu2[...])
        )
        back[:, pl.ds(pl.multiple_of(step * NTILE, NTILE), NTILE)] = total.astype(BF)

    @pl.when(step == tiles)
    def _():
        loads[4].wait()
        loads[5].wait()

    @pl.when(step >= tiles)
    def _():
        total = None
        for hidden, weight in ((hidden1, wd1), (hidden2, wd2)):
            for j in range(PAIR):
                left_value = jnp.concatenate([hidden[i, j] for i in range(hidden.shape[0])], -1)
                term = dot(left_value, weight[:, j].reshape(left_value.shape[1], NTILE))
                total = term if total is None else total + term
        partial[...] = total.astype(BF)

    def copy(group, hop):
        source, target = (sent, landed) if group < GROUPS else (probs_sent, probs_landed)
        at = (hop, group) if group < GROUPS else (hop,)
        return pltpu.make_async_remote_copy(
            src_ref=source.at[at], dst_ref=target.at[at],
            send_sem=send_sem.at[hop, group], recv_sem=recv_sem.at[hop, group],
            device_id={"expert": right}, device_id_type=MESH,
        )

    def advance(group, hop):
        at = (slice(group * lanes, (group + 1) * lanes) if group < GROUPS else slice(columns, columns + LANES))
        block = pl.ds(pl.multiple_of(lax.rem(here - 1 - hop + count, count) * rows, rows), rows)
        total = (back[block, at] if group < GROUPS else probs[block, :]).astype(F32)
        if hop:
            copy(group, hop - 1).wait_recv()
            total = total + (landed[hop - 1, group] if group < GROUPS else probs_landed[hop - 1]).astype(F32)
        if hop == count - 1:
            back_out[:, at] = total
            return
        if group < GROUPS:
            sent[hop, group] = total.astype(BF)
        else:
            probs_sent[hop] = total.astype(BF)
        copy(group, hop).start()

    for at, actions in steps.items():

        @pl.when(step == at)
        def _():
            for group, hop in actions:
                advance(group, hop)

    @pl.when(step == pl.num_programs(0) - 1)
    def _():
        for hop in range(count - 1):
            for group in range(GROUPS + 1):
                copy(group, hop).wait_send()


def middle(pair1, pair2, probs, weights1, weights2, count, call):
    (hg1, dg1, du1), (hg2, dg2, du2) = pair1, pair2
    devices, _, rows, block = hg1.shape
    width = devices * PAIR * block
    tiles = width // NTILE
    flat1, flat2 = [w.reshape(width, w.shape[3]) for w in (weights1, weights2)]
    anywhere = pl.BlockSpec(memory_space=pl.ANY)
    gate = pl.BlockSpec((NTILE, width), lambda s: (jnp.minimum(s, tiles - 1), 0))
    up = pl.BlockSpec((NTILE, width), lambda s: (jnp.minimum(s, tiles - 1), 1))
    second = lambda s: jnp.clip(s - tiles, 0, tiles - 1)
    weight = pl.BlockSpec((devices, PAIR, block, NTILE), lambda s: (0, 0, 0, 2 * width // NTILE + second(s)))
    dma = pltpu.SemaphoreType.DMA
    lanes = width // GROUPS
    return pl.pallas_call(
        functools.partial(middle_kernel, count, tiles, ring_steps(count, tiles, 2 * tiles - 1)),
        grid=(2 * tiles,),
        in_specs=[anywhere] * 6
        + [pl.BlockSpec((rows, LANES), lambda s: (0, 0), pipeline_mode=pl.Buffered(1))]
        + [gate, up, gate, up, weight, weight],
        out_specs=[
            pl.BlockSpec((rows // count, width + LANES), lambda s: (0, 0), pipeline_mode=pl.Buffered(1)),
            pl.BlockSpec((rows, NTILE), lambda s: (0, second(s))),
        ],
        out_shape=[
            jax.ShapeDtypeStruct((rows // count, width + LANES), F32),
            jax.ShapeDtypeStruct((rows, width), BF),
        ],
        scratch_shapes=[pltpu.VMEM((rows, width), BF)] * 4
        + [pltpu.VMEM(hg1.shape, BF)] * 2
        + [
            pltpu.VMEM((rows, width), BF),
            pltpu.VMEM((count - 1, GROUPS, rows // count, lanes), BF),
            pltpu.VMEM((count - 1, GROUPS, rows // count, lanes), BF),
            pltpu.VMEM((count - 1, rows // count, LANES), BF),
            pltpu.VMEM((count - 1, rows // count, LANES), BF),
            dma((6,)),
            dma((count - 1, GROUPS + 1)),
            dma((count - 1, GROUPS + 1)),
        ],
        compiler_params=pltpu.CompilerParams(
            collective_id=call, has_side_effects=True, vmem_limit_bytes=67043328
        ),
        cost_estimate=SHORT,
        name="middle",
    )(dg1, du1, dg2, du2, hg1, hg2, probs, flat1, flat1, flat2, flat2, weights1, weights2)


def body(
    tokens,
    routes,
    prefix,
    query_weight,
    key_weight,
    value_weight,
    output_weight,
    router_weight,
    attention_gain,
    feedforward_gain,
    query_gain,
    key_gain,
    expert_in,
    expert_down,
    cotangent,
):
    count = lax.axis_size("expert")
    here = lax.axis_index("expert")
    rows, width = tokens.shape
    cols = width // count
    experts_all = router_weight.shape[1]
    local = expert_in.shape[1]
    ff_rows = expert_down.shape[0]
    ff = expert_in.shape[2] // 2
    master = query_weight.shape[0]

    def gather(value):
        return lax.all_gather(value, "group", axis=0, tiled=True)

    cores = [list(range(core, width // master, 2)) for core in range(2)]

    def scatter_all(value):
        return lax.psum_scatter(value, "group", scatter_dimension=0, tiled=True)

    def scatter(value):
        return lax.psum_scatter(value, "group", scatter_dimension=0, tiled=True, axis_index_groups=cores)

    def own_cols(weight):
        return lax.dynamic_slice(weight, (0, here * cols), (master, cols)).astype(BF)

    small = jnp.concatenate(
        [
            jnp.pad(router_weight, ((0, 0), (0, LANES // 2 - experts_all))),
            jnp.stack([attention_gain, feedforward_gain, query_gain, key_gain], 1),
            jnp.zeros((master, LANES // 2 - 4), F32),
        ],
        1,
    ).astype(BF)
    dense = gather(
        jnp.concatenate(
            [own_cols(query_weight), own_cols(key_weight), own_cols(value_weight), output_weight.astype(BF), small],
            1,
        )
    )
    qkv_weight = dense[:, : 3 * cols]
    out_weight = dense[:, 3 * cols : 3 * cols + width]
    router = dense[:, 3 * cols + width :]
    gains = router[:, LANES // 2 :].astype(F32).T
    gain_one, gain_two = gains[0:1], gains[1:2]
    gain_query = lax.dynamic_slice(gains[2:3], (0, here * cols), (1, cols))
    gain_key = lax.dynamic_slice(gains[3:4], (0, here * cols), (1, cols))

    expert_ids = jnp.arange(experts_all, dtype=jnp.int32)
    selected = jnp.sum((routes[:, :, None] == expert_ids).astype(F32), 1)
    sent = jnp.concatenate(
        [tokens, jnp.pad(selected, ((0, 0), (0, LANES - experts_all))).astype(BF)], 1
    )
    sent, own1, own2 = gather_and_prep(sent, expert_in, expert_down, count, 2)
    weights1, weights2 = [gather(own).reshape(-1, PAIR, ff_rows, own.shape[1]) for own in (own1, own2)]
    x_all = sent[:, :width].astype(F32)
    chosen = sent[:, width:].astype(F32)

    steps = jnp.arange(HEAD_DIM // 2).astype(F32)
    freq = jnp.exp(steps * (-2.0 * math.log(THETA) / HEAD_DIM))
    angle = jnp.arange(LEN).astype(F32)[:, None] * freq[None, :]
    cosine = jnp.concatenate([jnp.cos(angle)] * 2, 1)
    sine = jnp.concatenate([-jnp.sin(angle), jnp.sin(angle)], 1)

    hidden_one = (x_all * row_scale(x_all) * gain_one).astype(BF)
    cot_blocks = [cotangent]

    def cot_hop(value, *done):
        if len(cot_blocks) < count:
            cot_blocks.append(shift(after(cot_blocks[-1], *done), count, 1))
            value = after(value, cot_blocks[-1])
        return value

    hidden_one = cot_hop(hidden_one, sent)
    qkv = dot(hidden_one, qkv_weight)
    query_lin, key_lin = qkv[:, :cols], qkv[:, cols : 2 * cols]
    value_bf = qkv[:, 2 * cols :].astype(BF)
    value_bf = cot_hop(value_bf)
    squares = jnp.stack([jnp.sum(query_lin * query_lin, -1), jnp.sum(key_lin * key_lin, -1)])
    scales = exchange_sum(after(squares, value_bf), count, 0)
    between = scales
    scales = lax.rsqrt(scales / width + EPS)
    scale_query, scale_key = scales[0][:, None], scales[1][:, None]
    attended, query_bf, key_bf, lse = attend(
        prefix, query_lin, key_lin, value_bf, scale_query, scale_key, gain_query, gain_key, cosine, sine
    )
    attended_bf = heads_to_rows(cot_hop(attended, between), count, 4)

    xfloat = tokens.astype(F32)
    resid = xfloat + dot(attended_bf, out_weight)
    scale_two = row_scale(resid)
    normed_two = resid * scale_two
    hidden_two = (normed_two * gain_two).astype(BF)
    while len(cot_blocks) < count:
        hidden_two = cot_hop(hidden_two, attended_bf)
    b_all, = gather_rows((hidden_two,), count, 3)
    cot_all = jnp.zeros((LEN, width), BF)
    for step, block in enumerate(cot_blocks):
        cot_all = lax.dynamic_update_slice(cot_all, block, (((here - step) % count) * rows, 0))

    def route(value):
        lanes = lax.broadcasted_iota(jnp.int32, (1, LANES), 1)
        return jax.nn.softmax(jnp.where(lanes < experts_all, dot(value, router), -1e30), -1)

    gates = route(b_all) * chosen
    own_probs = route(hidden_two)
    first = jnp.full((1,), here * local, jnp.int32)
    devices = width // master
    hg1, dg1, du1, dgate1 = experts(first, b_all, cot_all, weights1, gates, ff)
    term1, = grad_terms(hg1, b_all, cot_all, dg1, du1, 9)
    sum1 = scatter(term1)
    hg2, dg2, du2, dgate2 = experts(first + PAIR, after(b_all, term1), cot_all, weights2, gates, ff)
    dprobs = (dgate1 + dgate2) * chosen

    back, partial = middle((hg1, dg1, du1), (hg2, dg2, du2), dprobs, weights1, weights2, count, 8)
    grad_probs = back[:, width:]
    grad_logits = (
        own_probs * (grad_probs - jnp.sum(grad_probs * own_probs, -1, keepdims=True))
    ).astype(BF)
    grad_router = dot_tn(grad_logits, hidden_two)[:experts_all]
    grad_two = back[:, :width] + dot_nt(grad_logits, router)
    gain_two_term = jnp.sum(grad_two * normed_two, 0)
    grad_out = cotangent.astype(F32)
    grad_resid = grad_out + norm_back(resid, scale_two, grad_two * gain_two)
    grad_attn_out = grad_resid.astype(BF)
    output_term = dot_tn(attended_bf, grad_attn_out).astype(BF)
    output_sum = scatter_all(output_term)
    term2, first_out, heads_grad = grad_terms(
        hg2, b_all, cot_all, dg2, after(du2, output_term), 10, partial, grad_attn_out, dense, count
    )
    sum2 = scatter(term2)
    ring_out = Ring(partial, first_out, count, here)

    wq, wk, dvl, inner, gain_q_term, gain_k_term = attend_back(
        prefix, query_bf, key_bf, value_bf, heads_grad, lse, query_lin, key_lin,
        scale_query, scale_key, gain_query, gain_key, cosine, sine,
    )
    last = ring_out.hop(inner)
    inner = exchange_sum(after(inner, last).T, count, 1) / width
    ring_out.total = after(ring_out.total, inner)
    dql = scale_query * wq - query_lin * (scale_query**3 * inner[0][:, None])
    dkl = scale_key * wk - key_lin * (scale_key**3 * inner[1][:, None])
    dqkv = jnp.concatenate([dql.astype(BF), dkl.astype(BF), dvl], 1)

    def spread(value):
        return lax.dynamic_update_slice(jnp.zeros((1, width), F32), value, (0, here * cols))

    scale_one = row_scale(xfloat)
    sums = jnp.concatenate(
        [
            jnp.zeros((1, width), F32),
            gain_two_term[None],
            spread(gain_q_term),
            spread(gain_k_term),
            jnp.zeros((4, width), F32),
            grad_router,
        ]
    )
    grad_hidden, *dense_grads, sums = tail(
        after(dqkv, sum1), dense, hidden_one, output_sum, xfloat * scale_one, sums, count, devices, 6
    )

    output = (resid + ring_out.finish(grad_hidden)).astype(BF)
    grad_tokens = grad_resid + norm_back(xfloat, scale_one, grad_hidden * gain_one)
    grad_in, grad_down, grad_q, grad_k, grad_v, grad_out_weight = finish_grads(sum1, sum2, dense_grads)
    return (
        output,
        grad_tokens,
        grad_q,
        grad_k,
        grad_v,
        grad_out_weight,
        sums[8:].T,
        sums[0],
        sums[1],
        sums[2],
        sums[3],
        grad_in,
        grad_down,
    )


def solution(mesh):
    in_specs = (
        P(("group", "expert"), None),
        P(("group", "expert"), None),
        P("group"),
        P("group", None),
        P("group", None),
        P("group", None),
        P("group", None),
        P("group", None),
        P("group"),
        P("group"),
        P("group"),
        P("group"),
        P("group", "expert", None),
        P("group", "expert", None),
        P(("group", "expert"), None),
    )
    out_specs = (
        P(("group", "expert"), None),
        P(("group", "expert"), None),
        P("group", None),
        P("group", None),
        P("group", None),
        P("group", None),
        P("group", None),
        P("group"),
        P("group"),
        P("group"),
        P("group"),
        P("group", "expert", None),
        P("group", "expert", None),
    )
    return jax.shard_map(body, mesh=mesh, in_specs=in_specs, out_specs=out_specs, check_vma=False)
```

time: 1500 us -> 848 us (0.57)
  waiting for transfers between devices: 841 us -> 22.9 us
  Pallas kernels: 127 us -> 672 us
  matrix products: 236 us -> 31.6 us
  local copies, waits for them, and re-layouts: 122 us -> 33.4 us
  starting transfers between devices: 70.3 us -> 8.79 us
  other arithmetic: 70.3 us -> 54 us
    pallas_call x2 -> x12, Pallas kernels: 90.8 us -> 635 us  [the longest x1 177 us: tail(): pl.pallas_call(functools.partial(tail_kernel, count, groups), out_shape=[...]
    ppermute x30 -> x5, waiting for transfers between devices: 417 us -> 22.1 us  [shift(): lax.ppermute(value, 'expert', [(i, (i + step) % count) for i in range(cou...]
    reduce_scatter x4 -> x3, waiting for transfers between devices: 229 us -> 0.01 us  [the longest x2 0.01 us: scatter(): lax.psum_scatter(value, 'group', scatter_dimension=0, tiled=True, axis_in...]
    dot_general x15 -> x1, matrix products: 125 us -> 3.92 us  [dot_nt(): lax.dot_general(left, right, (((1,), (1,)), ((), ())), preferred_element_...]
    unnamed x14 -> x6, waiting for transfers between devices: 113 us -> 0.76 us
    dot_general x5 -> x2, matrix products: 68.4 us -> 6.05 us  [dot_tn(): lax.dot_general(left, right, (((0,), (0,)), ((), ())), preferred_element_...]
    all_gather x1 -> x0, waiting for transfers between devices: 61.6 us -> none  [body(): grad_qkv = lax.all_gather(grad_qkv, 'expert', axis=0, tiled=False)]
    ppermute x30 -> x5, starting transfers between devices: 69.1 us -> 8.55 us  [shift(): lax.ppermute(value, 'expert', [(i, (i + step) % count) for i in range(cou...]
  transfers between devices with their start and end apart: 43 -> 11, of which waited for: 29 -> 3; matrix products, arithmetic and copies ran while one was open for 23% -> 12% of each run, Pallas kernels for 4% -> 79%
where the time goes in v2:
time: 848 us; the launch traced here: 839 us
  Pallas kernels  672 us (79%)
  other arithmetic  54 us (6%)
  local copies, waits for them, and re-layouts  33.4 us (4%)
  matrix products  31.6 us (4%)
  waiting for transfers between devices  22.9 us (3%)
  between operations  15.7 us (2%)
  starting transfers between devices  8.79 us (1%)
    pallas_call x1, Pallas kernels, tail(): pl.pallas_call(functools.partial(tail_kernel, count, groups), out_shape=[...  177 us
    pallas_call x1, Pallas kernels, middle(): pl.pallas_call(functools.partial(middle_kernel, count, tiles, ring_steps(...  95.1 us
    pallas_call x2, Pallas kernels, grad_terms(): pl.pallas_call(functools.partial(grads_kernel, count), grid=(blocks,), in...  86.5 us
    pallas_call x1, Pallas kernels, gather_and_prep(): pl.pallas_call(functools.partial(prep_kernel, count, halves), grid=(maste...  81 us
    pallas_call x1, Pallas kernels, gather_rows(): pl.pallas_call(functools.partial(gather_only, count, arrays), grid=(1,),...  76.6 us
    pallas_call x2, Pallas kernels, experts(): pl.pallas_call(expert_kernel, grid_spec=pltpu.PrefetchScalarGridSpec(num_...  72.9 us
    pallas_call x1, Pallas kernels, attend_back(): pl.pallas_call(attend_back_kernel, out_shape=[jax.ShapeDtypeStruct(ql.sha...  24.7 us
    ppermute x5, waiting for transfers between devices, shift(): lax.ppermute(value, 'expert', [(i, (i + step) % count) for i in range(cou...  22.1 us
  transfers between devices with their start and end apart: 11, of which 3 were waited for; matrix products, arithmetic and copies ran while one was open for 12% of the time, Pallas kernels for 79%

profile of v2, /device:TPU:0, one launch (start us, length us, event | category | flops | bytes accessed | tf_op | source)
XLA Modules:
  0.0 838.6 jit_solution(7832651427203619102)
XLA Ops:
  11.2 1.7 convert_element_type.115
  13.0 1.1 dynamic-slice_convert_fusion.2
  14.1 1.3 dynamic-slice_convert_fusion
  15.4 2.0 concatenate.22
  17.7 1.1 fusion.15.value
  18.8 81.0 %gather2.1 = (bf16[1024,2176]{1,0:T(8,128)(2,1)}, bf16[256,6144]{1,0:T(8,128)(2,1)}, bf16[256,6144]{1,0:T(8,128)(2,1)}) custom-call(bf16[256,2176]{1,0:T(8,128)(2,1)} %fusion.15.value, f32[256,4,2048]{2,1,0:T(4,128)} %up.1, f32[128,4,2048]{2,1,0:T(4,128)} %lower.1), custom_call_target="tpu_custom_call" | custom-call | flops 1000000 | bytes 1000000 | tf_op jit(solution)/shard_map/gather2/pallas_call | solution.py:240
  101.0 1.1 collective-permute-start
  102.1 3.0 fusion.20
  105.7 2.5 pad_maximum_fusion.1
  108.2 3.1 fusion
  111.3 3.0 broadcast_in_dim.55
  114.2 1.0 constant_dynamic-update-slice_fusion.5
  115.3 12.2 %collective-permute-done = bf16[256,2048]{1,0:T(8,128)(2,1)} collective-permute-done((bf16[256,2048]{1,0:T(8,128)(2,1)S(1)}, bf16[256,2048]{1,0:T(8,128)(2,1)}, u32[]{:S(2)}, u32[]{:S(2)}) %collective-permute-start) | collective-permute-done | bytes 1048608 | tf_op jit(solution)/shard_map/ppermute | solution.py:47
  127.5 1.2 convert_bitcast_fusion
  128.7 1.4 fusion.28
  130.8 2.9 fusion.2.hidden
  133.7 10.3 %fusion.5 = f32[1024,1536]{1,0:T(8,128)S(1)} fusion(bf16[1024,2048]{1,0:T(8,128)(2,1)S(1)} %fusion.2.hidden, bf16[2048,3712]{1,0:T(8,128)(2,1)} %all-gather.4.cloned.1.call-done.refs_2_.refs_3_.refs_4_.refs_5_.weight), kind=kOutput, calls=%fused_computation.8 | convolution fusion | flops 6442450944 | bytes 16777216 | tf_op jit(solution)/shard_map/dot_general | solution.py:26
  144.0 1.2 slice.151.vb
  145.2 8.1 collective-permute-done.1
  153.3 2.3 multiply_reduce_fusion.4
  156.2 6.8 exchange0.1
  163.0 0.9 collective-permute-start.2
  163.9 2.3 constant_dynamic-update-slice_fusion.4
  166.2 2.3 constant_dynamic-update-slice_fusion.3
  170.6 1.1 copy.77.sq
  171.6 1.1 copy.78.sk
  172.7 12.5 %attend.1 = (bf16[1024,512]{1,0:T(8,128)(2,1)}, bf16[1024,512]{1,0:T(8,128)(2,1)}, bf16[1024,512]{1,0:T(8,128)(2,1)}, f32[4,1024,1]{2,1,0:T(8,128)}) custom-call(s32[1]{0:T(128)S(6)} %copy.96.prefix_ref, f32[1024,512]{1,0:T(8,128)} %get-tuple-element.126.ql, f32[1024,512]{1,0:T(8,128)} %get-tuple-element.125.kl, bf16[1024,512]{1,0:T(8,128)(2,1)} %slice.151.vb, ...), custom_call_target="tpu_custom_call" | custom-call | flops 1000000 | bytes 1000000 | tf_op jit(solution)/shard_map/attend/pallas_call | solution.py:844
  185.2 1.8 collective-permute-done.2
  187.0 19.4 %heads4.1 = bf16[256,2048]{1,0:T(8,128)(2,1)} custom-call(bf16[1024,512]{1,0:T(8,128)(2,1)} %get-tuple-element.71.value), custom_call_target="tpu_custom_call" | custom-call | flops 1000000 | bytes 1000000 | tf_op jit(solution)/shard_map/heads4/pallas_call | solution.py:449
  206.3 6.2 multiply_reduce_fusion.2
  213.9 1.2 multiply_convert_fusion.refs_0_
  215.1 76.6 %gather3.1.b = bf16[1024,2048]{1,0:T(8,128)(2,1)} custom-call(bf16[256,2048]{1,0:T(8,128)(2,1)} %multiply_convert_fusion.refs_0_), custom_call_target="tpu_custom_call" | custom-call | flops 1000000 | bytes 1000000 | tf_op jit(solution)/shard_map/gather3/pallas_call | solution.py:200
  291.7 3.7 fusion.32
  295.8 2.3 constant_dynamic-update-slice_fusion.2.c.cot
  298.1 2.1 convert_multiply_fusion.7.gates
  300.2 36.0 %experts.2 = (bf16[8,2,1024,128]{3,2,1,0:T(8,128)(2,1)}, bf16[1024,2048]{1,0:T(8,128)(2,1)}, bf16[1024,2048]{1,0:T(8,128)(2,1)}, f32[1024,128]{1,0:T(8,128)}) custom-call(s32[1]{0:T(128)} %bitcast.5.first, bf16[1024,2048]{1,0:T(8,128)(2,1)} %gather3.1.b, bf16[1024,2048]{1,0:T(8,128)(2,1)} %constant_dynamic-update-slice_fusion.2.c.cot, ...), custom_call_target="tpu_custom_call" | custom-call | flops 1000000 | bytes 1000000 | tf_op jit(solution)/shard_map/experts/pallas_call | solution.py:972
  336.2 35.7 %grads9.1 = bf16[1024,6144]{1,0:T(8,128)(2,1)} custom-call(bf16[8,2,1024,128]{3,2,1,0:T(8,128)(2,1)} %get-tuple-element.75.hg.hg1, bf16[1024,2048]{1,0:T(8,128)(2,1)} %gather3.1.b, bf16[1024,2048]{1,0:T(8,128)(2,1)} %constant_dynamic-update-slice_fusion.2.c.cot, bf16[1024,2048]{1,0:T(8,128)(2,1)} %get-tuple-element.73.dg.dg1, ...), custom_call_target="tpu_custom_call" | custom-call | flops 1000000 | bytes 1000000 | tf_op jit(solution)/shard_map/grads9/pallas_call | solution.py:402
  372.0 1.1 copy-done.9
  373.2 1.5 fusion.33
  376.1 36.9 %experts.3 = (bf16[8,2,1024,128]{3,2,1,0:T(8,128)(2,1)}, bf16[1024,2048]{1,0:T(8,128)(2,1)}, bf16[1024,2048]{1,0:T(8,128)(2,1)}, f32[1024,128]{1,0:T(8,128)}) custom-call(s32[1]{0:T(128)S(6)} %add.150.first, bf16[1024,2048]{1,0:T(8,128)(2,1)} %gather3.1.b, bf16[1024,2048]{1,0:T(8,128)(2,1)} %constant_dynamic-update-slice_fusion.2.c.cot, ...), custom_call_target="tpu_custom_call" | custom-call | flops 1000000 | bytes 1000000 | tf_op jit(solution)/shard_map/experts/pallas_call | solution.py:972
  413.0 2.0 convert_multiply_fusion.6.probs
  414.9 95.1 %middle.1 = (f32[256,2176]{1,0:T(8,128)}, bf16[1024,2048]{1,0:T(8,128)(2,1)}) custom-call(bf16[1024,2048]{1,0:T(8,128)(2,1)} %get-tuple-element.73.dg.dg1, bf16[1024,2048]{1,0:T(8,128)(2,1)} %get-tuple-element.74.du.du1, bf16[1024,2048]{1,0:T(8,128)(2,1)} %get-tuple-element.78.dg2.dg, bf16[1024,2048]{1,0:T(8,128)(2,1)} %get-tuple-element.85.du2.du, ...), custom_call_target="tpu_custom_call" | custom-call | flops 1000000 | bytes 1000000 | tf_op jit(solution)/shard_map/middle/pallas_call | solution.py:1143
  510.1 1.2 multiply_reduce_fusion.5
  511.3 1.2 multiply_convert_fusion.1
  512.5 3.9 multiply_reduce_fusion
  516.5 2.0 fusion.27
  518.5 1.0 copy-done.8
  519.5 5.8 convolution_convert_fusion
  525.4 50.8 %grads10.1 = (bf16[1024,6144]{1,0:T(8,128)(2,1)}, bf16[256,2048]{1,0:T(8,128)(2,1)}, bf16[1024,512]{1,0:T(8,128)(2,1)}) custom-call(bf16[8,2,1024,128]{3,2,1,0:T(8,128)(2,1)} %get-tuple-element.80.hg2.hg, bf16[1024,2048]{1,0:T(8,128)(2,1)} %gather3.1.b, bf16[1024,2048]{1,0:T(8,128)(2,1)} %constant_dynamic-update-slice_fusion.2.c.cot, ...), custom_call_target="tpu_custom_call" | custom-call | flops 1000000 | bytes 1000000 | tf_op jit(solution)/shard_map/grads10/pallas_call | solution.py:402
  576.2 1.2 copy-done.4
  577.7 1.6 add_convert_fusion.1
  579.4 5.9 collective-permute-start.3
  585.9 1.6 convert_multiply_fusion.4.normed
  587.5 24.7 %attend_back.1 = (f32[1024,512]{1,0:T(8,128)}, f32[1024,512]{1,0:T(8,128)}, bf16[1024,512]{1,0:T(8,128)(2,1)}, f32[1024,2]{1,0:T(8,128)}, f32[1,512]{1,0:T(1,128)}, /*index=5*/f32[1,512]{1,0:T(1,128)}) custom-call(s32[1]{0:T(128)S(6)} %copy.96.prefix_ref, bf16[1024,512]{1,0:T(8,128)(2,1)} %get-tuple-element.87.qb, bf16[1024,512]{1,0:T(8,128)(2,1)} %get-tuple-element.88.kb, ...), custom_call_target="tpu_custom_call" | custom-call | flops 1000000 | bytes 1000000 | tf_op jit(solution)/shard_map/attend_back/pallas_call | solution.py:909
  613.9 1.4 concatenate.26.sums
  615.2 3.0 convert_add_fusion.1
  619.0 6.8 exchange1.1
  627.2 3.7 subtract_convert_fusion.1
  630.9 1.8 pad_maximum_fusion.grads
  632.7 176.9 %tail.1 = (f32[256,2048]{1,0:T(8,128)}, bf16[256,2048]{1,0:T(8,128)(2,1)}, bf16[256,2048]{1,0:T(8,128)(2,1)}, bf16[256,2048]{1,0:T(8,128)(2,1)}, bf16[256,2048]{1,0:T(8,128)(2,1)}, /*index=5*/f32[24,256]{1,0:T(8,128)}) custom-call(bf16[1024,1536]{1,0:T(8,128)(2,1)} %pad_maximum_fusion.grads, ...), custom_call_target="tpu_custom_call" | custom-call | flops 1000000 | bytes 1000000 | tf_op jit(solution)/shard_map/tail/pallas_call | solution.py:714
  809.7 2.4 fusion.14
  813.3 3.2 add_convert_fusion
  816.5 1.9 fusion.13
  818.5 13.0 %finish.1 = (f32[256,4,2048]{2,1,0:T(4,128)}, f32[128,4,2048]{2,1,0:T(4,128)}, f32[256,2048]{1,0:T(8,128)}, f32[256,2048]{1,0:T(8,128)}, f32[256,2048]{1,0:T(8,128)}, /*index=5*/f32[256,2048]{1,0:T(8,128)}) custom-call(bf16[256,6144]{1,0:T(8,128)(2,1)} %reduce-scatter.4.cloned.1.call-done.refs_0_.refs_1_.refs_2_, ...), custom_call_target="tpu_custom_call" | custom-call | flops 1000000 | bytes 1000000 | tf_op jit(solution)/shard_map/finish/pallas_call | solution.py:789
  (151 shorter events, 18.1 us)
Async XLA Ops:
  7.2 120.3 %all-gather.4.cloned.1.call-start = ((), (), s32[]{:S(2)}) async-start(), calls=%async_computation.3 | async-start | bytes 17104896 | tf_op jit(solution)/shard_map/all_gather | solution.py:1205
  15.4 2.1 copy-start.38
  15.4 2.3 copy-start.3
  17.5 282.7 %all-gather.6.cloned.1.call-start = ((), (), s32[]{:S(2)}) async-start(), calls=%async_computation.4 | async-start | bytes 28311552 | tf_op jit(solution)/shard_map/all_gather | solution.py:1205
  99.7 1.2 copy-start.14
  99.8 276.3 %all-gather.8.cloned.1.call-start = ((), (), s32[]{:S(2)}) async-start(), calls=%async_computation.5 | async-start | bytes 28311552 | tf_op jit(solution)/shard_map/all_gather | solution.py:1205
  100.5 532.2 %reduce-scatter.4.cloned.1.call-start = ((), (), s32[]{:S(2)}) async-start(), calls=%async_computation.6 | async-start | bytes 15728640 | tf_op jit(solution)/shard_map/reduce_scatter | solution.py:1213
  101.0 26.5 %collective-permute-start = (bf16[256,2048]{1,0:T(8,128)(2,1)S(1)}, bf16[256,2048]{1,0:T(8,128)(2,1)}, u32[]{:S(2)}, u32[]{:S(2)}) collective-permute-start(bf16[256,2048]{1,0:T(8,128)(2,1)S(1)} %copy-done.14), channel_id=1, source_target_pairs={{0,1},{1,2},{2,3},{3,0},{4,5},{5,6},{6,7},{7,4},{8,9},{9,10},{10,1... | collective-permute-start | bytes 3145736 | tf_op jit(solution)/shard_map/ppermute | solution.py:47
  105.0 186.7 %copy-start.41 = (pred[128]{0:T(512)(128)(4,1)}, pred[128]{0:T(512)(128)(4,1)S(1)}, u32[]{:S(2)}) copy-start(pred[128]{0:T(512)(128)(4,1)S(1)} %iota_compare_fusion.2) | copy-start | bytes 388
  127.5 25.8 %collective-permute-start.1 = (bf16[256,2048]{1,0:T(8,128)(2,1)}, bf16[256,2048]{1,0:T(8,128)(2,1)}, u32[]{:S(2)}, u32[]{:S(2)}) collective-permute-start(bf16[256,2048]{1,0:T(8,128)(2,1)} %collective-permute-done), channel_id=1, source_target_pairs={{0,1},{1,2},{2,3},{3,0},{4,5},{5,6},{6,7},{7,4},{8,9},{9,10},{10,1... | collective-permute-start | bytes 3145736 | tf_op jit(solution)/shard_map/ppermute | solution.py:47
  130.2 0.6 copy-start.24
  130.2 83.0 %copy-start.26 = (f32[2048]{0:T(1024)}, f32[2048]{0:T(1024)S(1)}, u32[]{:S(2)}) copy-start(f32[2048]{0:T(1024)S(1)} %get-tuple-element.130) | copy-start | bytes 24580
  133.7 10.3 %copy-start.6 = (bf16[1024,2048]{1,0:T(8,128)(2,1)}, bf16[1024,2048]{1,0:T(8,128)(2,1)S(1)}, u32[]{:S(2)}) copy-start(bf16[1024,2048]{1,0:T(8,128)(2,1)S(1)} %fusion.2.hidden) | copy-start | bytes 12582916
  144.0 11.6 %copy-start.7 = (f32[1024,1536]{1,0:T(8,128)}, f32[1024,1536]{1,0:T(8,128)S(1)}, u32[]{:S(2)}) copy-start(f32[1024,1536]{1,0:T(8,128)S(1)} %fusion.5) | copy-start | bytes 18874372
  163.0 24.0 %collective-permute-start.2 = (bf16[256,2048]{1,0:T(8,128)(2,1)}, bf16[256,2048]{1,0:T(8,128)(2,1)}, u32[]{:S(2)}, u32[]{:S(2)}) collective-permute-start(bf16[256,2048]{1,0:T(8,128)(2,1)} %collective-permute-done.1), channel_id=1, source_target_pairs={{0,1},{1,2},{2,3},{3,0},{4,5},{5,6},{6,7},{7,4},{8,9},{9,10},{10,1... | collective-permute-start | bytes 3145736 | tf_op jit(solution)/shard_map/ppermute | solution.py:47
  166.2 3.8 copy-start.31
  212.5 1.3 copy-start
  213.2 0.7 copy-start.33
  371.9 1.2 copy-start.9
  371.9 1.2 copy-start.42
  372.0 260.8 %reduce-scatter.6.cloned.1.call-start = ((), (), s32[]{:S(2)}) async-start(), calls=%async_computation.7 | async-start | bytes 9437184 | tf_op jit(solution)/shard_map/reduce_scatter | solution.py:1210
  374.7 0.6 copy-start.17
  374.7 0.6 copy-start.35
  376.1 36.9 %copy-start.22 = (f32[1024,128]{1,0:T(8,128)S(1)}, f32[1024,128]{1,0:T(8,128)}, u32[]{:S(2)}) copy-start(f32[1024,128]{1,0:T(8,128)} %get-tuple-element.81) | copy-start | bytes 1572868
  512.5 4.0 copy-start.20
  512.5 4.0 copy-start.1
  512.5 4.0 copy-start.15
  512.5 4.0 copy-start.27
  512.5 4.0 copy-start.34
  512.5 4.0 copy-start.40
  516.5 3.0 copy-start.13
  518.5 1.0 copy-start.8
  525.3 293.1 %reduce-scatter.8.cloned.1.call-start = ((), (), s32[]{:S(2)}) async-start(), calls=%async_computation.8 | async-start | bytes 15728640 | tf_op jit(solution)/shard_map/reduce_scatter | solution.py:1213
  576.2 1.2 copy-start.4
  576.2 1.6 copy-start.18
  579.4 35.9 %collective-permute-start.3 = (bf16[256,2048]{1,0:T(8,128)(2,1)S(1)}, bf16[256,2048]{1,0:T(8,128)(2,1)}, u32[]{:S(2)}, u32[]{:S(2)}) collective-permute-start(bf16[256,2048]{1,0:T(8,128)(2,1)S(1)} %add_convert_fusion.1), channel_id=1, source_target_pairs={{0,1},{1,2},{2,3},{3,0},{4,5},{5,6},{6,7},{7,4},{8,9},{9,10},{10,1... | collective-permute-start | bytes 3145736 | tf_op jit(solution)/shard_map/ppermute | solution.py:47
  585.9 1.6 copy-start.36
  587.5 26.1 %copy-start.10 = (bf16[256,2048]{1,0:T(8,128)(2,1)S(1)}, bf16[256,2048]{1,0:T(8,128)(2,1)}, u32[]{:S(2)}) copy-start(bf16[256,2048]{1,0:T(8,128)(2,1)} %multiply_convert_fusion.refs_0_) | copy-start | bytes 3145732
  587.5 26.1 %copy-start.21 = (bf16[256,128]{1,0:T(8,128)(2,1)S(1)}, bf16[256,128]{1,0:T(8,128)(2,1)}, u32[]{:S(2)}) copy-start(bf16[256,128]{1,0:T(8,128)(2,1)} %copy-done.20) | copy-start | bytes 196612
  587.5 26.4 %copy-start.30 = (f32[2048]{0:T(1024)S(1)}, f32[2048]{0:T(1024)}, u32[]{:S(2)}) copy-start(f32[2048]{0:T(1024)} %get-tuple-element.117) | copy-start | bytes 24580
  613.8 13.4 %copy-start.28 = (f32[1,1024]{1,0:T(1,128)S(1)}, f32[1,1024]{1,0:T(1,128)}, u32[]{:S(2)}) copy-start(f32[1,1024]{1,0:T(1,128)} %get-tuple-element.135) | copy-start | bytes 12292
  613.8 13.4 %copy-start.29 = (f32[1,1024]{1,0:T(1,128)S(1)}, f32[1,1024]{1,0:T(1,128)}, u32[]{:S(2)}) copy-start(f32[1,1024]{1,0:T(1,128)} %get-tuple-element.138) | copy-start | bytes 12292
  613.8 13.4 %copy-start.16 = (f32[1024,512]{1,0:T(8,128)S(1)}, f32[1024,512]{1,0:T(8,128)}, u32[]{:S(2)}) copy-start(f32[1024,512]{1,0:T(8,128)} %get-tuple-element.95) | copy-start | bytes 6291460
  615.2 3.0 copy-start.23
  626.5 183.1 %collective-permute-start.4 = (bf16[256,2048]{1,0:T(8,128)(2,1)}, bf16[256,2048]{1,0:T(8,128)(2,1)}, u32[]{:S(2)}, u32[]{:S(2)}) collective-permute-start(bf16[256,2048]{1,0:T(8,128)(2,1)} %convert_add_fusion.1), channel_id=1, source_target_pairs={{0,1},{1,2},{2,3},{3,0},{4,5},{5,6},{6,7},{7,4},{8,9},{9,10},{10,1... | collective-permute-start | bytes 3145736 | tf_op jit(solution)/shard_map/ppermute | solution.py:47
  627.2 3.7 copy-start.19
  809.6 2.4 copy-start.32
  809.6 3.6 copy-start.2
  809.7 6.8 copy-start.25
  813.2 3.2 copy-start.5
  813.2 3.2 copy-start.11
  813.2 3.2 copy-start.12
  813.2 3.3 copy-start.37
  813.3 3.3 copy-start.39
Sparse Core Ops, SparseCore 0:
  17.6 85.8 all-gather.3
  105.4 125.3 all-gather.5
  232.7 131.3 all-gather.7
  372.1 119.0 reduce-scatter.3
  525.4 77.5 reduce-scatter.5
  606.3 148.0 reduce-scatter.7

commit v3 on v2

--- a/solution.py
+++ b/solution.py
@@ -414,6 +414,63 @@
     )(*operands)
 
 
+def pair_kernel(left, right, out, sent, landed, send_sem, recv_sem):
+    step = pl.program_id(0)
+    group = lax.axis_index("group")
+    core, other = lax.rem(group, 2), flipped(group, 1)
+    size, chips = out.shape[0], landed.shape[0]
+
+    def copy(chip):
+        return pltpu.make_async_remote_copy(
+            src_ref=sent.at[chip], dst_ref=landed.at[chip], send_sem=send_sem.at[chip], recv_sem=recv_sem.at[chip],
+            device_id={"group": other}, device_id_type=MESH,
+        )
+
+    def term(place):
+        return dot_tn(left[:, pl.ds(pl.multiple_of(place * size, size), size)], right[...])
+
+    @pl.when(step == 0)
+    def _():
+        barrier = pltpu.get_barrier_semaphore()
+        pl.semaphore_signal(barrier, inc=1, device_id={"group": other}, device_id_type=MESH)
+        pl.semaphore_wait(barrier, 1)
+
+    @pl.when(step < chips)
+    def _():
+        sent[step] = term(2 * step + 1 - core).astype(BF)
+        copy(step).start()
+
+    @pl.when(step >= chips)
+    def _():
+        chip = step - chips
+        total = term(2 * chip + core)
+        copy(chip).wait_recv()
+        out[...] = (total + landed[chip].astype(F32)).astype(BF)
+
+    @pl.when(step == 2 * chips - 1)
+    def _():
+        for chip in range(chips):
+            copy(chip).wait_send()
+
+
+def pair_terms(left, right, groups, call):
+    size, chips = left.shape[1] // groups, groups // 2
+    columns = right.shape[1]
+    whole = lambda value: pl.BlockSpec(value.shape, lambda p: (0, 0))
+    dma = pltpu.SemaphoreType.DMA
+    return pl.pallas_call(
+        pair_kernel,
+        grid=(groups,),
+        in_specs=[whole(left), whole(right)],
+        out_specs=pl.BlockSpec((size, columns), lambda p: (jnp.maximum(p - chips, 0), 0)),
+        out_shape=jax.ShapeDtypeStruct((chips * size, columns), BF),
+        scratch_shapes=[pltpu.VMEM((chips, size, columns), BF)] * 2 + [dma((chips,))] * 2,
+        compiler_params=pltpu.CompilerParams(collective_id=call, has_side_effects=True),
+        cost_estimate=SHORT,
+        name="pair%d" % call,
+    )(left, right)
+
+
 def heads_kernel(count, value, out, send_sem, recv_sem, own_sem):
     here = lax.axis_index("expert")
     rows, cols = out.shape[0], value.shape[1]
@@ -475,14 +532,14 @@
 
 
 def tail_kernel(
-    count, groups, grads, weight, hidden, output_sum, normed, sums, rows_out, *refs
+    count, groups, grads, weight, hidden, normed, sums, rows_out, *refs
 ):
-    final_outs, sums_out, refs = refs[:4], refs[4], refs[5:]
+    final_outs, sums_out, refs = refs[:3], refs[3], refs[4:]
     (
-        query_out, key_out, value_out, output_out, final_sem,
-        sent, landed, core_out, core_in, held, step_in, done, part_sent, part_in, small, small_in, small_sum,
+        query_out, key_out, value_out, final_sem,
+        sent, landed, core_out, core_in, held, step_in, done, small, small_in, small_sum,
         all_in, own_sem, token_send, token_recv, core_send, core_recv, step_send, step_recv, whole_send,
-        whole_recv, part_send, part_recv, sum_send, sum_recv, small_send, small_recv, all_send, all_recv,
+        whole_recv, small_send, small_recv, all_send, all_recv,
     ) = refs
     here, group = lax.axis_index("expert"), lax.axis_index("group")
     right, left = lax.rem(here + 1, count), lax.rem(here + count - 1, count)
@@ -501,7 +558,6 @@
     half = width // 2
     master, columns = held.shape[1:]
     cols = width // count
-    slab = master // count
 
     def to(axis, other, source, target, send, receive):
         return pltpu.make_async_remote_copy(
@@ -617,39 +673,14 @@
                 for copy in copies[stream][level + 1]:
                     copy.start()
 
-    def slab_of(other):
-        return pl.ds(pl.multiple_of(other * slab, slab), slab)
-
-    def slab_hop(step):
-        return to("expert", right, part_sent.at[step], part_in.at[step], part_send.at[step], part_recv.at[step])
-
-    def slab_step(step):
-        total = output_sum[slab_of(lax.rem(here - 1 - step + count, count)), :].astype(F32)
-        if step:
-            slab_hop(step - 1).wait_recv()
-            total = total + part_in[step - 1].astype(F32)
-        if step < count - 1:
-            part_sent[step] = total.astype(BF)
-            slab_hop(step).start()
-        else:
-            output_out[slab_of(here), :] = total.astype(BF)
-
-    def sum_hop(step):
-        place = output_out.at[slab_of(lax.rem(here - step + count, count))]
-        return to("expert", right, place, place, sum_send.at[step], sum_recv.at[step])
-
-    slab_step(0)
     levels = iter(range(len(bits)))
     for step in range(1, count):
         token_step(step)
-        slab_step(step)
         level = next(levels, None)
         if level is not None:
             reduce_step(level)
-    for level in levels:
-        reduce_step(level)
-    whole_start()
-    sum_hop(0).start()
+            if level == len(bits) - 1:
+                whole_start()
     small[...] = sums[...]
     small[0:1, :] = jnp.sum(rows_out[...] * normed[...], 0, keepdims=True)
     small_copies = [
@@ -673,8 +704,6 @@
         for piece in range(pieces):
             whole_hop(step - 1, piece).wait_recv()
             whole_hop(step, piece).start()
-        sum_hop(step - 1).wait_recv()
-        sum_hop(step).start()
     for i, copy in enumerate(all_copies):
         copy.wait()
         total = total + all_in[i]
@@ -682,18 +711,15 @@
     for piece in range(pieces):
         own[piece].wait()
         whole_hop(count - 2, piece).wait_recv()
-    sum_hop(count - 2).wait_recv()
     finals = [
         pltpu.make_async_copy(source, target, final_sem.at[i])
-        for i, (source, target) in enumerate(zip((query_out, key_out, value_out, output_out), final_outs))
+        for i, (source, target) in enumerate(zip((query_out, key_out, value_out), final_outs))
     ]
     for copy in finals:
         copy.start()
     for copy in core:
         copy.wait_send()
     for step in range(count - 1):
-        slab_hop(step).wait_send()
-        sum_hop(step).wait_send()
         if step >= count - 3:
             for piece in range(2):
                 token_hop(step, piece).wait_send()
@@ -703,31 +729,29 @@
         copy.wait()
 
 
-def tail(grads, dense, hidden, output_sum, normed, sums, count, groups, call):
+def tail(grads, dense, hidden, normed, sums, count, groups, call):
     rows, width = hidden.shape[0] // count, hidden.shape[1]
     own_columns = grads.shape[1]
     master = width // groups
     rest = groups // 2
-    slab = master // count
     dma = pltpu.SemaphoreType.DMA
     vmem = pl.BlockSpec(memory_space=pltpu.VMEM)
     return pl.pallas_call(
         functools.partial(tail_kernel, count, groups),
-        out_shape=[jax.ShapeDtypeStruct((rows, width), F32)] + [jax.ShapeDtypeStruct((master, width), BF)] * 4
+        out_shape=[jax.ShapeDtypeStruct((rows, width), F32)] + [jax.ShapeDtypeStruct((master, width), BF)] * 3
         + [jax.ShapeDtypeStruct((sums.shape[0], master), F32)],
         grid=(1,),
         in_specs=[
             pl.BlockSpec(grads.shape, lambda i: (0, 0)),
             pl.BlockSpec((width, own_columns), lambda i: (0, 0)),
             pl.BlockSpec(hidden.shape, lambda i: (0, 0)),
-            pl.BlockSpec(output_sum.shape, lambda i: (0, 0)),
             pl.BlockSpec(normed.shape, lambda i: (0, 0)),
             pl.BlockSpec(sums.shape, lambda i: (0, 0)),
         ],
-        out_specs=[vmem] + [pl.BlockSpec(memory_space=pl.ANY)] * 4 + [vmem],
-        scratch_shapes=[pltpu.VMEM((master, width), BF)] * 4
+        out_specs=[vmem] + [pl.BlockSpec(memory_space=pl.ANY)] * 3 + [vmem],
+        scratch_shapes=[pltpu.VMEM((master, width), BF)] * 3
         + [
-            dma((4,)),
+            dma((3,)),
             pltpu.VMEM((2, 2, rows, width // 2), BF),
             pltpu.VMEM((count - 1, 2, rows, width // 2), BF),
             pltpu.VMEM((rest, master, own_columns), BF),
@@ -735,8 +759,6 @@
             pltpu.VMEM((rest, master, own_columns), BF),
             pltpu.VMEM((2, rest - 1, master, own_columns // 2), BF),
             pltpu.VMEM((master, own_columns), BF),
-            pltpu.VMEM((count - 1, slab, width), BF),
-            pltpu.VMEM((count - 1, slab, width), BF),
             pltpu.VMEM(sums.shape, F32),
             pltpu.VMEM((groups - 1, sums.shape[0], master), F32),
             pltpu.VMEM((sums.shape[0], master), F32),
@@ -751,7 +773,6 @@
             dma((count - 1, 3)),
             dma((count - 1, 3)),
         ]
-        + [dma((count - 1,))] * 4
         + [dma((groups - 1,))] * 2
         + [dma((count - 1,))] * 2,
         compiler_params=pltpu.CompilerParams(
@@ -759,7 +780,7 @@
         ),
         cost_estimate=SHORT,
         name="tail",
-    )(grads, dense, hidden, output_sum, normed, sums)
+    )(grads, dense, hidden, normed, sums)
 
 
 def finish_kernel(*refs):
@@ -1206,9 +1227,6 @@
 
     cores = [list(range(core, width // master, 2)) for core in range(2)]
 
-    def scatter_all(value):
-        return lax.psum_scatter(value, "group", scatter_dimension=0, tiled=True)
-
     def scatter(value):
         return lax.psum_scatter(value, "group", scatter_dimension=0, tiled=True, axis_index_groups=cores)
 
@@ -1304,6 +1322,7 @@
     dprobs = (dgate1 + dgate2) * chosen
 
     back, partial = middle((hg1, dg1, du1), (hg2, dg2, du2), dprobs, weights1, weights2, count, 8)
+    back = after(back, sum1)
     grad_probs = back[:, width:]
     grad_logits = (
         own_probs * (grad_probs - jnp.sum(grad_probs * own_probs, -1, keepdims=True))
@@ -1314,13 +1333,14 @@
     grad_out = cotangent.astype(F32)
     grad_resid = grad_out + norm_back(resid, scale_two, grad_two * gain_two)
     grad_attn_out = grad_resid.astype(BF)
-    output_term = dot_tn(attended_bf, grad_attn_out).astype(BF)
-    output_sum = scatter_all(output_term)
+    output_term = pair_terms(attended_bf, grad_attn_out, devices, 12)
+    output_sum = scatter(output_term)
     term2, first_out, heads_grad = grad_terms(
         hg2, b_all, cot_all, dg2, after(du2, output_term), 10, partial, grad_attn_out, dense, count
     )
     sum2 = scatter(term2)
     ring_out = Ring(partial, first_out, count, here)
+    output_sum = lax.psum(after(output_sum, heads_grad), "expert")
 
     wq, wk, dvl, inner, gain_q_term, gain_k_term = attend_back(
         prefix, query_bf, key_bf, value_bf, heads_grad, lse, query_lin, key_lin,
@@ -1348,12 +1368,14 @@
         ]
     )
     grad_hidden, *dense_grads, sums = tail(
-        after(dqkv, sum1), dense, hidden_one, output_sum, xfloat * scale_one, sums, count, devices, 6
+        dqkv, dense, hidden_one, xfloat * scale_one, sums, count, devices, 6
     )
 
     output = (resid + ring_out.finish(grad_hidden)).astype(BF)
     grad_tokens = grad_resid + norm_back(xfloat, scale_one, grad_hidden * gain_one)
-    grad_in, grad_down, grad_q, grad_k, grad_v, grad_out_weight = finish_grads(sum1, sum2, dense_grads)
+    grad_in, grad_down, grad_q, grad_k, grad_v, grad_out_weight = finish_grads(
+        sum1, sum2, [*dense_grads, output_sum]
+    )
     return (
         output,
         grad_tokens,

time: 848 us -> 842 us (level)
  Pallas kernels: 672 us -> 659 us
  waiting for transfers between devices: 22.9 us -> 35.2 us
    pallas_call x1, Pallas kernels: 177 us -> 153 us  [tail(): pl.pallas_call(functools.partial(tail_kernel, count, groups), out_shape=[...]
    pallas_call x0 -> x1, Pallas kernels: none -> 10.7 us  [pair_terms(): pl.pallas_call(pair_kernel, grid=(groups,), in_specs=[whole(left), whole(...]
    ppermute x5, waiting for transfers between devices: 22.1 us -> 32.2 us  [shift(): lax.ppermute(value, 'expert', [(i, (i + step) % count) for i in range(cou...]
  transfers between devices with their start and end apart: 11 -> 12, of which waited for: 3 -> 5; matrix products, arithmetic and copies ran while one was open for 12% -> 11% of each run, Pallas kernels for 79% -> 76%
where the time goes in v3:
time: 842 us; the launch traced here: 832 us
  Pallas kernels  659 us (78%)
  other arithmetic  55.4 us (7%)
  waiting for transfers between devices  35.2 us (4%)
  local copies, waits for them, and re-layouts  33.3 us (4%)
  matrix products  25.8 us (3%)
  between operations  15.7 us (2%)
    pallas_call x1, Pallas kernels, tail(): pl.pallas_call(functools.partial(tail_kernel, count, groups), out_shape=[...  153 us
    pallas_call x1, Pallas kernels, middle(): pl.pallas_call(functools.partial(middle_kernel, count, tiles, ring_steps(...  95.1 us
    pallas_call x2, Pallas kernels, grad_terms(): pl.pallas_call(functools.partial(grads_kernel, count), grid=(blocks,), in...  86.7 us
    pallas_call x1, Pallas kernels, gather_and_prep(): pl.pallas_call(functools.partial(prep_kernel, count, halves), grid=(maste...  80.9 us
    pallas_call x1, Pallas kernels, gather_rows(): pl.pallas_call(functools.partial(gather_only, count, arrays), grid=(1,),...  76.6 us
    pallas_call x2, Pallas kernels, experts(): pl.pallas_call(expert_kernel, grid_spec=pltpu.PrefetchScalarGridSpec(num_...  72.9 us
    ppermute x5, waiting for transfers between devices, shift(): lax.ppermute(value, 'expert', [(i, (i + step) % count) for i in range(cou...  32.2 us
    pallas_call x1, Pallas kernels, attend_back(): pl.pallas_call(attend_back_kernel, out_shape=[jax.ShapeDtypeStruct(ql.sha...  24 us
  transfers between devices with their start and end apart: 12, of which 5 were waited for; matrix products, arithmetic and copies ran while one was open for 11% of the time, Pallas kernels for 76%

profile of v3, /device:TPU:0, one launch (start us, length us, event | category | flops | bytes accessed | tf_op | source)
XLA Modules:
  0.0 832.3 jit_solution(11220427166015744080)
XLA Ops:
  11.2 1.7 convert_element_type.112
  13.0 1.1 dynamic-slice_convert_fusion.2
  14.1 1.3 dynamic-slice_convert_fusion
  15.4 2.0 concatenate.22
  17.7 1.1 fusion.15.value
  18.8 80.9 %gather2.1 = (bf16[1024,2176]{1,0:T(8,128)(2,1)}, bf16[256,6144]{1,0:T(8,128)(2,1)}, bf16[256,6144]{1,0:T(8,128)(2,1)}) custom-call(bf16[256,2176]{1,0:T(8,128)(2,1)} %fusion.15.value, f32[256,4,2048]{2,1,0:T(4,128)} %up.1, f32[128,4,2048]{2,1,0:T(4,128)} %lower.1), custom_call_target="tpu_custom_call" | custom-call | flops 1000000 | bytes 1000000 | tf_op jit(solution)/shard_map/gather2/pallas_call | solution.py:240
  100.9 1.1 collective-permute-start
  102.0 3.0 fusion.20
  105.6 2.5 pad_maximum_fusion.1
  108.2 3.1 fusion
  111.3 3.0 broadcast_in_dim.55
  115.3 12.2 %collective-permute-done = bf16[256,2048]{1,0:T(8,128)(2,1)} collective-permute-done((bf16[256,2048]{1,0:T(8,128)(2,1)S(1)}, bf16[256,2048]{1,0:T(8,128)(2,1)}, u32[]{:S(2)}, u32[]{:S(2)}) %collective-permute-start) | collective-permute-done | bytes 1048608 | tf_op jit(solution)/shard_map/ppermute | solution.py:47
  127.4 1.2 convert_bitcast_fusion
  128.7 1.4 fusion.28
  130.7 2.9 fusion.2.hidden
  133.6 10.3 %fusion.5 = f32[1024,1536]{1,0:T(8,128)S(1)} fusion(bf16[1024,2048]{1,0:T(8,128)(2,1)S(1)} %fusion.2.hidden, bf16[2048,3712]{1,0:T(8,128)(2,1)} %all-gather.4.cloned.1.call-done.refs_2_.refs_3_.refs_4_.refs_5_.weight), kind=kOutput, calls=%fused_computation.7 | convolution fusion | flops 6442450944 | bytes 16777216 | tf_op jit(solution)/shard_map/dot_general | solution.py:26
  143.9 1.2 slice.151.vb
  145.2 8.1 collective-permute-done.1
  153.2 2.3 multiply_reduce_fusion.4
  156.1 6.8 exchange0.1
  163.9 2.3 constant_dynamic-update-slice_fusion.4
  166.2 2.3 constant_dynamic-update-slice_fusion.3
  170.6 1.1 copy.77.sq
  171.6 1.0 copy.78.sk
  172.7 12.5 %attend.1 = (bf16[1024,512]{1,0:T(8,128)(2,1)}, bf16[1024,512]{1,0:T(8,128)(2,1)}, bf16[1024,512]{1,0:T(8,128)(2,1)}, f32[4,1024,1]{2,1,0:T(8,128)}) custom-call(s32[1]{0:T(128)S(6)} %copy.97.prefix_ref, f32[1024,512]{1,0:T(8,128)} %get-tuple-element.126.ql, f32[1024,512]{1,0:T(8,128)} %get-tuple-element.125.kl, bf16[1024,512]{1,0:T(8,128)(2,1)} %slice.151.vb, ...), custom_call_target="tpu_custom_call" | custom-call | flops 1000000 | bytes 1000000 | tf_op jit(solution)/shard_map/attend/pallas_call | solution.py:865
  185.2 1.8 collective-permute-done.2
  187.0 19.4 %heads4.1.left = bf16[256,2048]{1,0:T(8,128)(2,1)} custom-call(bf16[1024,512]{1,0:T(8,128)(2,1)} %get-tuple-element.71.value), custom_call_target="tpu_custom_call" | custom-call | flops 1000000 | bytes 1000000 | tf_op jit(solution)/shard_map/heads4/pallas_call | solution.py:506
  206.4 6.2 multiply_reduce_fusion.2
  213.9 1.2 multiply_convert_fusion.refs_0_
  215.2 76.6 %gather3.1.b = bf16[1024,2048]{1,0:T(8,128)(2,1)} custom-call(bf16[256,2048]{1,0:T(8,128)(2,1)} %multiply_convert_fusion.refs_0_), custom_call_target="tpu_custom_call" | custom-call | flops 1000000 | bytes 1000000 | tf_op jit(solution)/shard_map/gather3/pallas_call | solution.py:200
  291.8 3.6 fusion.32
  295.8 2.3 constant_dynamic-update-slice_fusion.2.c.cot
  298.1 2.1 convert_multiply_fusion.7.gates
  300.2 36.0 %experts.2 = (bf16[8,2,1024,128]{3,2,1,0:T(8,128)(2,1)}, bf16[1024,2048]{1,0:T(8,128)(2,1)}, bf16[1024,2048]{1,0:T(8,128)(2,1)}, f32[1024,128]{1,0:T(8,128)}) custom-call(s32[1]{0:T(128)} %bitcast.5.first, bf16[1024,2048]{1,0:T(8,128)(2,1)} %gather3.1.b, bf16[1024,2048]{1,0:T(8,128)(2,1)} %constant_dynamic-update-slice_fusion.2.c.cot, ...), custom_call_target="tpu_custom_call" | custom-call | flops 1000000 | bytes 1000000 | tf_op jit(solution)/shard_map/experts/pallas_call | solution.py:993
  336.2 35.8 %grads9.1 = bf16[1024,6144]{1,0:T(8,128)(2,1)} custom-call(bf16[8,2,1024,128]{3,2,1,0:T(8,128)(2,1)} %get-tuple-element.75.hg.hg1, bf16[1024,2048]{1,0:T(8,128)(2,1)} %gather3.1.b, bf16[1024,2048]{1,0:T(8,128)(2,1)} %constant_dynamic-update-slice_fusion.2.c.cot, bf16[1024,2048]{1,0:T(8,128)(2,1)} %get-tuple-element.73.dg.dg1, ...), custom_call_target="tpu_custom_call" | custom-call | flops 1000000 | bytes 1000000 | tf_op jit(solution)/shard_map/grads9/pallas_call | solution.py:402
  372.1 1.1 copy-done.8
  373.2 1.5 fusion.33
  376.2 36.9 %experts.3 = (bf16[8,2,1024,128]{3,2,1,0:T(8,128)(2,1)}, bf16[1024,2048]{1,0:T(8,128)(2,1)}, bf16[1024,2048]{1,0:T(8,128)(2,1)}, f32[1024,128]{1,0:T(8,128)}) custom-call(s32[1]{0:T(128)S(6)} %add.152.first, bf16[1024,2048]{1,0:T(8,128)(2,1)} %gather3.1.b, bf16[1024,2048]{1,0:T(8,128)(2,1)} %constant_dynamic-update-slice_fusion.2.c.cot, ...), custom_call_target="tpu_custom_call" | custom-call | flops 1000000 | bytes 1000000 | tf_op jit(solution)/shard_map/experts/pallas_call | solution.py:993
  413.0 2.0 convert_multiply_fusion.6.probs
  415.0 95.1 %middle.1 = (f32[256,2176]{1,0:T(8,128)}, bf16[1024,2048]{1,0:T(8,128)(2,1)}) custom-call(bf16[1024,2048]{1,0:T(8,128)(2,1)} %get-tuple-element.73.dg.dg1, bf16[1024,2048]{1,0:T(8,128)(2,1)} %get-tuple-element.74.du.du1, bf16[1024,2048]{1,0:T(8,128)(2,1)} %get-tuple-element.78.dg2.dg, bf16[1024,2048]{1,0:T(8,128)(2,1)} %get-tuple-element.86.du2.du, ...), custom_call_target="tpu_custom_call" | custom-call | flops 1000000 | bytes 1000000 | tf_op jit(solution)/shard_map/middle/pallas_call | solution.py:1164
  510.1 1.2 multiply_reduce_fusion.5
  511.3 1.2 multiply_convert_fusion.1
  512.5 3.9 multiply_reduce_fusion
  516.5 2.4 fusion.27
  518.9 10.7 %pair12.1 = bf16[1024,2048]{1,0:T(8,128)(2,1)} custom-call(bf16[256,2048]{1,0:T(8,128)(2,1)} %heads4.1.left, bf16[256,2048]{1,0:T(8,128)(2,1)} %get-tuple-element.121.right.refs_1_), custom_call_target="tpu_custom_call" | custom-call | flops 1000000 | bytes 1000000 | tf_op jit(solution)/shard_map/pair12/pallas_call | solution.py:461
  529.6 50.9 %grads10.1 = (bf16[1024,6144]{1,0:T(8,128)(2,1)}, bf16[256,2048]{1,0:T(8,128)(2,1)}, bf16[1024,512]{1,0:T(8,128)(2,1)}) custom-call(bf16[8,2,1024,128]{3,2,1,0:T(8,128)(2,1)} %get-tuple-element.80.hg2.hg, bf16[1024,2048]{1,0:T(8,128)(2,1)} %gather3.1.b, bf16[1024,2048]{1,0:T(8,128)(2,1)} %constant_dynamic-update-slice_fusion.2.c.cot, ...), custom_call_target="tpu_custom_call" | custom-call | flops 1000000 | bytes 1000000 | tf_op jit(solution)/shard_map/grads10/pallas_call | solution.py:402
  580.6 1.5 reduce-scatter.8.cloned.1.call-done
  583.7 1.6 add_convert_fusion.1
  585.4 4.4 collective-permute-start.3
  590.3 1.6 convert_multiply_fusion.4.normed
  591.9 24.0 %attend_back.1 = (f32[1024,512]{1,0:T(8,128)}, f32[1024,512]{1,0:T(8,128)}, bf16[1024,512]{1,0:T(8,128)(2,1)}, f32[1024,2]{1,0:T(8,128)}, f32[1,512]{1,0:T(1,128)}, /*index=5*/f32[1,512]{1,0:T(1,128)}) custom-call(s32[1]{0:T(128)S(6)} %copy.97.prefix_ref, bf16[1024,512]{1,0:T(8,128)(2,1)} %get-tuple-element.88.qb, bf16[1024,512]{1,0:T(8,128)(2,1)} %get-tuple-element.89.kb, ...), custom_call_target="tpu_custom_call" | custom-call | flops 1000000 | bytes 1000000 | tf_op jit(solution)/shard_map/attend_back/pallas_call | solution.py:930
  617.6 1.4 concatenate.26.sums
  618.9 10.2 %collective-permute-done.3 = bf16[256,2048]{1,0:T(8,128)(2,1)} collective-permute-done((bf16[256,2048]{1,0:T(8,128)(2,1)S(1)}, bf16[256,2048]{1,0:T(8,128)(2,1)}, u32[]{:S(2)}, u32[]{:S(2)}) %collective-permute-start.3) | collective-permute-done | bytes 1048608 | tf_op jit(solution)/shard_map/ppermute | solution.py:47
  629.1 3.0 convert_add_fusion.1
  632.9 8.0 exchange1.1
  642.5 3.4 subtract_convert_fusion.1
  645.9 1.8 pad_maximum_fusion.grads
  647.7 152.7 %tail.1 = (f32[256,2048]{1,0:T(8,128)}, bf16[256,2048]{1,0:T(8,128)(2,1)}, bf16[256,2048]{1,0:T(8,128)(2,1)}, bf16[256,2048]{1,0:T(8,128)(2,1)}, f32[24,256]{1,0:T(8,128)}) custom-call(bf16[1024,1536]{1,0:T(8,128)(2,1)} %pad_maximum_fusion.grads, bf16[2048,3712]{1,0:T(8,128)(2,1)} %all-gather.4.cloned.1.call-done.refs_2_.refs_3_.refs_4_.refs_5_.weight, ...), custom_call_target="tpu_custom_call" | custom-call | flops 1000000 | bytes 1000000 | tf_op jit(solution)/shard_map/tail/pallas_call | solution.py:739
  800.4 1.5 fusion.29
  801.9 2.2 fusion.14
  804.1 1.3 slice_bitcast_fusion
  805.5 3.7 fusion.13
  809.1 3.0 add_convert_fusion
  812.2 13.0 %finish.1 = (f32[256,4,2048]{2,1,0:T(4,128)}, f32[128,4,2048]{2,1,0:T(4,128)}, f32[256,2048]{1,0:T(8,128)}, f32[256,2048]{1,0:T(8,128)}, f32[256,2048]{1,0:T(8,128)}, /*index=5*/f32[256,2048]{1,0:T(8,128)}) custom-call(bf16[256,6144]{1,0:T(8,128)(2,1)} %reduce-scatter.4.cloned.1.call-done.refs_0_.refs_1_.refs_2_, ...), custom_call_target="tpu_custom_call" | custom-call | flops 1000000 | bytes 1000000 | tf_op jit(solution)/shard_map/finish/pallas_call | solution.py:810
  (146 shorter events, 20.1 us)
Async XLA Ops:
  7.2 120.3 %all-gather.4.cloned.1.call-start = ((), (), s32[]{:S(2)}) async-start(), calls=%async_computation.3 | async-start | bytes 17104896 | tf_op jit(solution)/shard_map/all_gather | solution.py:1226
  15.4 2.1 copy-start.34
  15.4 2.3 copy-start.3
  17.5 282.7 %all-gather.6.cloned.1.call-start = ((), (), s32[]{:S(2)}) async-start(), calls=%async_computation.4 | async-start | bytes 28311552 | tf_op jit(solution)/shard_map/all_gather | solution.py:1226
  99.7 1.2 copy-start.11
  99.7 276.4 %all-gather.8.cloned.1.call-start = ((), (), s32[]{:S(2)}) async-start(), calls=%async_computation.5 | async-start | bytes 28311552 | tf_op jit(solution)/shard_map/all_gather | solution.py:1226
  100.5 409.6 %reduce-scatter.4.cloned.1.call-start = ((), (), s32[]{:S(2)}) async-start(), calls=%async_computation.6 | async-start | bytes 15728640 | tf_op jit(solution)/shard_map/reduce_scatter | solution.py:1231
  100.9 26.5 %collective-permute-start = (bf16[256,2048]{1,0:T(8,128)(2,1)S(1)}, bf16[256,2048]{1,0:T(8,128)(2,1)}, u32[]{:S(2)}, u32[]{:S(2)}) collective-permute-start(bf16[256,2048]{1,0:T(8,128)(2,1)S(1)} %copy-done.11), channel_id=1, source_target_pairs={{0,1},{1,2},{2,3},{3,0},{4,5},{5,6},{6,7},{7,4},{8,9},{9,10},{10,1... | collective-permute-start | bytes 3145736 | tf_op jit(solution)/shard_map/ppermute | solution.py:47
  105.0 186.8 %copy-start.37 = (pred[128]{0:T(512)(128)(4,1)}, pred[128]{0:T(512)(128)(4,1)S(1)}, u32[]{:S(2)}) copy-start(pred[128]{0:T(512)(128)(4,1)S(1)} %iota_compare_fusion.2) | copy-start | bytes 388
  127.4 25.8 %collective-permute-start.1 = (bf16[256,2048]{1,0:T(8,128)(2,1)}, bf16[256,2048]{1,0:T(8,128)(2,1)}, u32[]{:S(2)}, u32[]{:S(2)}) collective-permute-start(bf16[256,2048]{1,0:T(8,128)(2,1)} %collective-permute-done), channel_id=1, source_target_pairs={{0,1},{1,2},{2,3},{3,0},{4,5},{5,6},{6,7},{7,4},{8,9},{9,10},{10,1... | collective-permute-start | bytes 3145736 | tf_op jit(solution)/shard_map/ppermute | solution.py:47
  130.1 0.6 copy-start.21
  130.2 83.1 %copy-start.23 = (f32[2048]{0:T(1024)}, f32[2048]{0:T(1024)S(1)}, u32[]{:S(2)}) copy-start(f32[2048]{0:T(1024)S(1)} %get-tuple-element.130) | copy-start | bytes 24580
  133.6 10.3 %copy-start.6 = (bf16[1024,2048]{1,0:T(8,128)(2,1)}, bf16[1024,2048]{1,0:T(8,128)(2,1)S(1)}, u32[]{:S(2)}) copy-start(bf16[1024,2048]{1,0:T(8,128)(2,1)S(1)} %fusion.2.hidden) | copy-start | bytes 12582916
  143.9 11.6 %copy-start.7 = (f32[1024,1536]{1,0:T(8,128)}, f32[1024,1536]{1,0:T(8,128)S(1)}, u32[]{:S(2)}) copy-start(f32[1024,1536]{1,0:T(8,128)S(1)} %fusion.5) | copy-start | bytes 18874372
  163.0 24.0 %collective-permute-start.2 = (bf16[256,2048]{1,0:T(8,128)(2,1)}, bf16[256,2048]{1,0:T(8,128)(2,1)}, u32[]{:S(2)}, u32[]{:S(2)}) collective-permute-start(bf16[256,2048]{1,0:T(8,128)(2,1)} %collective-permute-done.1), channel_id=1, source_target_pairs={{0,1},{1,2},{2,3},{3,0},{4,5},{5,6},{6,7},{7,4},{8,9},{9,10},{10,1... | collective-permute-start | bytes 3145736 | tf_op jit(solution)/shard_map/ppermute | solution.py:47
  166.2 3.8 copy-start.28
  212.6 1.3 copy-start
  213.2 0.7 copy-start.29
  372.0 1.2 copy-start.8
  372.0 1.2 copy-start.38
  372.0 210.1 %reduce-scatter.8.cloned.1.call-start = ((), (), s32[]{:S(2)}) async-start(), calls=%async_computation.8 | async-start | bytes 5242880 | tf_op jit(solution)/shard_map/reduce_scatter | solution.py:1231
  374.7 0.7 copy-start.14
  374.7 0.7 copy-start.31
  376.2 36.9 %copy-start.19 = (f32[1024,128]{1,0:T(8,128)S(1)}, f32[1024,128]{1,0:T(8,128)}, u32[]{:S(2)}) copy-start(f32[1024,128]{1,0:T(8,128)} %get-tuple-element.81) | copy-start | bytes 1572868
  512.5 4.0 copy-start.17
  512.5 4.0 copy-start.1
  512.5 4.0 copy-start.12
  512.5 4.0 copy-start.24
  512.5 4.0 copy-start.30
  512.5 4.0 copy-start.36
  529.6 282.6 %all-reduce.4.cloned.1.call-start = ((), (), s32[]{:S(2)}) async-start(), calls=%async_computation.9 | async-start | bytes 2097152 | tf_op jit(solution)/shard_map/psum | solution.py:1343
  582.2 230.0 %reduce-scatter.6.cloned.1.call-start = ((), (), s32[]{:S(2)}) async-start(), calls=%async_computation.7 | async-start | bytes 15728640 | tf_op jit(solution)/shard_map/reduce_scatter | solution.py:1231
  582.2 1.2 copy-start.4
  582.2 1.5 copy-start.15
  585.4 43.8 %collective-permute-start.3 = (bf16[256,2048]{1,0:T(8,128)(2,1)S(1)}, bf16[256,2048]{1,0:T(8,128)(2,1)}, u32[]{:S(2)}, u32[]{:S(2)}) collective-permute-start(bf16[256,2048]{1,0:T(8,128)(2,1)S(1)} %add_convert_fusion.1), channel_id=1, source_target_pairs={{0,1},{1,2},{2,3},{3,0},{4,5},{5,6},{6,7},{7,4},{8,9},{9,10},{10,1... | collective-permute-start | bytes 3145736 | tf_op jit(solution)/shard_map/ppermute | solution.py:47
  590.3 1.6 copy-start.32
  591.9 25.4 %copy-start.9 = (bf16[256,2048]{1,0:T(8,128)(2,1)S(1)}, bf16[256,2048]{1,0:T(8,128)(2,1)}, u32[]{:S(2)}) copy-start(bf16[256,2048]{1,0:T(8,128)(2,1)} %multiply_convert_fusion.refs_0_) | copy-start | bytes 3145732
  591.9 25.4 %copy-start.18 = (bf16[256,128]{1,0:T(8,128)(2,1)S(1)}, bf16[256,128]{1,0:T(8,128)(2,1)}, u32[]{:S(2)}) copy-start(bf16[256,128]{1,0:T(8,128)(2,1)} %copy-done.17) | copy-start | bytes 196612
  591.9 25.7 %copy-start.27 = (f32[2048]{0:T(1024)S(1)}, f32[2048]{0:T(1024)}, u32[]{:S(2)}) copy-start(f32[2048]{0:T(1024)} %get-tuple-element.117) | copy-start | bytes 24580
  617.5 24.9 %copy-start.25 = (f32[1,1024]{1,0:T(1,128)S(1)}, f32[1,1024]{1,0:T(1,128)}, u32[]{:S(2)}) copy-start(f32[1,1024]{1,0:T(1,128)} %get-tuple-element.135) | copy-start | bytes 12292
  617.5 24.9 %copy-start.26 = (f32[1,1024]{1,0:T(1,128)S(1)}, f32[1,1024]{1,0:T(1,128)}, u32[]{:S(2)}) copy-start(f32[1,1024]{1,0:T(1,128)} %get-tuple-element.138) | copy-start | bytes 12292
  617.6 24.9 %copy-start.13 = (f32[1024,512]{1,0:T(8,128)S(1)}, f32[1024,512]{1,0:T(8,128)}, u32[]{:S(2)}) copy-start(f32[1024,512]{1,0:T(8,128)} %get-tuple-element.96) | copy-start | bytes 6291460
  629.1 3.0 copy-start.20
  641.6 167.5 %collective-permute-start.4 = (bf16[256,2048]{1,0:T(8,128)(2,1)}, bf16[256,2048]{1,0:T(8,128)(2,1)}, u32[]{:S(2)}, u32[]{:S(2)}) collective-permute-start(bf16[256,2048]{1,0:T(8,128)(2,1)} %convert_add_fusion.1), channel_id=1, source_target_pairs={{0,1},{1,2},{2,3},{3,0},{4,5},{5,6},{6,7},{7,4},{8,9},{9,10},{10,1... | collective-permute-start | bytes 3145736 | tf_op jit(solution)/shard_map/ppermute | solution.py:47
  642.5 3.4 copy-start.16
  800.4 5.1 copy-start.5
  800.4 5.1 copy-start.10
  800.4 5.1 copy-start.22
  800.4 5.1 copy-start.33
  800.4 5.1 copy-start.35
  805.5 3.7 copy-start.2
Sparse Core Ops, SparseCore 0:
  17.6 85.8 all-gather.3
  105.4 125.3 all-gather.5
  232.7 131.3 all-gather.7
  372.1 119.0 reduce-scatter.3
  529.7 52.3 reduce-scatter.7
  584.5 78.2 all-reduce.3
  665.9 138.4 reduce-scatter.5
